TPU v7x, 32 devices: a whole 2x2x4 slice. The times are simulated.
32 devices in a mesh: krow: 16 (over z, x, core), kcol: 2 (over y).
Axes of the slice: x: 2, y: 2, z: 4, core: 2. Of those that a mesh axis runs over, the one named last changes fastest.
Arguments:
- green: bfloat16 [4, 2, 16, 4, 256, 256], P(None, None, 'krow', 'kcol'), may hold values from -6 to 6
- screened: float32 [16, 4, 65536], P(None, None, ('krow', 'kcol')), may hold values from 0.1 to 1
Outputs:
- sigma: bfloat16 [4, 2, 16, 4, 256, 256], P(None, None, 'krow', 'kcol')
- dressed: bfloat16 [4, 2, 16, 4, 256, 256], P(None, None, 'krow', 'kcol')
All inputs are finite; a program needn't handle non-finite values.
Results may differ from a plain program's by a relative error of at most 0.0053.
Values may be sent and summed in bfloat16 or wider, within the bound.
No kernel may reach another device: no remote copies, remote signals or barrier semaphores. Data moves between devices by JAX's collectives and lax.ppermute only.
A program may use at most 64 MiB of HBM per device.

v0:
```python
import math

import jax
import jax.numpy as jnp
import numpy as np
from jax import lax
from jax.experimental import pallas as pl
from jax.experimental.pallas import tpu as pltpu
from jax.sharding import PartitionSpec as P

AXES = ("krow", "kcol")
ENERGY_CHUNKS = 1


def phase(length, sign):
    step = np.arange(length)
    angle = 2.0 * math.pi * (step[:, None] * step[None, :] % length) / length
    return np.cos(angle), sign * np.sin(angle)


def split_high_low(table):
    high = jnp.asarray(table, jnp.float32).astype(jnp.bfloat16)
    rest = jnp.asarray(table, jnp.float32) - high.astype(jnp.float32)
    return jnp.concatenate((high, rest.astype(jnp.bfloat16)), 0)


def row_tables(k_one, k_two, rows):
    tables = []
    for sign, scale in ((1.0, -1.0 / (k_one * k_two)), (-1.0, 1.0)):
        cosine, sine = phase(k_one, sign)
        block = np.empty((k_one, 2, k_one, 2))
        block[:, 0, :, 0] = cosine
        block[:, 0, :, 1] = -sine
        block[:, 1, :, 0] = sine
        block[:, 1, :, 1] = cosine
        square = block.reshape(2 * k_one, 2 * k_one) * scale
        tables.append(split_high_low(np.kron(square, np.eye(rows))))
    return tables


def turned(value, part, length, sign):
    re, im = value
    if part == 0:
        return value
    if 4 * part == length:
        return (-im, re) if sign > 0 else (im, -re)
    cosine = math.cos(2.0 * math.pi * part / length)
    sine = sign * math.sin(2.0 * math.pi * part / length)
    return cosine * re - sine * im, sine * re + cosine * im


def turns(values, sign):
    length = len(values)
    if length == 1:
        return values
    if length % 2:
        sums = []
        for r in range(length):
            terms = [turned(v, k * r % length, length, sign) for k, v in enumerate(values)]
            sums.append((sum(t[0] for t in terms), sum(t[1] for t in terms)))
        return sums
    even, odd = turns(values[::2], sign), turns(values[1::2], sign)
    odd = [turned(v, r, length, sign) for r, v in enumerate(odd)]
    pairs = list(zip(even, odd))
    return [(a[0] + b[0], a[1] + b[1]) for a, b in pairs] + [
        (a[0] - b[0], a[1] - b[1]) for a, b in pairs
    ]


def fourier_kernel(x_ref, w_ref, fwd_ref, inv_ref, o_ref):
    k_one, kcols, _, _, kcol_each, rows, width = x_ref.shape
    size = k_one * 2 * rows
    forward, inverse = fwd_ref[...], inv_ref[...]
    spots = [(c, k) for c in range(kcols) for k in range(kcol_each)]
    state = []
    for c, k in spots:
        block = x_ref[:, c, 0, :, k].reshape(size, width)
        both = jnp.dot(forward, block, preferred_element_type=jnp.float32)
        both = (both[:size] + both[size:]).reshape(k_one, 2, rows, width)
        state.append((both[:, 0], both[:, 1]))
    state = turns(state, 1)
    state = [(w_ref[:, r] * re, w_ref[:, r] * im) for r, (re, im) in enumerate(state)]
    state = turns(state, -1)
    for (c, k), (re, im) in zip(spots, state):
        block = jnp.stack((re, im), 1).reshape(size, width)
        high = block.astype(jnp.bfloat16)
        low = (block - high.astype(jnp.float32)).astype(jnp.bfloat16)
        both = jnp.dot(inverse, high, preferred_element_type=jnp.float32)
        out = both[:size] + both[size:]
        out = out + jnp.dot(inverse[:size], low, preferred_element_type=jnp.float32)
        o_ref[:, c, 0, :, k] = out.astype(jnp.bfloat16).reshape(k_one, 2, rows, width)


def fourier(pieces, weights, kcols):
    devices, energies, parts, each, rows, width = pieces.shape
    k_one, k_two = weights.shape[:2]
    x = pieces.reshape(k_one, kcols, energies, parts, each, rows, width)
    forward, inverse = row_tables(k_one, k_two, rows)
    block = pl.BlockSpec(
        (k_one, kcols, 1, parts, each, rows, width), lambda e: (0, 0, e, 0, 0, 0, 0)
    )
    whole = lambda a: pl.BlockSpec(a.shape, lambda e: (0,) * a.ndim)
    size = k_one * parts * rows
    out = pl.pallas_call(
        fourier_kernel,
        grid=(energies,),
        in_specs=[block, whole(weights), whole(forward), whole(inverse)],
        out_specs=block,
        out_shape=jax.ShapeDtypeStruct(x.shape, jnp.bfloat16),
        cost_estimate=pl.CostEstimate(
            flops=2 * 5 * size * size * width * k_two * energies,
            bytes_accessed=4 * x.size + 4 * weights.size,
            transcendentals=0,
        ),
        compiler_params=pltpu.CompilerParams(vmem_limit_bytes=40 * 2**20),
        name="fourier",
    )(x, weights, forward, inverse)
    return out.reshape(pieces.shape)


def dyson_kernel(s_ref, g_ref, so_ref, d_ref):
    orbitals = g_ref.shape[-1]
    sr = s_ref[:, 0, 0, 0].reshape(orbitals, orbitals)
    si = s_ref[:, 0, 1, 0].reshape(orbitals, orbitals)
    so_ref[0, 0, 0, 0] = sr
    so_ref[0, 1, 0, 0] = si
    gr, gi = g_ref[0, 0, 0, 0], g_ref[0, 1, 0, 0]
    dot = lambda a, b: jnp.dot(a, b, preferred_element_type=jnp.float32)
    kr = (dot(gr, sr) - dot(gi, si)).astype(jnp.bfloat16)
    ki = (dot(gr, si) + dot(gi, sr)).astype(jnp.bfloat16)
    scale = 1.0 / orbitals
    dr = gr.astype(jnp.float32) + (dot(kr, gr) - dot(ki, gi)) * scale
    di = gi.astype(jnp.float32) + (dot(kr, gi) + dot(ki, gr)) * scale
    d_ref[0, 0, 0, 0] = dr.astype(jnp.bfloat16)
    d_ref[0, 1, 0, 0] = di.astype(jnp.bfloat16)


def dyson(pieces, green):
    devices, energies, parts, each, rows, orbitals = pieces.shape
    flat = pl.BlockSpec(
        (1, parts, 1, 1, orbitals, orbitals), lambda e, k: (e, 0, 0, k, 0, 0)
    )
    shape = jax.ShapeDtypeStruct(green.shape, jnp.bfloat16)
    return pl.pallas_call(
        dyson_kernel,
        grid=(energies, each),
        in_specs=[
            pl.BlockSpec(
                (devices, 1, parts, 1, rows, orbitals), lambda e, k: (0, e, 0, k, 0, 0)
            ),
            flat,
        ],
        out_specs=[flat, flat],
        out_shape=[shape, shape],
        cost_estimate=pl.CostEstimate(
            flops=16 * orbitals**3 * each * energies,
            bytes_accessed=8 * green.size,
            transcendentals=0,
        ),
        name="dyson",
    )(pieces, green)


def exchange(blocks):
    return lax.all_to_all(blocks, AXES, split_axis=0, concat_axis=0, tiled=True)


def per_device(green, screened):
    kcols = lax.axis_size("kcol")
    devices = lax.axis_size("krow") * kcols
    energies, parts, _, each, orbitals, width = green.shape
    rows = orbitals // devices
    weights = screened.reshape(screened.shape[:2] + (rows, width))
    step = energies // ENERGY_CHUNKS
    chunks = [green[e : e + step] for e in range(0, energies, step)]
    middle = []
    for part in chunks:
        blocks = part.reshape(step, parts, each, devices, rows, width)
        blocks = jnp.transpose(blocks, (3, 0, 1, 2, 4, 5))
        middle.append(fourier(exchange(blocks), weights, kcols))
    outs = [dyson(exchange(m), part) for m, part in zip(middle, chunks)]
    return tuple(jnp.concatenate(o, 0) for o in zip(*outs))


def solution(mesh):
    spec = P(None, None, "krow", "kcol", None, None)
    return jax.shard_map(
        per_device,
        mesh=mesh,
        in_specs=(spec, P(None, None, AXES)),
        out_specs=(spec, spec),
        check_vma=False,
    )
```

profile of v0, /device:TPU:0, one launch (start us, length us, event | category | flops | bytes accessed | tf_op | source)
XLA Modules:
  0.0 125.2 jit_solution(5042933533636356631)
XLA Ops:
  0.6 3.2 %copy_bitcast_fusion = bf16[32,4,2,2,8,256]{5,4,3,2,1,0:T(8,128)(2,1)} fusion(bf16[4,2,1,2,256,256]{5,4,3,2,1,0:T(8,128)(2,1)} %g_ref.1), kind=kLoop, calls=%fused_computation | loop fusion | bytes 4194304 | tf_op jit(solution)/shard_map/transpose | solution.py:179
  3.8 0.0 copy-start
  3.8 0.0 copy-start.1
  3.8 7.3 %all-to-all-start = ((bf16[32,4,2,2,8,256]{5,4,3,2,1,0:T(8,128)(2,1)}), bf16[32,4,2,2,8,256]{5,4,3,2,1,0:T(8,128)(2,1)S(1)}, u32[]{:S(2)}, u32[]{:S(2)}) async-start(bf16[32,4,2,2,8,256]{5,4,3,2,1,0:T(8,128)(2,1)} %copy_bitcast_fusion), calls=%async_computation | async-start | bytes 4194304 | tf_op jit(solution)/shard_map/all_to_all | solution.py:165
  11.2 1.3 %reshape.18.w_ref = f32[16,4,8,256]{3,2,1,0:T(8,128)S(1)} reshape(f32[16,4,2048]{2,1,0:T(4,128)} %param.7) | data formatting | bytes 1048576 | tf_op jit(solution)/shard_map/reshape | solution.py:173
  12.5 47.4 %all-to-all-done = bf16[32,4,2,2,8,256]{5,4,3,2,1,0:T(8,128)(2,1)S(1)} async-done(((bf16[32,4,2,2,8,256]{5,4,3,2,1,0:T(8,128)(2,1)}), bf16[32,4,2,2,8,256]{5,4,3,2,1,0:T(8,128)(2,1)S(1)}, u32[]{:S(2)}, u32[]{:S(2)}) %all-to-all-start) | async-done | bytes 2097184 | tf_op jit(solution)/shard_map/all_to_all | solution.py:165
  59.8 0.0 copy-done
  59.8 0.0 copy-done.1
  59.9 4.8 %fourier.1 = bf16[16,2,4,2,2,8,256]{6,5,4,3,2,1,0:T(8,128)(2,1)S(1)} custom-call(bf16[16,2,4,2,2,8,256]{6,5,4,3,2,1,0:T(8,128)(2,1)S(1)} %bitcast.7, f32[16,4,8,256]{3,2,1,0:T(8,128)S(1)} %reshape.18.w_ref, bf16[512,256]{1,0:T(8,128)(2,1)S(1)} %copy-done.1, bf16[512,256]{1,0:T(8,128)(2,1)S(1)} %copy-done), custom_call_target="tpu_custom_call" | custom-call | flops 2684354560 | bytes 4718592 | tf_op jit(solution)/shard_map/fourier/pallas_call | solution.py:104
  64.7 52.2 %all_to_all.10.s_ref = bf16[32,4,2,2,8,256]{5,4,3,2,1,0:T(8,128)(2,1)} all-to-all(bf16[32,4,2,2,8,256]{5,4,3,2,1,0:T(8,128)(2,1)S(1)} %bitcast.8), channel_id=1, replica_groups=mesh['krow'=16,'kcol'=2] {'krow','kcol'}, dimensions={0} | all-to-all | bytes 4194304 | tf_op jit(solution)/shard_map/all_to_all | solution.py:165
  116.9 8.3 %dyson.1 = (bf16[4,2,1,2,256,256]{5,4,3,2,1,0:T(8,128)(2,1)}, bf16[4,2,1,2,256,256]{5,4,3,2,1,0:T(8,128)(2,1)}) custom-call(bf16[32,4,2,2,8,256]{5,4,3,2,1,0:T(8,128)(2,1)} %all_to_all.10.s_ref, bf16[4,2,1,2,256,256]{5,4,3,2,1,0:T(8,128)(2,1)} %g_ref.1), custom_call_target="tpu_custom_call" | custom-call | flops 2147483648 | bytes 8388608 | tf_op jit(solution)/shard_map/dyson/pallas_call | solution.py:144
Async XLA Ops:
  3.8 56.0 %copy-start = (bf16[512,256]{1,0:T(8,128)(2,1)S(1)}, bf16[512,256]{1,0:T(8,128)(2,1)}, u32[]{:S(2)}) copy-start(bf16[512,256]{1,0:T(8,128)(2,1)} %constant.16.inv_ref) | copy-start | bytes 786436
  3.8 56.0 %copy-start.1 = (bf16[512,256]{1,0:T(8,128)(2,1)S(1)}, bf16[512,256]{1,0:T(8,128)(2,1)}, u32[]{:S(2)}) copy-start(bf16[512,256]{1,0:T(8,128)(2,1)} %constant.11.fwd_ref) | copy-start | bytes 786436
  3.8 56.0 %all-to-all-start = ((bf16[32,4,2,2,8,256]{5,4,3,2,1,0:T(8,128)(2,1)}), bf16[32,4,2,2,8,256]{5,4,3,2,1,0:T(8,128)(2,1)S(1)}, u32[]{:S(2)}, u32[]{:S(2)}) async-start(bf16[32,4,2,2,8,256]{5,4,3,2,1,0:T(8,128)(2,1)} %copy_bitcast_fusion), calls=%async_computation | async-start | bytes 4194304 | tf_op jit(solution)/shard_map/all_to_all | solution.py:165
where the time goes:
time: 126 us; the launch traced here: 125 us
  blocking collectives  52.2 us (41%)
  waiting for transfers between devices  47.4 us (38%)
  Pallas kernels  13.1 us (10%)
  starting transfers between devices  7.33 us (6%)
  local copies, waits for them, and re-layouts  4.53 us (4%)
    all_to_all x1, blocking collectives, exchange(): return lax.all_to_all(blocks, AXES, split_axis=0, concat_axis=0, tiled=True)  52.2 us
    all_to_all x1, waiting for transfers between devices, exchange(): return lax.all_to_all(blocks, AXES, split_axis=0, concat_axis=0, tiled=True)  47.4 us
    pallas_call x1, Pallas kernels, dyson(): pl.pallas_call(dyson_kernel, grid=(energies, each), in_specs=[pl.BlockSpe...  8.29 us
    all_to_all x1, starting transfers between devices, exchange(): return lax.all_to_all(blocks, AXES, split_axis=0, concat_axis=0, tiled=True)  7.33 us
    pallas_call x1, Pallas kernels, fourier(): pl.pallas_call(fourier_kernel, grid=(energies,), in_specs=[block, whole(w...  4.81 us
    transpose x1, local copies, waits for them, and re-layouts, per_device(): blocks = jnp.transpose(blocks, (3, 0, 1, 2, 4, 5))  3.2 us
  transfers between devices with their start and end apart: 1, of which 1 were waited for; matrix products, arithmetic and copies ran while one was open for 1% of the time, Pallas kernels for 0%

commit v1 on v0

v1 whole, which is shorter than its diff:
```python
import functools
import math
import typing

import jax
import jax.numpy as jnp
import numpy as np
from jax import lax
from jax.experimental import pallas as pl
from jax.experimental.pallas import tpu as pltpu
from jax.sharding import PartitionSpec as P


AXES = ("krow", "kcol")


def phase(length, sign):
    step = np.arange(length)
    angle = 2.0 * math.pi * (step[:, None] * step[None, :] % length) / length
    return np.cos(angle), sign * np.sin(angle)


def split_high_low(table):
    high = jnp.asarray(table, jnp.float32).astype(jnp.bfloat16)
    rest = jnp.asarray(table, jnp.float32) - high.astype(jnp.float32)
    return high, rest.astype(jnp.bfloat16)


def row_tables(k_one, k_two, rows):
    tables = []
    for sign, scale in ((1.0, -1.0 / (k_one * k_two)), (-1.0, 1.0)):
        cosine, sine = phase(k_one, sign)
        block = np.empty((k_one, 2, k_one, 2))
        block[:, 0, :, 0] = cosine
        block[:, 0, :, 1] = -sine
        block[:, 1, :, 0] = sine
        block[:, 1, :, 1] = cosine
        square = block.reshape(2 * k_one, 2 * k_one) * scale
        high, low = split_high_low(np.kron(square, np.eye(rows)))
        tables.append(jnp.concatenate((high, low) if sign > 0 else (high, low, high), 1))
    return tables


def turned(value, part, length, sign):
    re, im = value
    if part == 0:
        return value
    if 4 * part == length:
        return (-im, re) if sign > 0 else (im, -re)
    cosine = math.cos(2.0 * math.pi * part / length)
    sine = sign * math.sin(2.0 * math.pi * part / length)
    return cosine * re - sine * im, sine * re + cosine * im


def turns(values, sign):
    length = len(values)
    if length == 1:
        return values
    if length % 2:
        sums = []
        for r in range(length):
            terms = [turned(v, k * r % length, length, sign) for k, v in enumerate(values)]
            sums.append((sum(t[0] for t in terms), sum(t[1] for t in terms)))
        return sums
    even, odd = turns(values[::2], sign), turns(values[1::2], sign)
    odd = [turned(v, r, length, sign) for r, v in enumerate(odd)]
    pairs = list(zip(even, odd))
    return [(a[0] + b[0], a[1] + b[1]) for a, b in pairs] + [
        (a[0] - b[0], a[1] - b[1]) for a, b in pairs
    ]


def own_index(kcols):
    return lax.axis_index("krow") * kcols + lax.axis_index("kcol")


def fourier_kernel(kcols, relative, x_ref, w_ref, fwd_ref, inv_ref, o_ref):
    devices, _, _, kcol_each, rows, width = x_ref.shape
    k_one = devices // kcols
    size = k_one * 2 * rows
    me = own_index(kcols) if relative else 0
    spots = [(c, k) for c in range(kcols) for k in range(kcol_each)]

    def slot(one, c):
        place = one * kcols + c
        return place ^ me if relative else place

    def load(c, e, k):
        parts = [x_ref[slot(one, c), e, :, k] for one in range(k_one)]
        return jnp.stack(parts, 0).reshape(size, width)

    def store(c, k, value):
        for one in range(k_one):
            o_ref[slot(one, c), 0, :, k] = value[one]

    e = pl.program_id(0)
    forward, inverse = fwd_ref[...], inv_ref[...]
    state = []
    for c, k in spots:
        block = load(c, e, k)
        block = jnp.concatenate((block, block), 0)
        out = jnp.dot(forward, block, preferred_element_type=jnp.float32)
        out = out.reshape(k_one, 2, rows, width)
        state.append((out[:, 0], out[:, 1]))
    state = turns(state, 1)
    state = [(w_ref[:, r] * re, w_ref[:, r] * im) for r, (re, im) in enumerate(state)]
    state = turns(state, -1)
    for (c, k), (re, im) in zip(spots, state):
        block = jnp.stack((re, im), 1).reshape(size, width)
        high = block.astype(jnp.bfloat16)
        low = (block - high.astype(jnp.float32)).astype(jnp.bfloat16)
        block = jnp.concatenate((high, high, low), 0)
        out = jnp.dot(inverse, block, preferred_element_type=jnp.float32)
        store(c, k, out.astype(jnp.bfloat16).reshape(k_one, 2, rows, width))


LOCAL = pl.BlockSpec(memory_space=pltpu.VMEM)


PARAMS = pltpu.CompilerParams(vmem_limit_bytes=16 * 2**20)


def near(value):
    return pltpu.with_memory_space_constraint(value, pltpu.VMEM)


def far(value):
    return pltpu.with_memory_space_constraint(value, pltpu.HBM)


def fourier(pieces, weights, kcols, relative):
    _, energies, parts, each, rows, width = pieces.shape
    k_one, k_two = weights.shape[:2]
    forward, inverse = row_tables(k_one, k_two, rows)
    size = k_one * parts * rows
    return pl.pallas_call(
        functools.partial(fourier_kernel, kcols, relative),
        grid=(energies,),
        in_specs=[LOCAL] * 4,
        out_specs=pl.BlockSpec(
            (pieces.shape[0], 1, parts, each, rows, width), lambda e: (0, e, 0, 0, 0, 0)
        ),
        out_shape=(pltpu.VMEM if relative else pltpu.HBM)(pieces.shape, jnp.bfloat16),
        cost_estimate=pl.CostEstimate(
            flops=2 * 5 * size * size * width * k_two * energies,
            bytes_accessed=4 * pieces.size + 4 * weights.size,
            transcendentals=0,
        ),
        compiler_params=PARAMS,
    )(near(pieces), near(weights), near(forward), near(inverse))


def gather_kernel(g_ref, o_ref, held, sems, out_sems):
    _, energies, parts, each = held.shape[:4]
    spots = [(p, k) for p in range(parts) for k in range(each)]
    inward = [
        [
            pltpu.make_async_copy(
                g_ref.at[e, p, k], held.at[:, e, p, k], sems.at[e, n]
            )
            for n, (p, k) in enumerate(spots)
        ]
        for e in range(energies)
    ]
    outward = [
        pltpu.make_async_copy(held.at[:, e], o_ref.at[:, e], out_sems.at[e])
        for e in range(energies)
    ]
    for copies in inward:
        for copy in copies:
            copy.start()
    for copies, last in zip(inward, outward):
        for copy in copies:
            copy.wait()
        last.start()
    for last in outward:
        last.wait()


def by_device(blocks, energies):
    _, parts, each, devices, rows, width = blocks.shape
    shape = (devices, energies, parts, each, rows, width)
    return pl.pallas_call(
        gather_kernel,
        in_specs=[pl.BlockSpec(memory_space=pltpu.HBM)],
        out_specs=pl.BlockSpec(memory_space=pltpu.HBM),
        out_shape=pltpu.HBM(shape, blocks.dtype),
        scratch_shapes=[
            pltpu.VMEM(shape, blocks.dtype),
            pltpu.SemaphoreType.DMA((energies, parts * each)),
            pltpu.SemaphoreType.DMA((energies,)),
        ],
        compiler_params=PARAMS,
        name="by_device",
    )(far(blocks))


def offset_kernel(first, kcols, g_ref, *refs):
    held, sems = refs[-2:]
    outs = refs[:-2]
    energies, parts, each, devices = held.shape[:4]
    spots = [(e, p, k) for e in range(energies) for p in range(parts) for k in range(each)]
    copies = [
        pltpu.make_async_copy(g_ref.at[first + e, p, k], held.at[e, p, k], sems.at[n])
        for n, (e, p, k) in enumerate(spots)
    ]
    for copy in copies:
        copy.start()
    me = own_index(kcols)
    share = devices // len(outs)
    for copy, (e, p, k) in zip(copies, spots):
        copy.wait()
        for j in range(devices):
            outs[j // share][j % share, e, p, k] = held[e, p, k, j ^ me]


def by_offset(blocks, first, energies, kcols, pieces):
    _, parts, each, devices, rows, width = blocks.shape
    shape = (devices // pieces, energies, parts, each, rows, width)
    return pl.pallas_call(
        functools.partial(offset_kernel, first, kcols),
        in_specs=[pl.BlockSpec(memory_space=pltpu.HBM)],
        out_specs=[LOCAL] * pieces,
        out_shape=[pltpu.VMEM(shape, blocks.dtype)] * pieces,
        scratch_shapes=[
            pltpu.VMEM((energies,) + blocks.shape[1:], blocks.dtype),
            pltpu.SemaphoreType.DMA((energies * parts * each,)),
        ],
        compiler_params=PARAMS,
        name="by_offset",
    )(far(blocks))


def dyson_kernel(first, kcols, relative, s_ref, g_ref, *refs):
    so_ref, d_ref = refs[-2:]
    devices, orbitals = s_ref.shape[0], g_ref.shape[-1]
    e, k = pl.program_id(0), pl.program_id(1)
    if relative:
        me = own_index(kcols)
        load = lambda p: jnp.stack([s_ref[d ^ me, e, p, k] for d in range(devices)], 0)
    else:
        load = lambda p: s_ref[:, e, p, k]
    sr, si = (load(p).reshape(orbitals, orbitals) for p in range(2))
    so_ref[0, 0, 0, 0] = sr
    so_ref[0, 1, 0, 0] = si
    gr, gi = g_ref[first + e, 0, 0, k], g_ref[first + e, 1, 0, k]

    def product(ar, ai, br, bi):
        left = jnp.concatenate(
            (jnp.concatenate((ar, -ai), 1), jnp.concatenate((ai, ar), 1)), 0
        )
        right = jnp.concatenate((br, bi), 0)
        out = jnp.dot(left, right, preferred_element_type=jnp.float32)
        return out[:orbitals], out[orbitals:]

    kr, ki = (a.astype(jnp.bfloat16) for a in product(gr, gi, sr, si))
    cr, ci = product(kr, ki, gr, gi)
    scale = 1.0 / orbitals
    dr = gr.astype(jnp.float32) + cr * scale
    di = gi.astype(jnp.float32) + ci * scale
    d_ref[0, 0, 0, 0] = dr.astype(jnp.bfloat16)
    d_ref[0, 1, 0, 0] = di.astype(jnp.bfloat16)


def dyson(pieces, green, first, kcols, relative, earlier):
    _, energies, parts, each, _, orbitals = pieces.shape
    flat = pl.BlockSpec(
        (1, parts, 1, 1, orbitals, orbitals), lambda e, k: (first + e, 0, 0, k, 0, 0)
    )
    shape = pltpu.HBM(green.shape, jnp.bfloat16)
    return pl.pallas_call(
        functools.partial(dyson_kernel, first, kcols, relative),
        grid=(energies, each),
        in_specs=[LOCAL, LOCAL] + [pl.BlockSpec(memory_space=pltpu.HBM)] * len(earlier),
        out_specs=[flat, flat],
        out_shape=[shape, shape],
        input_output_aliases={2 + n: n for n in range(len(earlier))},
        cost_estimate=pl.CostEstimate(
            flops=16 * orbitals**3 * each * energies,
            bytes_accessed=16 * pieces.size,
            transcendentals=0,
        ),
        compiler_params=PARAMS,
    )(near(pieces), near(green), *earlier)


def exchange(blocks):
    return lax.all_to_all(blocks, AXES, split_axis=0, concat_axis=0, tiled=True)


def swap(pieces, dims):
    counts, devices = pieces.counts, math.prod(pieces.counts)
    strides = [math.prod(counts[d + 1 :]) for d in range(len(counts))]

    def level(part, left, offset):
        if not left:
            if offset == 0:
                return part
            pairs = [(d, d ^ offset) for d in range(devices)]
            return lax.ppermute(part, AXES, pairs)
        dim, rest = left[0], left[1:]
        cut = (
            part
            if isinstance(part, (list, tuple))
            else [lax.slice_in_dim(part, q, q + 1, axis=dim) for q in range(counts[dim])]
        )
        back = [level(c, rest, offset + q * strides[dim]) for q, c in enumerate(cut)]
        return lax.concatenate(back, dim)

    return Side(counts, level(pieces.blocks, dims, 0))


class Side(typing.NamedTuple):
    counts: tuple
    blocks: typing.Any

    def merged(self):
        return self.blocks.reshape((-1,) + self.blocks.shape[len(self.counts) :])

    @classmethod
    def of(cls, counts, blocks):
        return cls(counts, blocks.reshape(counts + blocks.shape[1:]))


def per_device(green, screened):
    krows, kcols = lax.axis_size("krow"), lax.axis_size("kcol")
    devices = krows * kcols
    energies, parts, _, each, orbitals, width = green.shape
    rows = orbitals // devices
    weights = screened.reshape(screened.shape[:2] + (rows, width))
    blocks = green.reshape(energies, parts, each, devices, rows, width)
    aside = 1 if kcols == 2 and krows in (8, 16) and energies > 1 else 0
    main = energies - aside
    earlier = ()
    if aside:
        counts = (krows // 4, 2, 2, kcols)
        cut = by_offset(blocks, main, aside, kcols, counts[0])
        side = Side(counts, [c.reshape((1,) + counts[1:] + c.shape[1:]) for c in cut])
        side = swap(side, (0,))
        side = swap(side, (2,))
        side = swap(side, (1, 3))
        turned = fourier(side.merged(), weights, kcols, True)
        side = swap(Side.of(counts, turned), (2,))
        side = swap(side, (0,))
        side = swap(side, (1, 3))
        earlier = dyson(side.merged(), green, main, kcols, True, ())
    middle = exchange(by_device(blocks, main))
    middle = fourier(middle, weights, kcols, False)
    middle = exchange(middle)
    return tuple(dyson(middle, green, 0, kcols, False, earlier))


def solution(mesh):
    spec = P(None, None, "krow", "kcol", None, None)
    return jax.shard_map(
        per_device,
        mesh=mesh,
        in_specs=(spec, P(None, None, AXES)),
        out_specs=(spec, spec),
        check_vma=False,
    )
```

time: 126 us -> 151 us (1.20)
  waiting for transfers between devices: 47.4 us -> 104 us
  blocking collectives: 52.2 us -> 0 us
  starting transfers between devices: 7.33 us -> 27.2 us
  Pallas kernels: 13.1 us -> 17.8 us
  local copies, waits for them, and re-layouts: 4.53 us -> 0.41 us
    ppermute x0 -> x14, waiting for transfers between devices: none -> 67 us  [level(): return lax.ppermute(part, AXES, pairs)]
    all_to_all x1 -> x0, blocking collectives: 52.2 us -> none  [exchange(): return lax.all_to_all(blocks, AXES, split_axis=0, concat_axis=0, tiled=True)]
    ppermute x0 -> x14, starting transfers between devices: none -> 16.1 us  [level(): return lax.ppermute(part, AXES, pairs)]
    all_to_all x1 -> x2, waiting for transfers between devices: 47.4 us -> 37.2 us  [exchange(): return lax.all_to_all(blocks, AXES, split_axis=0, concat_axis=0, tiled=True)]
    pallas_call x2 -> x6, Pallas kernels: 13.1 us -> 17.8 us  [the longest x2 8.8 us: dyson(): pl.pallas_call(functools.partial(dyson_kernel, first, kcols, relative), g...]
    all_to_all x1 -> x2, starting transfers between devices: 7.33 us -> 11.1 us  [exchange(): return lax.all_to_all(blocks, AXES, split_axis=0, concat_axis=0, tiled=True)]
    transpose x1 -> x0, local copies, waits for them, and re-layouts: 3.2 us -> none  [per_device(): blocks = jnp.transpose(blocks, (3, 0, 1, 2, 4, 5))]
  transfers between devices with their start and end apart: 1 -> 16, of which waited for: 1 -> 14; matrix products, arithmetic and copies ran while one was open for 1% -> 0% of each run, Pallas kernels for 0% -> 3%
where the time goes in v1:
time: 151 us
  waiting for transfers between devices  104 us (69%)
  starting transfers between devices  27.2 us (18%)
  Pallas kernels  17.8 us (12%)
    ppermute x14, waiting for transfers between devices, level(): return lax.ppermute(part, AXES, pairs)  67 us
    all_to_all x2, waiting for transfers between devices, exchange(): return lax.all_to_all(blocks, AXES, split_axis=0, concat_axis=0, tiled=True)  37.2 us
    ppermute x14, starting transfers between devices, level(): return lax.ppermute(part, AXES, pairs)  16.1 us
    all_to_all x2, starting transfers between devices, exchange(): return lax.all_to_all(blocks, AXES, split_axis=0, concat_axis=0, tiled=True)  11.1 us
    pallas_call x2, Pallas kernels, dyson(): pl.pallas_call(functools.partial(dyson_kernel, first, kcols, relative), g...  8.8 us
    pallas_call x2, Pallas kernels, fourier(): pl.pallas_call(functools.partial(fourier_kernel, kcols, relative), grid=(...  5.45 us
  transfers between devices with their start and end apart: 16, of which 14 were waited for; matrix products, arithmetic and copies ran while one was open for 0% of the time, Pallas kernels for 3%

profile of v1, /device:TPU:0, one launch (start us, length us, event | category | flops | bytes accessed | tf_op | source)
XLA Modules:
  0.0 150.6 jit_solution(14674387513220958946)
XLA Ops:
  0.6 2.4 %by_device.1 = bf16[32,3,2,2,8,256]{5,4,3,2,1,0:T(8,128)(2,1)} custom-call(bf16[4,2,2,32,8,256]{5,4,3,2,1,0:T(8,128)(2,1)} %bitcast.16), custom_call_target="tpu_custom_call" | custom-call | tf_op jit(solution)/shard_map/by_device/pallas_call | solution.py:183
  3.0 0.0 copy-start.3
  3.0 0.0 copy-start.1
  3.0 0.0 copy-start.2
  3.1 7.3 %all-to-all-start = ((bf16[32,3,2,2,8,256]{5,4,3,2,1,0:T(8,128)(2,1)}), bf16[32,3,2,2,8,256]{5,4,3,2,1,0:T(8,128)(2,1)S(1)}, u32[]{:S(2)}, u32[]{:S(2)}) async-start(bf16[32,3,2,2,8,256]{5,4,3,2,1,0:T(8,128)(2,1)} %by_device.1), calls=%async_computation | async-start | bytes 3145728 | tf_op jit(solution)/shard_map/all_to_all | solution.py:288
  10.4 0.0 copy-done.3
  10.4 0.3 reshape.32.w_ref
  10.7 37.1 %all-to-all-done.x_ref = bf16[32,3,2,2,8,256]{5,4,3,2,1,0:T(8,128)(2,1)S(1)} async-done(((bf16[32,3,2,2,8,256]{5,4,3,2,1,0:T(8,128)(2,1)}), bf16[32,3,2,2,8,256]{5,4,3,2,1,0:T(8,128)(2,1)S(1)}, u32[]{:S(2)}, u32[]{:S(2)}) %all-to-all-start) | async-done | bytes 1572896 | tf_op jit(solution)/shard_map/all_to_all | solution.py:288
  47.8 0.0 copy-done.1
  47.8 4.3 %shard_map.113 = bf16[32,3,2,2,8,256]{5,4,3,2,1,0:T(8,128)(2,1)} custom-call(bf16[32,3,2,2,8,256]{5,4,3,2,1,0:T(8,128)(2,1)S(1)} %all-to-all-done.x_ref, f32[16,4,8,256]{3,2,1,0:T(8,128)S(1)} %reshape.32.w_ref, bf16[256,512]{1,0:T(8,128)(2,1)S(1)} %copy-done.2, bf16[256,768]{1,0:T(8,128)(2,1)S(1)} %copy-done.1), custom_call_target="tpu_custom_call" | custom-call | flops 2013265920 | bytes 3670016 | tf_op jit(solution)/shard_map/pallas_call | solution.py:136
  52.1 3.7 %all-to-all-start.1 = ((bf16[32,3,2,2,8,256]{5,4,3,2,1,0:T(8,128)(2,1)}), bf16[32,3,2,2,8,256]{5,4,3,2,1,0:T(8,128)(2,1)}, u32[]{:S(2)}, u32[]{:S(2)}) async-start(bf16[32,3,2,2,8,256]{5,4,3,2,1,0:T(8,128)(2,1)} %shard_map.113), calls=%async_computation.1 | async-start | bytes 3145728 | tf_op jit(solution)/shard_map/all_to_all | solution.py:288
  55.9 1.2 by_offset.1
  57.0 1.8 %collective-permute-start = (bf16[1,2,2,2,1,2,2,8,256]{8,7,6,5,3,2,1,0,4:T(8,128)(2,1)S(1)}, bf16[1,2,2,2,1,2,2,8,256]{8,7,6,5,3,2,1,0,4:T(8,128)(2,1)S(1)}, u32[]{:S(2)}, u32[]{:S(2)}) collective-permute-start(bf16[1,2,2,2,1,2,2,8,256]{8,7,6,5,3,2,1,0,4:T(8,128)(2,1)S(1)} %bitcast.24), channel_id=1, source_target_pairs={{0,8},{1,9},{2,10},{3,11},{4,12},{5,13},{6,14},{7,15},{8,0},{9,1},... | collective-permute-start | bytes 393224 | tf_op jit(solution)/shard_map/ppermute | solution.py:300
  58.8 2.4 %collective-permute-start.1 = (bf16[1,2,2,2,1,2,2,8,256]{8,7,6,5,3,2,1,0,4:T(8,128)(2,1)S(1)}, bf16[1,2,2,2,1,2,2,8,256]{8,7,6,5,3,2,1,0,4:T(8,128)(2,1)S(1)}, u32[]{:S(2)}, u32[]{:S(2)}) collective-permute-start(bf16[1,2,2,2,1,2,2,8,256]{8,7,6,5,3,2,1,0,4:T(8,128)(2,1)S(1)} %bitcast.23), channel_id=1, source_target_pairs={{0,16},{1,17},{2,18},{3,19},{4,20},{5,21},{6,22},{7,23},{8,24},{9,... | collective-permute-start | bytes 393224 | tf_op jit(solution)/shard_map/ppermute | solution.py:300
  61.2 0.3 collective-permute-start.2
  61.5 23.5 %collective-permute-done = bf16[1,2,2,2,1,2,2,8,256]{8,7,6,5,3,2,1,0,4:T(8,128)(2,1)S(1)} collective-permute-done((bf16[1,2,2,2,1,2,2,8,256]{8,7,6,5,3,2,1,0,4:T(8,128)(2,1)S(1)}, bf16[1,2,2,2,1,2,2,8,256]{8,7,6,5,3,2,1,0,4:T(8,128)(2,1)S(1)}, u32[]{:S(2)}, u32[]{:S(2)}) %collective-permute-start) | collective-permute-done | bytes 131104 | tf_op jit(solution)/shard_map/ppermute | solution.py:300
  85.0 17.2 %collective-permute-done.1 = bf16[1,2,2,2,1,2,2,8,256]{8,7,6,5,3,2,1,0,4:T(8,128)(2,1)S(1)} collective-permute-done((bf16[1,2,2,2,1,2,2,8,256]{8,7,6,5,3,2,1,0,4:T(8,128)(2,1)S(1)}, bf16[1,2,2,2,1,2,2,8,256]{8,7,6,5,3,2,1,0,4:T(8,128)(2,1)S(1)}, u32[]{:S(2)}, u32[]{:S(2)}) %collective-permute-start.1) | collective-permute-done | bytes 131104 | tf_op jit(solution)/shard_map/ppermute | solution.py:300
  102.2 0.0 collective-permute-done.2
  102.2 0.1 pad_maximum_fusion
  102.3 0.1 collective-permute-start.3
  102.4 1.5 %collective-permute-done.3 = bf16[4,2,1,2,1,2,2,8,256]{8,7,6,5,3,2,1,0,4:T(8,128)(2,1)S(1)} collective-permute-done((bf16[4,2,1,2,1,2,2,8,256]{8,7,6,5,3,2,1,0,4:T(8,128)(2,1)S(1)}, bf16[4,2,1,2,1,2,2,8,256]{8,7,6,5,3,2,1,0,4:T(8,128)(2,1)S(1)}, u32[]{:S(2)}, u32[]{:S(2)}) %collective-permute-start.3) | collective-permute-done | bytes 262176 | tf_op jit(solution)/shard_map/ppermute | solution.py:300
  104.0 1.6 %collective-permute-start.4 = (bf16[4,1,2,1,1,2,2,8,256]{8,7,6,5,3,2,1,0,4:T(8,128)(2,1)S(1)}, bf16[4,1,2,1,1,2,2,8,256]{8,7,6,5,3,2,1,0,4:T(8,128)(2,1)S(1)}, u32[]{:S(2)}, u32[]{:S(2)}) collective-permute-start(bf16[4,1,2,1,1,2,2,8,256]{8,7,6,5,3,2,1,0,4:T(8,128)(2,1)S(1)} %get-tuple-element.25), channel_id=1, source_target_pairs={{0,1},{1,0},{2,3},{3,2},{4,5},{5,4},{6,7},{7,6},{8,9},{9,8},{10,11... | collective-permute-start | bytes 393224 | tf_op jit(solution)/shard_map/ppermute | solution.py:300
  105.6 1.5 %collective-permute-start.6 = (bf16[4,1,2,1,1,2,2,8,256]{8,7,6,5,3,2,1,0,4:T(8,128)(2,1)S(1)}, bf16[4,1,2,1,1,2,2,8,256]{8,7,6,5,3,2,1,0,4:T(8,128)(2,1)S(1)}, u32[]{:S(2)}, u32[]{:S(2)}) collective-permute-start(bf16[4,1,2,1,1,2,2,8,256]{8,7,6,5,3,2,1,0,4:T(8,128)(2,1)S(1)} %get-tuple-element.26), channel_id=1, source_target_pairs={{0,5},{1,4},{2,7},{3,6},{4,1},{5,0},{6,3},{7,2},{8,13},{9,12},{10,... | collective-permute-start | bytes 393224 | tf_op jit(solution)/shard_map/ppermute | solution.py:300
  107.1 0.4 collective-permute-start.5
  107.5 4.4 %collective-permute-done.4 = bf16[4,1,2,1,1,2,2,8,256]{8,7,6,5,3,2,1,0,4:T(8,128)(2,1)S(1)} collective-permute-done((bf16[4,1,2,1,1,2,2,8,256]{8,7,6,5,3,2,1,0,4:T(8,128)(2,1)S(1)}, bf16[4,1,2,1,1,2,2,8,256]{8,7,6,5,3,2,1,0,4:T(8,128)(2,1)S(1)}, u32[]{:S(2)}, u32[]{:S(2)}) %collective-permute-start.4) | collective-permute-done | bytes 131104 | tf_op jit(solution)/shard_map/ppermute | solution.py:300
  111.9 0.9 collective-permute-done.6
  112.8 0.8 collective-permute-done.5
  113.6 0.1 maximum_maximum_fusion
  113.7 1.2 shard_map.114
  114.9 0.1 collective-permute-start.7
  115.0 1.5 %collective-permute-done.7 = bf16[4,2,1,2,1,2,2,8,256]{8,7,6,5,3,2,1,0,4:T(8,128)(2,1)S(1)} collective-permute-done((bf16[4,2,1,2,1,2,2,8,256]{8,7,6,5,3,2,1,0,4:T(8,128)(2,1)S(1)}, bf16[4,2,1,2,1,2,2,8,256]{8,7,6,5,3,2,1,0,4:T(8,128)(2,1)S(1)}, u32[]{:S(2)}, u32[]{:S(2)}) %collective-permute-start.7) | collective-permute-done | bytes 262176 | tf_op jit(solution)/shard_map/ppermute | solution.py:300
  116.5 2.9 %collective-permute-start.8 = (bf16[1,2,2,2,1,2,2,8,256]{8,7,6,5,3,2,1,0,4:T(8,128)(2,1)S(1)}, bf16[1,2,2,2,1,2,2,8,256]{8,7,6,5,3,2,1,0,4:T(8,128)(2,1)S(1)}, u32[]{:S(2)}, u32[]{:S(2)}) collective-permute-start(bf16[1,2,2,2,1,2,2,8,256]{8,7,6,5,3,2,1,0,4:T(8,128)(2,1)S(1)} %get-tuple-element.19), channel_id=1, source_target_pairs={{0,8},{1,9},{2,10},{3,11},{4,12},{5,13},{6,14},{7,15},{8,0},{9,1},... | collective-permute-start | bytes 393224 | tf_op jit(solution)/shard_map/ppermute | solution.py:300
  119.4 1.3 collective-permute-start.10
  120.7 0.2 collective-permute-start.9
  120.9 2.3 %collective-permute-done.8 = bf16[1,2,2,2,1,2,2,8,256]{8,7,6,5,3,2,1,0,4:T(8,128)(2,1)S(1)} collective-permute-done((bf16[1,2,2,2,1,2,2,8,256]{8,7,6,5,3,2,1,0,4:T(8,128)(2,1)S(1)}, bf16[1,2,2,2,1,2,2,8,256]{8,7,6,5,3,2,1,0,4:T(8,128)(2,1)S(1)}, u32[]{:S(2)}, u32[]{:S(2)}) %collective-permute-start.8) | collective-permute-done | bytes 131104 | tf_op jit(solution)/shard_map/ppermute | solution.py:300
  123.3 4.5 %collective-permute-done.10 = bf16[1,2,2,2,1,2,2,8,256]{8,7,6,5,3,2,1,0,4:T(8,128)(2,1)S(1)} collective-permute-done((bf16[1,2,2,2,1,2,2,8,256]{8,7,6,5,3,2,1,0,4:T(8,128)(2,1)S(1)}, bf16[1,2,2,2,1,2,2,8,256]{8,7,6,5,3,2,1,0,4:T(8,128)(2,1)S(1)}, u32[]{:S(2)}, u32[]{:S(2)}) %collective-permute-start.10) | collective-permute-done | bytes 131104 | tf_op jit(solution)/shard_map/ppermute | solution.py:300
  127.8 5.1 %collective-permute-done.9 = bf16[1,2,2,2,1,2,2,8,256]{8,7,6,5,3,2,1,0,4:T(8,128)(2,1)S(1)} collective-permute-done((bf16[1,2,2,2,1,2,2,8,256]{8,7,6,5,3,2,1,0,4:T(8,128)(2,1)S(1)}, bf16[1,2,2,2,1,2,2,8,256]{8,7,6,5,3,2,1,0,4:T(8,128)(2,1)S(1)}, u32[]{:S(2)}, u32[]{:S(2)}) %collective-permute-start.9) | collective-permute-done | bytes 131104 | tf_op jit(solution)/shard_map/ppermute | solution.py:300
  132.9 0.1 pad_maximum_fusion.1
  133.0 2.5 %collective-permute-start.13 = (bf16[4,1,2,1,1,2,2,8,256]{8,7,6,5,3,2,1,0,4:T(8,128)(2,1)S(1)}, bf16[4,1,2,1,1,2,2,8,256]{8,7,6,5,3,2,1,0,4:T(8,128)(2,1)S(1)}, u32[]{:S(2)}, u32[]{:S(2)}) collective-permute-start(bf16[4,1,2,1,1,2,2,8,256]{8,7,6,5,3,2,1,0,4:T(8,128)(2,1)S(1)} %get-tuple-element.15), channel_id=1, source_target_pairs={{0,5},{1,4},{2,7},{3,6},{4,1},{5,0},{6,3},{7,2},{8,13},{9,12},{10,... | collective-permute-start | bytes 393224 | tf_op jit(solution)/shard_map/ppermute | solution.py:300
  135.5 0.6 collective-permute-start.12
  136.1 0.5 collective-permute-start.11
  136.6 3.7 %collective-permute-done.13 = bf16[4,1,2,1,1,2,2,8,256]{8,7,6,5,3,2,1,0,4:T(8,128)(2,1)S(1)} collective-permute-done((bf16[4,1,2,1,1,2,2,8,256]{8,7,6,5,3,2,1,0,4:T(8,128)(2,1)S(1)}, bf16[4,1,2,1,1,2,2,8,256]{8,7,6,5,3,2,1,0,4:T(8,128)(2,1)S(1)}, u32[]{:S(2)}, u32[]{:S(2)}) %collective-permute-start.13) | collective-permute-done | bytes 131104 | tf_op jit(solution)/shard_map/ppermute | solution.py:300
  140.3 1.4 collective-permute-done.12
  141.7 0.1 collective-permute-done.11
  141.7 0.1 maximum_maximum_fusion.1
  141.8 2.3 %shard_map.115 = (bf16[4,2,1,2,256,256]{5,4,3,2,1,0:T(8,128)(2,1)}, bf16[4,2,1,2,256,256]{5,4,3,2,1,0:T(8,128)(2,1)}) custom-call(bf16[32,1,2,2,8,256]{5,4,3,2,1,0:T(8,128)(2,1)S(1)} %bitcast.18, bf16[4,2,1,2,256,256]{5,4,3,2,1,0:T(8,128)(2,1)S(1)} %copy-done), custom_call_target="tpu_custom_call" | custom-call | flops 536870912 | bytes 4194304 | tf_op jit(solution)/shard_map/pallas_call | solution.py:271
  144.1 0.0 all-to-all-done.1.s_ref
  144.1 6.5 %shard_map.116 = (bf16[4,2,1,2,256,256]{5,4,3,2,1,0:T(8,128)(2,1)}, bf16[4,2,1,2,256,256]{5,4,3,2,1,0:T(8,128)(2,1)}) custom-call(bf16[32,3,2,2,8,256]{5,4,3,2,1,0:T(8,128)(2,1)} %all-to-all-done.1.s_ref, bf16[4,2,1,2,256,256]{5,4,3,2,1,0:T(8,128)(2,1)S(1)} %copy-done, ...), custom_call_target="tpu_custom_call", output_to_operand_aliasing={{0}: (2, {}), {1}: (3, {})} | custom-call | flops 1610612736 | bytes 12582912 | tf_op jit(solution)/shard_map/pallas_call | solution.py:271
  (8 shorter events, 0.2 us)
Async XLA Ops:
  3.0 7.4 %copy-start.3 = (f32[16,4,2048]{2,1,0:T(4,128)S(1)}, f32[16,4,2048]{2,1,0:T(4,128)}, u32[]{:S(2)}) copy-start(f32[16,4,2048]{2,1,0:T(4,128)} %param.11) | copy-start | bytes 1572868
  3.0 44.8 %copy-start.1 = (bf16[256,768]{1,0:T(8,128)(2,1)S(1)}, bf16[256,768]{1,0:T(8,128)(2,1)}, u32[]{:S(2)}) copy-start(bf16[256,768]{1,0:T(8,128)(2,1)} %constant.16.inv_ref) | copy-start | bytes 1179652
  3.0 44.8 %copy-start.2 = (bf16[256,512]{1,0:T(8,128)(2,1)S(1)}, bf16[256,512]{1,0:T(8,128)(2,1)}, u32[]{:S(2)}) copy-start(bf16[256,512]{1,0:T(8,128)(2,1)} %constant.11.fwd_ref) | copy-start | bytes 786436
  3.1 44.8 %all-to-all-start = ((bf16[32,3,2,2,8,256]{5,4,3,2,1,0:T(8,128)(2,1)}), bf16[32,3,2,2,8,256]{5,4,3,2,1,0:T(8,128)(2,1)S(1)}, u32[]{:S(2)}, u32[]{:S(2)}) async-start(bf16[32,3,2,2,8,256]{5,4,3,2,1,0:T(8,128)(2,1)} %by_device.1), calls=%async_computation | async-start | bytes 3145728 | tf_op jit(solution)/shard_map/all_to_all | solution.py:288
  52.1 91.9 %all-to-all-start.1 = ((bf16[32,3,2,2,8,256]{5,4,3,2,1,0:T(8,128)(2,1)}), bf16[32,3,2,2,8,256]{5,4,3,2,1,0:T(8,128)(2,1)}, u32[]{:S(2)}, u32[]{:S(2)}) async-start(bf16[32,3,2,2,8,256]{5,4,3,2,1,0:T(8,128)(2,1)} %shard_map.113), calls=%async_computation.1 | async-start | bytes 3145728 | tf_op jit(solution)/shard_map/all_to_all | solution.py:288
  57.0 27.9 %collective-permute-start = (bf16[1,2,2,2,1,2,2,8,256]{8,7,6,5,3,2,1,0,4:T(8,128)(2,1)S(1)}, bf16[1,2,2,2,1,2,2,8,256]{8,7,6,5,3,2,1,0,4:T(8,128)(2,1)S(1)}, u32[]{:S(2)}, u32[]{:S(2)}) collective-permute-start(bf16[1,2,2,2,1,2,2,8,256]{8,7,6,5,3,2,1,0,4:T(8,128)(2,1)S(1)} %bitcast.24), channel_id=1, source_target_pairs={{0,8},{1,9},{2,10},{3,11},{4,12},{5,13},{6,14},{7,15},{8,0},{9,1},... | collective-permute-start | bytes 393224 | tf_op jit(solution)/shard_map/ppermute | solution.py:300
  58.8 43.4 %collective-permute-start.1 = (bf16[1,2,2,2,1,2,2,8,256]{8,7,6,5,3,2,1,0,4:T(8,128)(2,1)S(1)}, bf16[1,2,2,2,1,2,2,8,256]{8,7,6,5,3,2,1,0,4:T(8,128)(2,1)S(1)}, u32[]{:S(2)}, u32[]{:S(2)}) collective-permute-start(bf16[1,2,2,2,1,2,2,8,256]{8,7,6,5,3,2,1,0,4:T(8,128)(2,1)S(1)} %bitcast.23), channel_id=1, source_target_pairs={{0,16},{1,17},{2,18},{3,19},{4,20},{5,21},{6,22},{7,23},{8,24},{9,... | collective-permute-start | bytes 393224 | tf_op jit(solution)/shard_map/ppermute | solution.py:300
  61.2 41.0 %collective-permute-start.2 = (bf16[1,2,2,2,1,2,2,8,256]{8,7,6,5,3,2,1,0,4:T(8,128)(2,1)S(1)}, bf16[1,2,2,2,1,2,2,8,256]{8,7,6,5,3,2,1,0,4:T(8,128)(2,1)S(1)}, u32[]{:S(2)}, u32[]{:S(2)}) collective-permute-start(bf16[1,2,2,2,1,2,2,8,256]{8,7,6,5,3,2,1,0,4:T(8,128)(2,1)S(1)} %bitcast.22), channel_id=1, source_target_pairs={{0,24},{1,25},{2,26},{3,27},{4,28},{5,29},{6,30},{7,31},{8,16},{9,... | collective-permute-start | bytes 393224 | tf_op jit(solution)/shard_map/ppermute | solution.py:300
  102.3 1.6 %collective-permute-start.3 = (bf16[4,2,1,2,1,2,2,8,256]{8,7,6,5,3,2,1,0,4:T(8,128)(2,1)S(1)}, bf16[4,2,1,2,1,2,2,8,256]{8,7,6,5,3,2,1,0,4:T(8,128)(2,1)S(1)}, u32[]{:S(2)}, u32[]{:S(2)}) collective-permute-start(bf16[4,2,1,2,1,2,2,8,256]{8,7,6,5,3,2,1,0,4:T(8,128)(2,1)S(1)} %get-tuple-element.29), channel_id=1, source_target_pairs={{0,2},{1,3},{2,0},{3,1},{4,6},{5,7},{6,4},{7,5},{8,10},{9,11},{10,... | collective-permute-start | bytes 786440 | tf_op jit(solution)/shard_map/ppermute | solution.py:300
  104.0 8.0 %collective-permute-start.4 = (bf16[4,1,2,1,1,2,2,8,256]{8,7,6,5,3,2,1,0,4:T(8,128)(2,1)S(1)}, bf16[4,1,2,1,1,2,2,8,256]{8,7,6,5,3,2,1,0,4:T(8,128)(2,1)S(1)}, u32[]{:S(2)}, u32[]{:S(2)}) collective-permute-start(bf16[4,1,2,1,1,2,2,8,256]{8,7,6,5,3,2,1,0,4:T(8,128)(2,1)S(1)} %get-tuple-element.25), channel_id=1, source_target_pairs={{0,1},{1,0},{2,3},{3,2},{4,5},{5,4},{6,7},{7,6},{8,9},{9,8},{10,11... | collective-permute-start | bytes 393224 | tf_op jit(solution)/shard_map/ppermute | solution.py:300
  105.6 7.3 %collective-permute-start.6 = (bf16[4,1,2,1,1,2,2,8,256]{8,7,6,5,3,2,1,0,4:T(8,128)(2,1)S(1)}, bf16[4,1,2,1,1,2,2,8,256]{8,7,6,5,3,2,1,0,4:T(8,128)(2,1)S(1)}, u32[]{:S(2)}, u32[]{:S(2)}) collective-permute-start(bf16[4,1,2,1,1,2,2,8,256]{8,7,6,5,3,2,1,0,4:T(8,128)(2,1)S(1)} %get-tuple-element.26), channel_id=1, source_target_pairs={{0,5},{1,4},{2,7},{3,6},{4,1},{5,0},{6,3},{7,2},{8,13},{9,12},{10,... | collective-permute-start | bytes 393224 | tf_op jit(solution)/shard_map/ppermute | solution.py:300
  107.1 6.5 %collective-permute-start.5 = (bf16[4,1,2,1,1,2,2,8,256]{8,7,6,5,3,2,1,0,4:T(8,128)(2,1)S(1)}, bf16[4,1,2,1,1,2,2,8,256]{8,7,6,5,3,2,1,0,4:T(8,128)(2,1)S(1)}, u32[]{:S(2)}, u32[]{:S(2)}) collective-permute-start(bf16[4,1,2,1,1,2,2,8,256]{8,7,6,5,3,2,1,0,4:T(8,128)(2,1)S(1)} %get-tuple-element.27), channel_id=1, source_target_pairs={{0,4},{1,5},{2,6},{3,7},{4,0},{5,1},{6,2},{7,3},{8,12},{9,13},{10,... | collective-permute-start | bytes 393224 | tf_op jit(solution)/shard_map/ppermute | solution.py:300
  114.9 1.6 %collective-permute-start.7 = (bf16[4,2,1,2,1,2,2,8,256]{8,7,6,5,3,2,1,0,4:T(8,128)(2,1)S(1)}, bf16[4,2,1,2,1,2,2,8,256]{8,7,6,5,3,2,1,0,4:T(8,128)(2,1)S(1)}, u32[]{:S(2)}, u32[]{:S(2)}) collective-permute-start(bf16[4,2,1,2,1,2,2,8,256]{8,7,6,5,3,2,1,0,4:T(8,128)(2,1)S(1)} %get-tuple-element.23), channel_id=1, source_target_pairs={{0,2},{1,3},{2,0},{3,1},{4,6},{5,7},{6,4},{7,5},{8,10},{9,11},{10,... | collective-permute-start | bytes 786440 | tf_op jit(solution)/shard_map/ppermute | solution.py:300
  116.5 25.3 %copy-start = (bf16[4,2,1,2,256,256]{5,4,3,2,1,0:T(8,128)(2,1)S(1)}, bf16[4,2,1,2,256,256]{5,4,3,2,1,0:T(8,128)(2,1)}, u32[]{:S(2)}) copy-start(bf16[4,2,1,2,256,256]{5,4,3,2,1,0:T(8,128)(2,1)} %g_ref.3) | copy-start | bytes 6291460
  116.5 6.8 %collective-permute-start.8 = (bf16[1,2,2,2,1,2,2,8,256]{8,7,6,5,3,2,1,0,4:T(8,128)(2,1)S(1)}, bf16[1,2,2,2,1,2,2,8,256]{8,7,6,5,3,2,1,0,4:T(8,128)(2,1)S(1)}, u32[]{:S(2)}, u32[]{:S(2)}) collective-permute-start(bf16[1,2,2,2,1,2,2,8,256]{8,7,6,5,3,2,1,0,4:T(8,128)(2,1)S(1)} %get-tuple-element.19), channel_id=1, source_target_pairs={{0,8},{1,9},{2,10},{3,11},{4,12},{5,13},{6,14},{7,15},{8,0},{9,1},... | collective-permute-start | bytes 393224 | tf_op jit(solution)/shard_map/ppermute | solution.py:300
  119.4 8.3 %collective-permute-start.10 = (bf16[1,2,2,2,1,2,2,8,256]{8,7,6,5,3,2,1,0,4:T(8,128)(2,1)S(1)}, bf16[1,2,2,2,1,2,2,8,256]{8,7,6,5,3,2,1,0,4:T(8,128)(2,1)S(1)}, u32[]{:S(2)}, u32[]{:S(2)}) collective-permute-start(bf16[1,2,2,2,1,2,2,8,256]{8,7,6,5,3,2,1,0,4:T(8,128)(2,1)S(1)} %get-tuple-element.20), channel_id=1, source_target_pairs={{0,24},{1,25},{2,26},{3,27},{4,28},{5,29},{6,30},{7,31},{8,16},{9,... | collective-permute-start | bytes 393224 | tf_op jit(solution)/shard_map/ppermute | solution.py:300
  120.7 12.2 %collective-permute-start.9 = (bf16[1,2,2,2,1,2,2,8,256]{8,7,6,5,3,2,1,0,4:T(8,128)(2,1)S(1)}, bf16[1,2,2,2,1,2,2,8,256]{8,7,6,5,3,2,1,0,4:T(8,128)(2,1)S(1)}, u32[]{:S(2)}, u32[]{:S(2)}) collective-permute-start(bf16[1,2,2,2,1,2,2,8,256]{8,7,6,5,3,2,1,0,4:T(8,128)(2,1)S(1)} %get-tuple-element.21), channel_id=1, source_target_pairs={{0,16},{1,17},{2,18},{3,19},{4,20},{5,21},{6,22},{7,23},{8,24},{9,... | collective-permute-start | bytes 393224 | tf_op jit(solution)/shard_map/ppermute | solution.py:300
  133.0 7.3 %collective-permute-start.13 = (bf16[4,1,2,1,1,2,2,8,256]{8,7,6,5,3,2,1,0,4:T(8,128)(2,1)S(1)}, bf16[4,1,2,1,1,2,2,8,256]{8,7,6,5,3,2,1,0,4:T(8,128)(2,1)S(1)}, u32[]{:S(2)}, u32[]{:S(2)}) collective-permute-start(bf16[4,1,2,1,1,2,2,8,256]{8,7,6,5,3,2,1,0,4:T(8,128)(2,1)S(1)} %get-tuple-element.15), channel_id=1, source_target_pairs={{0,5},{1,4},{2,7},{3,6},{4,1},{5,0},{6,3},{7,2},{8,13},{9,12},{10,... | collective-permute-start | bytes 393224 | tf_op jit(solution)/shard_map/ppermute | solution.py:300
  135.5 6.2 %collective-permute-start.12 = (bf16[4,1,2,1,1,2,2,8,256]{8,7,6,5,3,2,1,0,4:T(8,128)(2,1)S(1)}, bf16[4,1,2,1,1,2,2,8,256]{8,7,6,5,3,2,1,0,4:T(8,128)(2,1)S(1)}, u32[]{:S(2)}, u32[]{:S(2)}) collective-permute-start(bf16[4,1,2,1,1,2,2,8,256]{8,7,6,5,3,2,1,0,4:T(8,128)(2,1)S(1)} %get-tuple-element.16), channel_id=1, source_target_pairs={{0,4},{1,5},{2,6},{3,7},{4,0},{5,1},{6,2},{7,3},{8,12},{9,13},{10,... | collective-permute-start | bytes 393224 | tf_op jit(solution)/shard_map/ppermute | solution.py:300
  136.1 5.7 %collective-permute-start.11 = (bf16[4,1,2,1,1,2,2,8,256]{8,7,6,5,3,2,1,0,4:T(8,128)(2,1)S(1)}, bf16[4,1,2,1,1,2,2,8,256]{8,7,6,5,3,2,1,0,4:T(8,128)(2,1)S(1)}, u32[]{:S(2)}, u32[]{:S(2)}) collective-permute-start(bf16[4,1,2,1,1,2,2,8,256]{8,7,6,5,3,2,1,0,4:T(8,128)(2,1)S(1)} %get-tuple-element.17), channel_id=1, source_target_pairs={{0,1},{1,0},{2,3},{3,2},{4,5},{5,4},{6,7},{7,6},{8,9},{9,8},{10,11... | collective-permute-start | bytes 393224 | tf_op jit(solution)/shard_map/ppermute | solution.py:300

commit v2 on v1

--- a/solution.py
+++ b/solution.py
@@ -74,12 +74,14 @@
     return lax.axis_index("krow") * kcols + lax.axis_index("kcol")
 
 
-def fourier_kernel(kcols, relative, x_ref, w_ref, fwd_ref, inv_ref, o_ref):
-    devices, _, _, kcol_each, rows, width = x_ref.shape
+def fourier_kernel(kcols, relative, x_ref, w_ref, fwd_ref, inv_ref, o_ref, *scratch):
+    devices, energies, _, kcol_each, rows, width = x_ref.shape
     k_one = devices // kcols
     size = k_one * 2 * rows
     me = own_index(kcols) if relative else 0
     spots = [(c, k) for c in range(kcols) for k in range(kcol_each)]
+    held = scratch[0] if scratch else o_ref
+    copies = []
 
     def slot(one, c):
         place = one * kcols + c
@@ -89,29 +91,35 @@
         parts = [x_ref[slot(one, c), e, :, k] for one in range(k_one)]
         return jnp.stack(parts, 0).reshape(size, width)
 
-    def store(c, k, value):
+    def store(c, e, k, value):
         for one in range(k_one):
-            o_ref[slot(one, c), 0, :, k] = value[one]
-
-    e = pl.program_id(0)
-    forward, inverse = fwd_ref[...], inv_ref[...]
-    state = []
-    for c, k in spots:
-        block = load(c, e, k)
-        block = jnp.concatenate((block, block), 0)
-        out = jnp.dot(forward, block, preferred_element_type=jnp.float32)
-        out = out.reshape(k_one, 2, rows, width)
-        state.append((out[:, 0], out[:, 1]))
-    state = turns(state, 1)
-    state = [(w_ref[:, r] * re, w_ref[:, r] * im) for r, (re, im) in enumerate(state)]
-    state = turns(state, -1)
-    for (c, k), (re, im) in zip(spots, state):
-        block = jnp.stack((re, im), 1).reshape(size, width)
-        high = block.astype(jnp.bfloat16)
-        low = (block - high.astype(jnp.float32)).astype(jnp.bfloat16)
-        block = jnp.concatenate((high, high, low), 0)
-        out = jnp.dot(inverse, block, preferred_element_type=jnp.float32)
-        store(c, k, out.astype(jnp.bfloat16).reshape(k_one, 2, rows, width))
+            held[slot(one, c), e, :, k] = value[one]
+
+    for e in range(energies):
+        state = []
+        for c, k in spots:
+            block = load(c, e, k)
+            block = jnp.concatenate((block, block), 0)
+            out = jnp.dot(fwd_ref[...], block, preferred_element_type=jnp.float32)
+            out = out.reshape(k_one, 2, rows, width)
+            state.append((out[:, 0], out[:, 1]))
+        state = turns(state, 1)
+        state = [(w_ref[:, r] * re, w_ref[:, r] * im) for r, (re, im) in enumerate(state)]
+        state = turns(state, -1)
+        for (c, k), (re, im) in zip(spots, state):
+            block = jnp.stack((re, im), 1).reshape(size, width)
+            high = block.astype(jnp.bfloat16)
+            low = (block - high.astype(jnp.float32)).astype(jnp.bfloat16)
+            block = jnp.concatenate((high, high, low), 0)
+            out = jnp.dot(inv_ref[...], block, preferred_element_type=jnp.float32)
+            store(c, e, k, out.astype(jnp.bfloat16).reshape(k_one, 2, rows, width))
+        if scratch:
+            copies.append(
+                pltpu.make_async_copy(held.at[:, e], o_ref.at[:, e], scratch[1].at[e])
+            )
+            copies[-1].start()
+    for copy in copies:
+        copy.wait()
 
 
 LOCAL = pl.BlockSpec(memory_space=pltpu.VMEM)
@@ -129,23 +137,23 @@
 
 
 def fourier(pieces, weights, kcols, relative):
-    _, energies, parts, each, rows, width = pieces.shape
+    _, energies, parts, _, rows, width = pieces.shape
     k_one, k_two = weights.shape[:2]
     forward, inverse = row_tables(k_one, k_two, rows)
     size = k_one * parts * rows
     return pl.pallas_call(
         functools.partial(fourier_kernel, kcols, relative),
-        grid=(energies,),
         in_specs=[LOCAL] * 4,
-        out_specs=pl.BlockSpec(
-            (pieces.shape[0], 1, parts, each, rows, width), lambda e: (0, e, 0, 0, 0, 0)
-        ),
+        out_specs=pl.BlockSpec(memory_space=pltpu.VMEM if relative else pltpu.HBM),
         out_shape=(pltpu.VMEM if relative else pltpu.HBM)(pieces.shape, jnp.bfloat16),
         cost_estimate=pl.CostEstimate(
             flops=2 * 5 * size * size * width * k_two * energies,
             bytes_accessed=4 * pieces.size + 4 * weights.size,
             transcendentals=0,
         ),
+        scratch_shapes=()
+        if relative
+        else [pltpu.VMEM(pieces.shape, jnp.bfloat16), pltpu.SemaphoreType.DMA((energies,))],
         compiler_params=PARAMS,
     )(near(pieces), near(weights), near(forward), near(inverse))
 
@@ -232,56 +240,70 @@
 
 
 def dyson_kernel(first, kcols, relative, s_ref, g_ref, *refs):
-    so_ref, d_ref = refs[-2:]
-    devices, orbitals = s_ref.shape[0], g_ref.shape[-1]
-    e, k = pl.program_id(0), pl.program_id(1)
+    so_ref, d_ref, s_held, d_held, s_sems, d_sems = refs[-6:]
+    devices, energies, parts, each, _, orbitals = s_ref.shape
+    me = own_index(kcols) if relative else 0
+    copies = []
+
+    def send(source, target, sem):
+        copies.append(pltpu.make_async_copy(source, target, sem))
+        copies[-1].start()
+
+    def product(ar, ai, br, bi):
+        right = jnp.concatenate((br, bi), 0)
+        dot = lambda left: jnp.dot(left, right, preferred_element_type=jnp.float32)
+        return dot(jnp.concatenate((ar, -ai), 1)), dot(jnp.concatenate((ai, ar), 1))
+
+    spots = [(e, k) for e in range(energies) for k in range(each)]
     if relative:
-        me = own_index(kcols)
-        load = lambda p: jnp.stack([s_ref[d ^ me, e, p, k] for d in range(devices)], 0)
-    else:
-        load = lambda p: s_ref[:, e, p, k]
-    sr, si = (load(p).reshape(orbitals, orbitals) for p in range(2))
-    so_ref[0, 0, 0, 0] = sr
-    so_ref[0, 1, 0, 0] = si
-    gr, gi = g_ref[first + e, 0, 0, k], g_ref[first + e, 1, 0, k]
-
-    def product(ar, ai, br, bi):
-        left = jnp.concatenate(
-            (jnp.concatenate((ar, -ai), 1), jnp.concatenate((ai, ar), 1)), 0
-        )
-        right = jnp.concatenate((br, bi), 0)
-        out = jnp.dot(left, right, preferred_element_type=jnp.float32)
-        return out[:orbitals], out[orbitals:]
-
-    kr, ki = (a.astype(jnp.bfloat16) for a in product(gr, gi, sr, si))
-    cr, ci = product(kr, ki, gr, gi)
-    scale = 1.0 / orbitals
-    dr = gr.astype(jnp.float32) + cr * scale
-    di = gi.astype(jnp.float32) + ci * scale
-    d_ref[0, 0, 0, 0] = dr.astype(jnp.bfloat16)
-    d_ref[0, 1, 0, 0] = di.astype(jnp.bfloat16)
+        for d in range(devices):
+            s_held[d] = s_ref[d ^ me]
+    whole_ref = s_held if relative else s_ref
+    for e, k in spots:
+        for p in range(parts):
+            source = whole_ref.at[:, e, p, k]
+            send(source, so_ref.at[first + e, p, k], s_sems.at[e, p, k])
+    for e, k in spots:
+        load = lambda p: whole_ref[:, e, p, k]
+        sr, si = (load(p).reshape(orbitals, orbitals) for p in range(2))
+        gr, gi = g_ref[e, 0, 0, k], g_ref[e, 1, 0, k]
+        kr, ki = (a.astype(jnp.bfloat16) for a in product(gr, gi, sr, si))
+        out = product(kr, ki, gr, gi)
+        for p, (whole, change) in enumerate(zip((gr, gi), out)):
+            whole = whole.astype(jnp.float32) + change * (1.0 / orbitals)
+            d_held[e, p, k] = whole.astype(jnp.bfloat16)
+            send(d_held.at[e, p, k], d_ref.at[first + e, p, 0, k], d_sems.at[e, p, k])
+    for copy in copies:
+        copy.wait()
 
 
 def dyson(pieces, green, first, kcols, relative, earlier):
-    _, energies, parts, each, _, orbitals = pieces.shape
-    flat = pl.BlockSpec(
-        (1, parts, 1, 1, orbitals, orbitals), lambda e, k: (first + e, 0, 0, k, 0, 0)
-    )
-    shape = pltpu.HBM(green.shape, jnp.bfloat16)
+    devices, energies, parts, each, rows, orbitals = pieces.shape
+    own = green[first : first + energies]
+    split = (energies, parts, each, devices, rows, orbitals)
+    far_spec = pl.BlockSpec(memory_space=pltpu.HBM)
     return pl.pallas_call(
         functools.partial(dyson_kernel, first, kcols, relative),
-        grid=(energies, each),
-        in_specs=[LOCAL, LOCAL] + [pl.BlockSpec(memory_space=pltpu.HBM)] * len(earlier),
-        out_specs=[flat, flat],
-        out_shape=[shape, shape],
+        in_specs=[LOCAL, LOCAL] + [far_spec] * len(earlier),
+        out_specs=[far_spec, far_spec],
+        out_shape=[
+            pltpu.HBM((green.shape[0],) + split[1:], jnp.bfloat16),
+            pltpu.HBM(green.shape, jnp.bfloat16),
+        ],
         input_output_aliases={2 + n: n for n in range(len(earlier))},
+        scratch_shapes=[
+            pltpu.VMEM(pieces.shape if relative else (1,) * 5 + (orbitals,), jnp.bfloat16),
+            pltpu.VMEM(split[:3] + (orbitals, orbitals), jnp.bfloat16),
+            pltpu.SemaphoreType.DMA(split[:3]),
+            pltpu.SemaphoreType.DMA(split[:3]),
+        ],
         cost_estimate=pl.CostEstimate(
             flops=16 * orbitals**3 * each * energies,
             bytes_accessed=16 * pieces.size,
             transcendentals=0,
         ),
         compiler_params=PARAMS,
-    )(near(pieces), near(green), *earlier)
+    )(near(pieces), near(own), *earlier)
 
 
 def exchange(blocks):
@@ -299,11 +321,9 @@
             pairs = [(d, d ^ offset) for d in range(devices)]
             return lax.ppermute(part, AXES, pairs)
         dim, rest = left[0], left[1:]
-        cut = (
-            part
-            if isinstance(part, (list, tuple))
-            else [lax.slice_in_dim(part, q, q + 1, axis=dim) for q in range(counts[dim])]
-        )
+        cut = part
+        if not isinstance(part, (list, tuple)):
+            cut = [lax.slice_in_dim(part, q, q + 1, axis=dim) for q in range(counts[dim])]
         back = [level(c, rest, offset + q * strides[dim]) for q, c in enumerate(cut)]
         return lax.concatenate(back, dim)
 
@@ -333,21 +353,24 @@
     main = energies - aside
     earlier = ()
     if aside:
-        counts = (krows // 4, 2, 2, kcols)
-        cut = by_offset(blocks, main, aside, kcols, counts[0])
-        side = Side(counts, [c.reshape((1,) + counts[1:] + c.shape[1:]) for c in cut])
-        side = swap(side, (0,))
-        side = swap(side, (2,))
-        side = swap(side, (1, 3))
+        counts = (krows // 8, 2, 2, 2, kcols)
+        cut = by_offset(blocks, main, aside, kcols, 2 * counts[0])
+        cut = [c.reshape((1, 1) + counts[2:] + c.shape[1:]) for c in cut]
+        side = Side(counts, [cut[2 * h : 2 * h + 2] for h in range(counts[0])])
+        side = swap(side, (0, 1))
+        side = swap(side, (3,))
+        side = swap(side, (2, 4))
         turned = fourier(side.merged(), weights, kcols, True)
         side = swap(Side.of(counts, turned), (2,))
-        side = swap(side, (0,))
-        side = swap(side, (1, 3))
+        side = swap(side, (0, 1))
+        side = swap(side, (3,))
+        side = swap(side, (4,))
         earlier = dyson(side.merged(), green, main, kcols, True, ())
     middle = exchange(by_device(blocks, main))
     middle = fourier(middle, weights, kcols, False)
     middle = exchange(middle)
-    return tuple(dyson(middle, green, 0, kcols, False, earlier))
+    sigma, dressed = dyson(middle, green, 0, kcols, False, earlier)
+    return sigma.reshape(green.shape), dressed
 
 
 def solution(mesh):

time: 151 us -> 127 us (0.84)
  waiting for transfers between devices: 104 us -> 81.4 us
  Pallas kernels: 17.8 us -> 13.8 us
    ppermute x14 -> x13, waiting for transfers between devices: 67 us -> 44.7 us  [level(): return lax.ppermute(part, AXES, pairs)]
    pallas_call x4, Pallas kernels: 14.2 us -> 10.2 us  [the longest x2 5.12 us: fourier(): pl.pallas_call(functools.partial(fourier_kernel, kcols, relative), in_spe...]
    ppermute x14 -> x13, starting transfers between devices: 16.1 us -> 17.2 us  [level(): return lax.ppermute(part, AXES, pairs)]
  transfers between devices with their start and end apart: 16 -> 15, of which waited for: 14 -> 11; matrix products, arithmetic and copies ran while one was open for 0% -> 2% of each run, Pallas kernels for 3% -> 6%
where the time goes in v2:
time: 127 us; the launch traced here: 126 us
  waiting for transfers between devices  81.4 us (64%)
  starting transfers between devices  27.7 us (22%)
  Pallas kernels  13.8 us (11%)
  local copies, waits for them, and re-layouts  1.6 us (1%)
    ppermute x13, waiting for transfers between devices, level(): return lax.ppermute(part, AXES, pairs)  44.7 us
    all_to_all x2, waiting for transfers between devices, exchange(): return lax.all_to_all(blocks, AXES, split_axis=0, concat_axis=0, tiled=True)  36.6 us
    ppermute x13, starting transfers between devices, level(): return lax.ppermute(part, AXES, pairs)  17.2 us
    all_to_all x2, starting transfers between devices, exchange(): return lax.all_to_all(blocks, AXES, split_axis=0, concat_axis=0, tiled=True)  10.5 us
    pallas_call x2, Pallas kernels, fourier(): pl.pallas_call(functools.partial(fourier_kernel, kcols, relative), in_spe...  5.12 us
    pallas_call x2, Pallas kernels, dyson(): pl.pallas_call(functools.partial(dyson_kernel, first, kcols, relative), i...  5.08 us
  transfers between devices with their start and end apart: 15, of which 11 were waited for; matrix products, arithmetic and copies ran while one was open for 2% of the time, Pallas kernels for 6%

profile of v2, /device:TPU:0, one launch (start us, length us, event | category | flops | bytes accessed | tf_op | source)
XLA Modules:
  0.0 126.5 jit_solution(13320531285223123526)
XLA Ops:
  0.6 2.4 %by_device.1 = bf16[32,3,2,2,8,256]{5,4,3,2,1,0:T(8,128)(2,1)} custom-call(bf16[4,2,2,32,8,256]{5,4,3,2,1,0:T(8,128)(2,1)} %bitcast.26), custom_call_target="tpu_custom_call" | custom-call | tf_op jit(solution)/shard_map/by_device/pallas_call | solution.py:191
  3.0 7.3 %all-to-all-start = ((bf16[32,3,2,2,8,256]{5,4,3,2,1,0:T(8,128)(2,1)}), bf16[32,3,2,2,8,256]{5,4,3,2,1,0:T(8,128)(2,1)S(1)}, u32[]{:S(2)}, u32[]{:S(2)}) async-start(bf16[32,3,2,2,8,256]{5,4,3,2,1,0:T(8,128)(2,1)} %by_device.1), calls=%async_computation | async-start | bytes 3145728 | tf_op jit(solution)/shard_map/all_to_all | solution.py:310
  10.4 0.0 copy-start
  10.4 0.0 copy-start.1
  10.4 1.2 by_offset.1
  11.6 1.8 %collective-permute-start = (bf16[1,1,2,2,2,1,2,2,8,256]{9,8,7,6,4,3,2,1,0,5:T(8,128)(2,1)S(1)}, bf16[1,1,2,2,2,1,2,2,8,256]{9,8,7,6,4,3,2,1,0,5:T(8,128)(2,1)S(1)}, u32[]{:S(2)}, u32[]{:S(2)}) collective-permute-start(bf16[1,1,2,2,2,1,2,2,8,256]{9,8,7,6,4,3,2,1,0,5:T(8,128)(2,1)S(1)} %bitcast.25), channel_id=1, source_target_pairs={{0,8},{1,9},{2,10},{3,11},{4,12},{5,13},{6,14},{7,15},{8,0},{9,1},... | collective-permute-start | bytes 393224 | tf_op jit(solution)/shard_map/ppermute | solution.py:322
  13.4 2.4 %collective-permute-start.1 = (bf16[1,1,2,2,2,1,2,2,8,256]{9,8,7,6,4,3,2,1,0,5:T(8,128)(2,1)S(1)}, bf16[1,1,2,2,2,1,2,2,8,256]{9,8,7,6,4,3,2,1,0,5:T(8,128)(2,1)S(1)}, u32[]{:S(2)}, u32[]{:S(2)}) collective-permute-start(bf16[1,1,2,2,2,1,2,2,8,256]{9,8,7,6,4,3,2,1,0,5:T(8,128)(2,1)S(1)} %bitcast.24), channel_id=1, source_target_pairs={{0,16},{1,17},{2,18},{3,19},{4,20},{5,21},{6,22},{7,23},{8,24},{9,... | collective-permute-start | bytes 393224 | tf_op jit(solution)/shard_map/ppermute | solution.py:322
  15.9 0.2 collective-permute-start.2
  16.1 1.3 %reshape.35.w_ref = f32[16,4,8,256]{3,2,1,0:T(8,128)S(1)} reshape(f32[16,4,2048]{2,1,0:T(4,128)} %param.11) | data formatting | bytes 1048576 | tf_op jit(solution)/shard_map/reshape | solution.py:350
  17.4 36.6 %all-to-all-done.x_ref = bf16[32,3,2,2,8,256]{5,4,3,2,1,0:T(8,128)(2,1)S(1)} async-done(((bf16[32,3,2,2,8,256]{5,4,3,2,1,0:T(8,128)(2,1)}), bf16[32,3,2,2,8,256]{5,4,3,2,1,0:T(8,128)(2,1)S(1)}, u32[]{:S(2)}, u32[]{:S(2)}) %all-to-all-start) | async-done | bytes 1572896 | tf_op jit(solution)/shard_map/all_to_all | solution.py:310
  54.0 0.0 copy-done
  54.0 0.0 copy-done.1
  54.0 4.0 %shard_map.113 = bf16[32,3,2,2,8,256]{5,4,3,2,1,0:T(8,128)(2,1)} custom-call(bf16[32,3,2,2,8,256]{5,4,3,2,1,0:T(8,128)(2,1)S(1)} %all-to-all-done.x_ref, f32[16,4,8,256]{3,2,1,0:T(8,128)S(1)} %reshape.35.w_ref, bf16[256,512]{1,0:T(8,128)(2,1)S(1)} %copy-done.1, bf16[256,768]{1,0:T(8,128)(2,1)S(1)} %copy-done), custom_call_target="tpu_custom_call" | custom-call | flops 2013265920 | bytes 3670016 | tf_op jit(solution)/shard_map/pallas_call | solution.py:144
  57.9 3.2 %all-to-all-start.1 = ((bf16[32,3,2,2,8,256]{5,4,3,2,1,0:T(8,128)(2,1)}), bf16[32,3,2,2,8,256]{5,4,3,2,1,0:T(8,128)(2,1)S(1)}, u32[]{:S(2)}, u32[]{:S(2)}) async-start(bf16[32,3,2,2,8,256]{5,4,3,2,1,0:T(8,128)(2,1)} %shard_map.113), calls=%async_computation.1 | async-start | bytes 3145728 | tf_op jit(solution)/shard_map/all_to_all | solution.py:310
  61.1 0.0 collective-permute-done
  61.2 0.0 collective-permute-done.1
  61.2 0.0 collective-permute-done.2
  61.2 1.0 maximum_maximum_fusion
  62.2 0.3 collective-permute-start.3
  62.5 1.3 %collective-permute-done.3 = bf16[2,2,2,1,2,1,2,2,8,256]{9,8,7,6,4,3,2,1,0,5:T(8,128)(2,1)S(1)} collective-permute-done((bf16[2,2,2,1,2,1,2,2,8,256]{9,8,7,6,4,3,2,1,0,5:T(8,128)(2,1)S(1)}, bf16[2,2,2,1,2,1,2,2,8,256]{9,8,7,6,4,3,2,1,0,5:T(8,128)(2,1)S(1)}, u32[]{:S(2)}, u32[]{:S(2)}) %collective-permute-start.3) | collective-permute-done | bytes 262176 | tf_op jit(solution)/shard_map/ppermute | solution.py:322
  63.8 1.8 %collective-permute-start.4 = (bf16[2,2,1,2,1,1,2,2,8,256]{9,8,7,6,4,3,2,1,0,5:T(8,128)(2,1)S(1)}, bf16[2,2,1,2,1,1,2,2,8,256]{9,8,7,6,4,3,2,1,0,5:T(8,128)(2,1)S(1)}, u32[]{:S(2)}, u32[]{:S(2)}) collective-permute-start(bf16[2,2,1,2,1,1,2,2,8,256]{9,8,7,6,4,3,2,1,0,5:T(8,128)(2,1)S(1)} %get-tuple-element.31), channel_id=1, source_target_pairs={{0,1},{1,0},{2,3},{3,2},{4,5},{5,4},{6,7},{7,6},{8,9},{9,8},{10,11... | collective-permute-start | bytes 393224 | tf_op jit(solution)/shard_map/ppermute | solution.py:322
  65.7 1.5 %collective-permute-start.6 = (bf16[2,2,1,2,1,1,2,2,8,256]{9,8,7,6,4,3,2,1,0,5:T(8,128)(2,1)S(1)}, bf16[2,2,1,2,1,1,2,2,8,256]{9,8,7,6,4,3,2,1,0,5:T(8,128)(2,1)S(1)}, u32[]{:S(2)}, u32[]{:S(2)}) collective-permute-start(bf16[2,2,1,2,1,1,2,2,8,256]{9,8,7,6,4,3,2,1,0,5:T(8,128)(2,1)S(1)} %get-tuple-element.32), channel_id=1, source_target_pairs={{0,5},{1,4},{2,7},{3,6},{4,1},{5,0},{6,3},{7,2},{8,13},{9,12},{10,... | collective-permute-start | bytes 393224 | tf_op jit(solution)/shard_map/ppermute | solution.py:322
  67.1 0.3 collective-permute-start.5
  67.4 12.0 %collective-permute-done.4 = bf16[2,2,1,2,1,1,2,2,8,256]{9,8,7,6,4,3,2,1,0,5:T(8,128)(2,1)S(1)} collective-permute-done((bf16[2,2,1,2,1,1,2,2,8,256]{9,8,7,6,4,3,2,1,0,5:T(8,128)(2,1)S(1)}, bf16[2,2,1,2,1,1,2,2,8,256]{9,8,7,6,4,3,2,1,0,5:T(8,128)(2,1)S(1)}, u32[]{:S(2)}, u32[]{:S(2)}) %collective-permute-start.4) | collective-permute-done | bytes 131104 | tf_op jit(solution)/shard_map/ppermute | solution.py:322
  79.3 2.2 %collective-permute-done.6 = bf16[2,2,1,2,1,1,2,2,8,256]{9,8,7,6,4,3,2,1,0,5:T(8,128)(2,1)S(1)} collective-permute-done((bf16[2,2,1,2,1,1,2,2,8,256]{9,8,7,6,4,3,2,1,0,5:T(8,128)(2,1)S(1)}, bf16[2,2,1,2,1,1,2,2,8,256]{9,8,7,6,4,3,2,1,0,5:T(8,128)(2,1)S(1)}, u32[]{:S(2)}, u32[]{:S(2)}) %collective-permute-start.6) | collective-permute-done | bytes 131104 | tf_op jit(solution)/shard_map/ppermute | solution.py:322
  81.6 0.4 collective-permute-done.5
  82.0 0.1 maximum_maximum_fusion.1
  82.0 1.2 shard_map.114
  83.2 2.6 %collective-permute-start.7 = (bf16[2,2,1,2,2,1,2,2,8,256]{9,8,7,6,4,3,2,1,0,5:T(8,128)(2,1)S(1)}, bf16[2,2,1,2,2,1,2,2,8,256]{9,8,7,6,4,3,2,1,0,5:T(8,128)(2,1)S(1)}, u32[]{:S(2)}, u32[]{:S(2)}) collective-permute-start(bf16[2,2,1,2,2,1,2,2,8,256]{9,8,7,6,4,3,2,1,0,5:T(8,128)(2,1)S(1)} %get-tuple-element.29), channel_id=1, source_target_pairs={{0,4},{1,5},{2,6},{3,7},{4,0},{5,1},{6,2},{7,3},{8,12},{9,13},{10,... | collective-permute-start | bytes 786440 | tf_op jit(solution)/shard_map/ppermute | solution.py:322
  85.8 8.1 %collective-permute-done.7 = bf16[2,2,1,2,2,1,2,2,8,256]{9,8,7,6,4,3,2,1,0,5:T(8,128)(2,1)S(1)} collective-permute-done((bf16[2,2,1,2,2,1,2,2,8,256]{9,8,7,6,4,3,2,1,0,5:T(8,128)(2,1)S(1)}, bf16[2,2,1,2,2,1,2,2,8,256]{9,8,7,6,4,3,2,1,0,5:T(8,128)(2,1)S(1)}, u32[]{:S(2)}, u32[]{:S(2)}) %collective-permute-start.7) | collective-permute-done | bytes 262176 | tf_op jit(solution)/shard_map/ppermute | solution.py:322
  93.9 0.0 copy-start.2
  94.0 2.8 %collective-permute-start.8 = (bf16[1,1,2,2,2,1,2,2,8,256]{9,8,7,6,4,3,2,1,0,5:T(8,128)(2,1)S(1)}, bf16[1,1,2,2,2,1,2,2,8,256]{9,8,7,6,4,3,2,1,0,5:T(8,128)(2,1)S(1)}, u32[]{:S(2)}, u32[]{:S(2)}) collective-permute-start(bf16[1,1,2,2,2,1,2,2,8,256]{9,8,7,6,4,3,2,1,0,5:T(8,128)(2,1)S(1)} %get-tuple-element.25), channel_id=1, source_target_pairs={{0,8},{1,9},{2,10},{3,11},{4,12},{5,13},{6,14},{7,15},{8,0},{9,1},... | collective-permute-start | bytes 393224 | tf_op jit(solution)/shard_map/ppermute | solution.py:322
  96.8 2.6 %collective-permute-start.10 = (bf16[1,1,2,2,2,1,2,2,8,256]{9,8,7,6,4,3,2,1,0,5:T(8,128)(2,1)S(1)}, bf16[1,1,2,2,2,1,2,2,8,256]{9,8,7,6,4,3,2,1,0,5:T(8,128)(2,1)S(1)}, u32[]{:S(2)}, u32[]{:S(2)}) collective-permute-start(bf16[1,1,2,2,2,1,2,2,8,256]{9,8,7,6,4,3,2,1,0,5:T(8,128)(2,1)S(1)} %get-tuple-element.26), channel_id=1, source_target_pairs={{0,24},{1,25},{2,26},{3,27},{4,28},{5,29},{6,30},{7,31},{8,16},{9,... | collective-permute-start | bytes 393224 | tf_op jit(solution)/shard_map/ppermute | solution.py:322
  99.4 0.5 collective-permute-start.9
  99.9 1.8 %collective-permute-done.8 = bf16[1,1,2,2,2,1,2,2,8,256]{9,8,7,6,4,3,2,1,0,5:T(8,128)(2,1)S(1)} collective-permute-done((bf16[1,1,2,2,2,1,2,2,8,256]{9,8,7,6,4,3,2,1,0,5:T(8,128)(2,1)S(1)}, bf16[1,1,2,2,2,1,2,2,8,256]{9,8,7,6,4,3,2,1,0,5:T(8,128)(2,1)S(1)}, u32[]{:S(2)}, u32[]{:S(2)}) %collective-permute-start.8) | collective-permute-done | bytes 131104 | tf_op jit(solution)/shard_map/ppermute | solution.py:322
  101.7 4.9 %collective-permute-done.10 = bf16[1,1,2,2,2,1,2,2,8,256]{9,8,7,6,4,3,2,1,0,5:T(8,128)(2,1)S(1)} collective-permute-done((bf16[1,1,2,2,2,1,2,2,8,256]{9,8,7,6,4,3,2,1,0,5:T(8,128)(2,1)S(1)}, bf16[1,1,2,2,2,1,2,2,8,256]{9,8,7,6,4,3,2,1,0,5:T(8,128)(2,1)S(1)}, u32[]{:S(2)}, u32[]{:S(2)}) %collective-permute-start.10) | collective-permute-done | bytes 131104 | tf_op jit(solution)/shard_map/ppermute | solution.py:322
  106.5 4.6 %collective-permute-done.9 = bf16[1,1,2,2,2,1,2,2,8,256]{9,8,7,6,4,3,2,1,0,5:T(8,128)(2,1)S(1)} collective-permute-done((bf16[1,1,2,2,2,1,2,2,8,256]{9,8,7,6,4,3,2,1,0,5:T(8,128)(2,1)S(1)}, bf16[1,1,2,2,2,1,2,2,8,256]{9,8,7,6,4,3,2,1,0,5:T(8,128)(2,1)S(1)}, u32[]{:S(2)}, u32[]{:S(2)}) %collective-permute-start.9) | collective-permute-done | bytes 131104 | tf_op jit(solution)/shard_map/ppermute | solution.py:322
  111.3 0.1 collective-permute-start.11
  111.3 1.5 %collective-permute-done.11 = bf16[2,2,2,1,2,1,2,2,8,256]{9,8,7,6,4,3,2,1,0,5:T(8,128)(2,1)S(1)} collective-permute-done((bf16[2,2,2,1,2,1,2,2,8,256]{9,8,7,6,4,3,2,1,0,5:T(8,128)(2,1)S(1)}, bf16[2,2,2,1,2,1,2,2,8,256]{9,8,7,6,4,3,2,1,0,5:T(8,128)(2,1)S(1)}, u32[]{:S(2)}, u32[]{:S(2)}) %collective-permute-start.11) | collective-permute-done | bytes 262176 | tf_op jit(solution)/shard_map/ppermute | solution.py:322
  112.9 0.3 collective-permute-start.12
  113.2 0.0 copy-done.2
  113.3 0.1 slice.66.g_ref
  113.4 8.0 %collective-permute-done.12 = bf16[2,2,2,2,1,1,2,2,8,256]{9,8,7,6,4,3,2,1,0,5:T(8,128)(2,1)S(1)} collective-permute-done((bf16[2,2,2,2,1,1,2,2,8,256]{9,8,7,6,4,3,2,1,0,5:T(8,128)(2,1)S(1)}, bf16[2,2,2,2,1,1,2,2,8,256]{9,8,7,6,4,3,2,1,0,5:T(8,128)(2,1)S(1)}, u32[]{:S(2)}, u32[]{:S(2)}) %collective-permute-start.12) | collective-permute-done | bytes 262176 | tf_op jit(solution)/shard_map/ppermute | solution.py:322
  121.3 0.1 pad_maximum_fusion
  121.4 1.7 %shard_map.115 = (bf16[4,2,2,32,8,256]{5,4,3,2,1,0:T(8,128)(2,1)}, bf16[4,2,1,2,256,256]{5,4,3,2,1,0:T(8,128)(2,1)}) custom-call(bf16[32,1,2,2,8,256]{5,4,3,2,1,0:T(8,128)(2,1)S(1)} %bitcast.21, bf16[1,2,1,2,256,256]{5,4,3,2,1,0:T(8,128)(2,1)S(1)} %slice.83.g_ref), custom_call_target="tpu_custom_call" | custom-call | flops 536870912 | bytes 4194304 | tf_op jit(solution)/shard_map/pallas_call | solution.py:285
  123.0 0.0 all-to-all-done.1.s_ref
  123.1 3.4 %shard_map.116 = (bf16[4,2,2,32,8,256]{5,4,3,2,1,0:T(8,128)(2,1)}, bf16[4,2,1,2,256,256]{5,4,3,2,1,0:T(8,128)(2,1)}) custom-call(bf16[32,3,2,2,8,256]{5,4,3,2,1,0:T(8,128)(2,1)S(1)} %all-to-all-done.1.s_ref, bf16[3,2,1,2,256,256]{5,4,3,2,1,0:T(8,128)(2,1)S(1)} %slice.66.g_ref, ...), custom_call_target="tpu_custom_call", output_to_operand_aliasing={{0}: (2, {}), {1}: (3, {})} | custom-call | flops 1610612736 | bytes 12582912 | tf_op jit(solution)/shard_map/pallas_call | solution.py:285
  (8 shorter events, 0.3 us)
Async XLA Ops:
  3.0 51.0 %all-to-all-start = ((bf16[32,3,2,2,8,256]{5,4,3,2,1,0:T(8,128)(2,1)}), bf16[32,3,2,2,8,256]{5,4,3,2,1,0:T(8,128)(2,1)S(1)}, u32[]{:S(2)}, u32[]{:S(2)}) async-start(bf16[32,3,2,2,8,256]{5,4,3,2,1,0:T(8,128)(2,1)} %by_device.1), calls=%async_computation | async-start | bytes 3145728 | tf_op jit(solution)/shard_map/all_to_all | solution.py:310
  10.4 43.6 %copy-start = (bf16[256,768]{1,0:T(8,128)(2,1)S(1)}, bf16[256,768]{1,0:T(8,128)(2,1)}, u32[]{:S(2)}) copy-start(bf16[256,768]{1,0:T(8,128)(2,1)} %constant.16.inv_ref) | copy-start | bytes 1179652
  10.4 43.6 %copy-start.1 = (bf16[256,512]{1,0:T(8,128)(2,1)S(1)}, bf16[256,512]{1,0:T(8,128)(2,1)}, u32[]{:S(2)}) copy-start(bf16[256,512]{1,0:T(8,128)(2,1)} %constant.11.fwd_ref) | copy-start | bytes 786436
  11.6 49.5 %collective-permute-start = (bf16[1,1,2,2,2,1,2,2,8,256]{9,8,7,6,4,3,2,1,0,5:T(8,128)(2,1)S(1)}, bf16[1,1,2,2,2,1,2,2,8,256]{9,8,7,6,4,3,2,1,0,5:T(8,128)(2,1)S(1)}, u32[]{:S(2)}, u32[]{:S(2)}) collective-permute-start(bf16[1,1,2,2,2,1,2,2,8,256]{9,8,7,6,4,3,2,1,0,5:T(8,128)(2,1)S(1)} %bitcast.25), channel_id=1, source_target_pairs={{0,8},{1,9},{2,10},{3,11},{4,12},{5,13},{6,14},{7,15},{8,0},{9,1},... | collective-permute-start | bytes 393224 | tf_op jit(solution)/shard_map/ppermute | solution.py:322
  13.4 47.7 %collective-permute-start.1 = (bf16[1,1,2,2,2,1,2,2,8,256]{9,8,7,6,4,3,2,1,0,5:T(8,128)(2,1)S(1)}, bf16[1,1,2,2,2,1,2,2,8,256]{9,8,7,6,4,3,2,1,0,5:T(8,128)(2,1)S(1)}, u32[]{:S(2)}, u32[]{:S(2)}) collective-permute-start(bf16[1,1,2,2,2,1,2,2,8,256]{9,8,7,6,4,3,2,1,0,5:T(8,128)(2,1)S(1)} %bitcast.24), channel_id=1, source_target_pairs={{0,16},{1,17},{2,18},{3,19},{4,20},{5,21},{6,22},{7,23},{8,24},{9,... | collective-permute-start | bytes 393224 | tf_op jit(solution)/shard_map/ppermute | solution.py:322
  15.9 45.3 %collective-permute-start.2 = (bf16[1,1,2,2,2,1,2,2,8,256]{9,8,7,6,4,3,2,1,0,5:T(8,128)(2,1)S(1)}, bf16[1,1,2,2,2,1,2,2,8,256]{9,8,7,6,4,3,2,1,0,5:T(8,128)(2,1)}, u32[]{:S(2)}, u32[]{:S(2)}) collective-permute-start(bf16[1,1,2,2,2,1,2,2,8,256]{9,8,7,6,4,3,2,1,0,5:T(8,128)(2,1)S(1)} %bitcast.23), channel_id=1, source_target_pairs={{0,24},{1,25},{2,26},{3,27},{4,28},{5,29},{6,30},{7,31},{8,16},{9,... | collective-permute-start | bytes 393224 | tf_op jit(solution)/shard_map/ppermute | solution.py:322
  57.9 65.1 %all-to-all-start.1 = ((bf16[32,3,2,2,8,256]{5,4,3,2,1,0:T(8,128)(2,1)}), bf16[32,3,2,2,8,256]{5,4,3,2,1,0:T(8,128)(2,1)S(1)}, u32[]{:S(2)}, u32[]{:S(2)}) async-start(bf16[32,3,2,2,8,256]{5,4,3,2,1,0:T(8,128)(2,1)} %shard_map.113), calls=%async_computation.1 | async-start | bytes 3145728 | tf_op jit(solution)/shard_map/all_to_all | solution.py:310
  62.2 1.6 %collective-permute-start.3 = (bf16[2,2,2,1,2,1,2,2,8,256]{9,8,7,6,4,3,2,1,0,5:T(8,128)(2,1)S(1)}, bf16[2,2,2,1,2,1,2,2,8,256]{9,8,7,6,4,3,2,1,0,5:T(8,128)(2,1)S(1)}, u32[]{:S(2)}, u32[]{:S(2)}) collective-permute-start(bf16[2,2,2,1,2,1,2,2,8,256]{9,8,7,6,4,3,2,1,0,5:T(8,128)(2,1)S(1)} %get-tuple-element.35), channel_id=1, source_target_pairs={{0,2},{1,3},{2,0},{3,1},{4,6},{5,7},{6,4},{7,5},{8,10},{9,11},{10,... | collective-permute-start | bytes 786440 | tf_op jit(solution)/shard_map/ppermute | solution.py:322
  63.8 15.5 %collective-permute-start.4 = (bf16[2,2,1,2,1,1,2,2,8,256]{9,8,7,6,4,3,2,1,0,5:T(8,128)(2,1)S(1)}, bf16[2,2,1,2,1,1,2,2,8,256]{9,8,7,6,4,3,2,1,0,5:T(8,128)(2,1)S(1)}, u32[]{:S(2)}, u32[]{:S(2)}) collective-permute-start(bf16[2,2,1,2,1,1,2,2,8,256]{9,8,7,6,4,3,2,1,0,5:T(8,128)(2,1)S(1)} %get-tuple-element.31), channel_id=1, source_target_pairs={{0,1},{1,0},{2,3},{3,2},{4,5},{5,4},{6,7},{7,6},{8,9},{9,8},{10,11... | collective-permute-start | bytes 393224 | tf_op jit(solution)/shard_map/ppermute | solution.py:322
  65.7 15.9 %collective-permute-start.6 = (bf16[2,2,1,2,1,1,2,2,8,256]{9,8,7,6,4,3,2,1,0,5:T(8,128)(2,1)S(1)}, bf16[2,2,1,2,1,1,2,2,8,256]{9,8,7,6,4,3,2,1,0,5:T(8,128)(2,1)S(1)}, u32[]{:S(2)}, u32[]{:S(2)}) collective-permute-start(bf16[2,2,1,2,1,1,2,2,8,256]{9,8,7,6,4,3,2,1,0,5:T(8,128)(2,1)S(1)} %get-tuple-element.32), channel_id=1, source_target_pairs={{0,5},{1,4},{2,7},{3,6},{4,1},{5,0},{6,3},{7,2},{8,13},{9,12},{10,... | collective-permute-start | bytes 393224 | tf_op jit(solution)/shard_map/ppermute | solution.py:322
  67.1 14.8 %collective-permute-start.5 = (bf16[2,2,1,2,1,1,2,2,8,256]{9,8,7,6,4,3,2,1,0,5:T(8,128)(2,1)S(1)}, bf16[2,2,1,2,1,1,2,2,8,256]{9,8,7,6,4,3,2,1,0,5:T(8,128)(2,1)S(1)}, u32[]{:S(2)}, u32[]{:S(2)}) collective-permute-start(bf16[2,2,1,2,1,1,2,2,8,256]{9,8,7,6,4,3,2,1,0,5:T(8,128)(2,1)S(1)} %get-tuple-element.33), channel_id=1, source_target_pairs={{0,4},{1,5},{2,6},{3,7},{4,0},{5,1},{6,2},{7,3},{8,12},{9,13},{10,... | collective-permute-start | bytes 393224 | tf_op jit(solution)/shard_map/ppermute | solution.py:322
  83.2 10.7 %collective-permute-start.7 = (bf16[2,2,1,2,2,1,2,2,8,256]{9,8,7,6,4,3,2,1,0,5:T(8,128)(2,1)S(1)}, bf16[2,2,1,2,2,1,2,2,8,256]{9,8,7,6,4,3,2,1,0,5:T(8,128)(2,1)S(1)}, u32[]{:S(2)}, u32[]{:S(2)}) collective-permute-start(bf16[2,2,1,2,2,1,2,2,8,256]{9,8,7,6,4,3,2,1,0,5:T(8,128)(2,1)S(1)} %get-tuple-element.29), channel_id=1, source_target_pairs={{0,4},{1,5},{2,6},{3,7},{4,0},{5,1},{6,2},{7,3},{8,12},{9,13},{10,... | collective-permute-start | bytes 786440 | tf_op jit(solution)/shard_map/ppermute | solution.py:322
  93.9 19.3 %copy-start.2 = (bf16[4,2,1,2,256,256]{5,4,3,2,1,0:T(8,128)(2,1)S(1)}, bf16[4,2,1,2,256,256]{5,4,3,2,1,0:T(8,128)(2,1)}, u32[]{:S(2)}) copy-start(bf16[4,2,1,2,256,256]{5,4,3,2,1,0:T(8,128)(2,1)} %param.10) | copy-start | bytes 6291460
  94.0 7.7 %collective-permute-start.8 = (bf16[1,1,2,2,2,1,2,2,8,256]{9,8,7,6,4,3,2,1,0,5:T(8,128)(2,1)S(1)}, bf16[1,1,2,2,2,1,2,2,8,256]{9,8,7,6,4,3,2,1,0,5:T(8,128)(2,1)S(1)}, u32[]{:S(2)}, u32[]{:S(2)}) collective-permute-start(bf16[1,1,2,2,2,1,2,2,8,256]{9,8,7,6,4,3,2,1,0,5:T(8,128)(2,1)S(1)} %get-tuple-element.25), channel_id=1, source_target_pairs={{0,8},{1,9},{2,10},{3,11},{4,12},{5,13},{6,14},{7,15},{8,0},{9,1},... | collective-permute-start | bytes 393224 | tf_op jit(solution)/shard_map/ppermute | solution.py:322
  96.8 9.8 %collective-permute-start.10 = (bf16[1,1,2,2,2,1,2,2,8,256]{9,8,7,6,4,3,2,1,0,5:T(8,128)(2,1)S(1)}, bf16[1,1,2,2,2,1,2,2,8,256]{9,8,7,6,4,3,2,1,0,5:T(8,128)(2,1)S(1)}, u32[]{:S(2)}, u32[]{:S(2)}) collective-permute-start(bf16[1,1,2,2,2,1,2,2,8,256]{9,8,7,6,4,3,2,1,0,5:T(8,128)(2,1)S(1)} %get-tuple-element.26), channel_id=1, source_target_pairs={{0,24},{1,25},{2,26},{3,27},{4,28},{5,29},{6,30},{7,31},{8,16},{9,... | collective-permute-start | bytes 393224 | tf_op jit(solution)/shard_map/ppermute | solution.py:322
  99.4 11.8 %collective-permute-start.9 = (bf16[1,1,2,2,2,1,2,2,8,256]{9,8,7,6,4,3,2,1,0,5:T(8,128)(2,1)S(1)}, bf16[1,1,2,2,2,1,2,2,8,256]{9,8,7,6,4,3,2,1,0,5:T(8,128)(2,1)S(1)}, u32[]{:S(2)}, u32[]{:S(2)}) collective-permute-start(bf16[1,1,2,2,2,1,2,2,8,256]{9,8,7,6,4,3,2,1,0,5:T(8,128)(2,1)S(1)} %get-tuple-element.27), channel_id=1, source_target_pairs={{0,16},{1,17},{2,18},{3,19},{4,20},{5,21},{6,22},{7,23},{8,24},{9,... | collective-permute-start | bytes 393224 | tf_op jit(solution)/shard_map/ppermute | solution.py:322
  111.3 1.6 %collective-permute-start.11 = (bf16[2,2,2,1,2,1,2,2,8,256]{9,8,7,6,4,3,2,1,0,5:T(8,128)(2,1)S(1)}, bf16[2,2,2,1,2,1,2,2,8,256]{9,8,7,6,4,3,2,1,0,5:T(8,128)(2,1)S(1)}, u32[]{:S(2)}, u32[]{:S(2)}) collective-permute-start(bf16[2,2,2,1,2,1,2,2,8,256]{9,8,7,6,4,3,2,1,0,5:T(8,128)(2,1)S(1)} %get-tuple-element.23), channel_id=1, source_target_pairs={{0,2},{1,3},{2,0},{3,1},{4,6},{5,7},{6,4},{7,5},{8,10},{9,11},{10,... | collective-permute-start | bytes 786440 | tf_op jit(solution)/shard_map/ppermute | solution.py:322
  112.9 8.4 %collective-permute-start.12 = (bf16[2,2,2,2,1,1,2,2,8,256]{9,8,7,6,4,3,2,1,0,5:T(8,128)(2,1)S(1)}, bf16[2,2,2,2,1,1,2,2,8,256]{9,8,7,6,4,3,2,1,0,5:T(8,128)(2,1)S(1)}, u32[]{:S(2)}, u32[]{:S(2)}) collective-permute-start(bf16[2,2,2,2,1,1,2,2,8,256]{9,8,7,6,4,3,2,1,0,5:T(8,128)(2,1)S(1)} %get-tuple-element.21), channel_id=1, source_target_pairs={{0,1},{1,0},{2,3},{3,2},{4,5},{5,4},{6,7},{7,6},{8,9},{9,8},{10,11... | collective-permute-start | bytes 786440 | tf_op jit(solution)/shard_map/ppermute | solution.py:322

commit v3 on v2

--- a/solution.py
+++ b/solution.py
@@ -263,15 +263,22 @@
         for p in range(parts):
             source = whole_ref.at[:, e, p, k]
             send(source, so_ref.at[first + e, p, k], s_sems.at[e, p, k])
-    for e, k in spots:
-        load = lambda p: whole_ref[:, e, p, k]
-        sr, si = (load(p).reshape(orbitals, orbitals) for p in range(2))
-        gr, gi = g_ref[e, 0, 0, k], g_ref[e, 1, 0, k]
-        kr, ki = (a.astype(jnp.bfloat16) for a in product(gr, gi, sr, si))
-        out = product(kr, ki, gr, gi)
-        for p, (whole, change) in enumerate(zip((gr, gi), out)):
+
+    def first_product(e, k):
+        sr, si = (whole_ref[:, e, p, k].reshape(orbitals, orbitals) for p in range(2))
+        out = product(g_ref[e, 0, 0, k], g_ref[e, 1, 0, k], sr, si)
+        return [a.astype(jnp.bfloat16) for a in out]
+
+    ahead = [first_product(*spots[0])]
+    for n, (e, k) in enumerate(spots):
+        if n + 1 < len(spots):
+            ahead.append(first_product(*spots[n + 1]))
+        green = g_ref[e, 0, 0, k], g_ref[e, 1, 0, k]
+        out = product(*ahead[n], *green)
+        for p, (whole, change) in enumerate(zip(green, out)):
             whole = whole.astype(jnp.float32) + change * (1.0 / orbitals)
             d_held[e, p, k] = whole.astype(jnp.bfloat16)
+        for p in range(parts):
             send(d_held.at[e, p, k], d_ref.at[first + e, p, 0, k], d_sems.at[e, p, k])
     for copy in copies:
         copy.wait()

time: 127 us -> 126 us (level)
  no operation moved by 1% of the time
where the time goes in v3:
time: 126 us
  waiting for transfers between devices  81.4 us (65%)
  starting transfers between devices  27.7 us (22%)
  Pallas kernels  13.4 us (11%)
  local copies, waits for them, and re-layouts  1.6 us (1%)
    ppermute x13, waiting for transfers between devices, level(): return lax.ppermute(part, AXES, pairs)  44.7 us
    all_to_all x2, waiting for transfers between devices, exchange(): return lax.all_to_all(blocks, AXES, split_axis=0, concat_axis=0, tiled=True)  36.6 us
    ppermute x13, starting transfers between devices, level(): return lax.ppermute(part, AXES, pairs)  17.2 us
    all_to_all x2, starting transfers between devices, exchange(): return lax.all_to_all(blocks, AXES, split_axis=0, concat_axis=0, tiled=True)  10.5 us
    pallas_call x2, Pallas kernels, fourier(): pl.pallas_call(functools.partial(fourier_kernel, kcols, relative), in_spe...  5.12 us
    pallas_call x2, Pallas kernels, dyson(): pl.pallas_call(functools.partial(dyson_kernel, first, kcols, relative), i...  4.7 us
  transfers between devices with their start and end apart: 15, of which 11 were waited for; matrix products, arithmetic and copies ran while one was open for 2% of the time, Pallas kernels for 6%

profile of v3, /device:TPU:0, one launch (start us, length us, event | category | flops | bytes accessed | tf_op | source)
XLA Modules:
  0.0 126.1 jit_solution(4190161177611779513)
XLA Ops:
  0.6 2.4 %by_device.1 = bf16[32,3,2,2,8,256]{5,4,3,2,1,0:T(8,128)(2,1)} custom-call(bf16[4,2,2,32,8,256]{5,4,3,2,1,0:T(8,128)(2,1)} %bitcast.26), custom_call_target="tpu_custom_call" | custom-call | tf_op jit(solution)/shard_map/by_device/pallas_call | solution.py:191
  3.0 7.3 %all-to-all-start = ((bf16[32,3,2,2,8,256]{5,4,3,2,1,0:T(8,128)(2,1)}), bf16[32,3,2,2,8,256]{5,4,3,2,1,0:T(8,128)(2,1)S(1)}, u32[]{:S(2)}, u32[]{:S(2)}) async-start(bf16[32,3,2,2,8,256]{5,4,3,2,1,0:T(8,128)(2,1)} %by_device.1), calls=%async_computation | async-start | bytes 3145728 | tf_op jit(solution)/shard_map/all_to_all | solution.py:317
  10.4 0.0 copy-start
  10.4 0.0 copy-start.1
  10.4 1.2 by_offset.1
  11.6 1.8 %collective-permute-start = (bf16[1,1,2,2,2,1,2,2,8,256]{9,8,7,6,4,3,2,1,0,5:T(8,128)(2,1)S(1)}, bf16[1,1,2,2,2,1,2,2,8,256]{9,8,7,6,4,3,2,1,0,5:T(8,128)(2,1)S(1)}, u32[]{:S(2)}, u32[]{:S(2)}) collective-permute-start(bf16[1,1,2,2,2,1,2,2,8,256]{9,8,7,6,4,3,2,1,0,5:T(8,128)(2,1)S(1)} %bitcast.25), channel_id=1, source_target_pairs={{0,8},{1,9},{2,10},{3,11},{4,12},{5,13},{6,14},{7,15},{8,0},{9,1},... | collective-permute-start | bytes 393224 | tf_op jit(solution)/shard_map/ppermute | solution.py:329
  13.4 2.4 %collective-permute-start.1 = (bf16[1,1,2,2,2,1,2,2,8,256]{9,8,7,6,4,3,2,1,0,5:T(8,128)(2,1)S(1)}, bf16[1,1,2,2,2,1,2,2,8,256]{9,8,7,6,4,3,2,1,0,5:T(8,128)(2,1)S(1)}, u32[]{:S(2)}, u32[]{:S(2)}) collective-permute-start(bf16[1,1,2,2,2,1,2,2,8,256]{9,8,7,6,4,3,2,1,0,5:T(8,128)(2,1)S(1)} %bitcast.24), channel_id=1, source_target_pairs={{0,16},{1,17},{2,18},{3,19},{4,20},{5,21},{6,22},{7,23},{8,24},{9,... | collective-permute-start | bytes 393224 | tf_op jit(solution)/shard_map/ppermute | solution.py:329
  15.9 0.2 collective-permute-start.2
  16.1 1.3 %reshape.35.w_ref = f32[16,4,8,256]{3,2,1,0:T(8,128)S(1)} reshape(f32[16,4,2048]{2,1,0:T(4,128)} %param.11) | data formatting | bytes 1048576 | tf_op jit(solution)/shard_map/reshape | solution.py:357
  17.4 36.6 %all-to-all-done.x_ref = bf16[32,3,2,2,8,256]{5,4,3,2,1,0:T(8,128)(2,1)S(1)} async-done(((bf16[32,3,2,2,8,256]{5,4,3,2,1,0:T(8,128)(2,1)}), bf16[32,3,2,2,8,256]{5,4,3,2,1,0:T(8,128)(2,1)S(1)}, u32[]{:S(2)}, u32[]{:S(2)}) %all-to-all-start) | async-done | bytes 1572896 | tf_op jit(solution)/shard_map/all_to_all | solution.py:317
  54.0 0.0 copy-done
  54.0 0.0 copy-done.1
  54.0 4.0 %shard_map.113 = bf16[32,3,2,2,8,256]{5,4,3,2,1,0:T(8,128)(2,1)} custom-call(bf16[32,3,2,2,8,256]{5,4,3,2,1,0:T(8,128)(2,1)S(1)} %all-to-all-done.x_ref, f32[16,4,8,256]{3,2,1,0:T(8,128)S(1)} %reshape.35.w_ref, bf16[256,512]{1,0:T(8,128)(2,1)S(1)} %copy-done.1, bf16[256,768]{1,0:T(8,128)(2,1)S(1)} %copy-done), custom_call_target="tpu_custom_call" | custom-call | flops 2013265920 | bytes 3670016 | tf_op jit(solution)/shard_map/pallas_call | solution.py:144
  57.9 3.2 %all-to-all-start.1 = ((bf16[32,3,2,2,8,256]{5,4,3,2,1,0:T(8,128)(2,1)}), bf16[32,3,2,2,8,256]{5,4,3,2,1,0:T(8,128)(2,1)S(1)}, u32[]{:S(2)}, u32[]{:S(2)}) async-start(bf16[32,3,2,2,8,256]{5,4,3,2,1,0:T(8,128)(2,1)} %shard_map.113), calls=%async_computation.1 | async-start | bytes 3145728 | tf_op jit(solution)/shard_map/all_to_all | solution.py:317
  61.1 0.0 collective-permute-done
  61.2 0.0 collective-permute-done.1
  61.2 0.0 collective-permute-done.2
  61.2 1.0 maximum_maximum_fusion
  62.2 0.3 collective-permute-start.3
  62.5 1.3 %collective-permute-done.3 = bf16[2,2,2,1,2,1,2,2,8,256]{9,8,7,6,4,3,2,1,0,5:T(8,128)(2,1)S(1)} collective-permute-done((bf16[2,2,2,1,2,1,2,2,8,256]{9,8,7,6,4,3,2,1,0,5:T(8,128)(2,1)S(1)}, bf16[2,2,2,1,2,1,2,2,8,256]{9,8,7,6,4,3,2,1,0,5:T(8,128)(2,1)S(1)}, u32[]{:S(2)}, u32[]{:S(2)}) %collective-permute-start.3) | collective-permute-done | bytes 262176 | tf_op jit(solution)/shard_map/ppermute | solution.py:329
  63.8 1.8 %collective-permute-start.4 = (bf16[2,2,1,2,1,1,2,2,8,256]{9,8,7,6,4,3,2,1,0,5:T(8,128)(2,1)S(1)}, bf16[2,2,1,2,1,1,2,2,8,256]{9,8,7,6,4,3,2,1,0,5:T(8,128)(2,1)S(1)}, u32[]{:S(2)}, u32[]{:S(2)}) collective-permute-start(bf16[2,2,1,2,1,1,2,2,8,256]{9,8,7,6,4,3,2,1,0,5:T(8,128)(2,1)S(1)} %get-tuple-element.31), channel_id=1, source_target_pairs={{0,1},{1,0},{2,3},{3,2},{4,5},{5,4},{6,7},{7,6},{8,9},{9,8},{10,11... | collective-permute-start | bytes 393224 | tf_op jit(solution)/shard_map/ppermute | solution.py:329
  65.7 1.5 %collective-permute-start.6 = (bf16[2,2,1,2,1,1,2,2,8,256]{9,8,7,6,4,3,2,1,0,5:T(8,128)(2,1)S(1)}, bf16[2,2,1,2,1,1,2,2,8,256]{9,8,7,6,4,3,2,1,0,5:T(8,128)(2,1)S(1)}, u32[]{:S(2)}, u32[]{:S(2)}) collective-permute-start(bf16[2,2,1,2,1,1,2,2,8,256]{9,8,7,6,4,3,2,1,0,5:T(8,128)(2,1)S(1)} %get-tuple-element.32), channel_id=1, source_target_pairs={{0,5},{1,4},{2,7},{3,6},{4,1},{5,0},{6,3},{7,2},{8,13},{9,12},{10,... | collective-permute-start | bytes 393224 | tf_op jit(solution)/shard_map/ppermute | solution.py:329
  67.1 0.3 collective-permute-start.5
  67.4 12.0 %collective-permute-done.4 = bf16[2,2,1,2,1,1,2,2,8,256]{9,8,7,6,4,3,2,1,0,5:T(8,128)(2,1)S(1)} collective-permute-done((bf16[2,2,1,2,1,1,2,2,8,256]{9,8,7,6,4,3,2,1,0,5:T(8,128)(2,1)S(1)}, bf16[2,2,1,2,1,1,2,2,8,256]{9,8,7,6,4,3,2,1,0,5:T(8,128)(2,1)S(1)}, u32[]{:S(2)}, u32[]{:S(2)}) %collective-permute-start.4) | collective-permute-done | bytes 131104 | tf_op jit(solution)/shard_map/ppermute | solution.py:329
  79.3 2.2 %collective-permute-done.6 = bf16[2,2,1,2,1,1,2,2,8,256]{9,8,7,6,4,3,2,1,0,5:T(8,128)(2,1)S(1)} collective-permute-done((bf16[2,2,1,2,1,1,2,2,8,256]{9,8,7,6,4,3,2,1,0,5:T(8,128)(2,1)S(1)}, bf16[2,2,1,2,1,1,2,2,8,256]{9,8,7,6,4,3,2,1,0,5:T(8,128)(2,1)S(1)}, u32[]{:S(2)}, u32[]{:S(2)}) %collective-permute-start.6) | collective-permute-done | bytes 131104 | tf_op jit(solution)/shard_map/ppermute | solution.py:329
  81.6 0.4 collective-permute-done.5
  82.0 0.1 maximum_maximum_fusion.1
  82.0 1.2 shard_map.114
  83.2 2.6 %collective-permute-start.7 = (bf16[2,2,1,2,2,1,2,2,8,256]{9,8,7,6,4,3,2,1,0,5:T(8,128)(2,1)S(1)}, bf16[2,2,1,2,2,1,2,2,8,256]{9,8,7,6,4,3,2,1,0,5:T(8,128)(2,1)S(1)}, u32[]{:S(2)}, u32[]{:S(2)}) collective-permute-start(bf16[2,2,1,2,2,1,2,2,8,256]{9,8,7,6,4,3,2,1,0,5:T(8,128)(2,1)S(1)} %get-tuple-element.29), channel_id=1, source_target_pairs={{0,4},{1,5},{2,6},{3,7},{4,0},{5,1},{6,2},{7,3},{8,12},{9,13},{10,... | collective-permute-start | bytes 786440 | tf_op jit(solution)/shard_map/ppermute | solution.py:329
  85.8 8.1 %collective-permute-done.7 = bf16[2,2,1,2,2,1,2,2,8,256]{9,8,7,6,4,3,2,1,0,5:T(8,128)(2,1)S(1)} collective-permute-done((bf16[2,2,1,2,2,1,2,2,8,256]{9,8,7,6,4,3,2,1,0,5:T(8,128)(2,1)S(1)}, bf16[2,2,1,2,2,1,2,2,8,256]{9,8,7,6,4,3,2,1,0,5:T(8,128)(2,1)S(1)}, u32[]{:S(2)}, u32[]{:S(2)}) %collective-permute-start.7) | collective-permute-done | bytes 262176 | tf_op jit(solution)/shard_map/ppermute | solution.py:329
  93.9 0.0 copy-start.2
  94.0 2.8 %collective-permute-start.8 = (bf16[1,1,2,2,2,1,2,2,8,256]{9,8,7,6,4,3,2,1,0,5:T(8,128)(2,1)S(1)}, bf16[1,1,2,2,2,1,2,2,8,256]{9,8,7,6,4,3,2,1,0,5:T(8,128)(2,1)S(1)}, u32[]{:S(2)}, u32[]{:S(2)}) collective-permute-start(bf16[1,1,2,2,2,1,2,2,8,256]{9,8,7,6,4,3,2,1,0,5:T(8,128)(2,1)S(1)} %get-tuple-element.25), channel_id=1, source_target_pairs={{0,8},{1,9},{2,10},{3,11},{4,12},{5,13},{6,14},{7,15},{8,0},{9,1},... | collective-permute-start | bytes 393224 | tf_op jit(solution)/shard_map/ppermute | solution.py:329
  96.8 2.6 %collective-permute-start.10 = (bf16[1,1,2,2,2,1,2,2,8,256]{9,8,7,6,4,3,2,1,0,5:T(8,128)(2,1)S(1)}, bf16[1,1,2,2,2,1,2,2,8,256]{9,8,7,6,4,3,2,1,0,5:T(8,128)(2,1)S(1)}, u32[]{:S(2)}, u32[]{:S(2)}) collective-permute-start(bf16[1,1,2,2,2,1,2,2,8,256]{9,8,7,6,4,3,2,1,0,5:T(8,128)(2,1)S(1)} %get-tuple-element.26), channel_id=1, source_target_pairs={{0,24},{1,25},{2,26},{3,27},{4,28},{5,29},{6,30},{7,31},{8,16},{9,... | collective-permute-start | bytes 393224 | tf_op jit(solution)/shard_map/ppermute | solution.py:329
  99.4 0.5 collective-permute-start.9
  99.9 1.8 %collective-permute-done.8 = bf16[1,1,2,2,2,1,2,2,8,256]{9,8,7,6,4,3,2,1,0,5:T(8,128)(2,1)S(1)} collective-permute-done((bf16[1,1,2,2,2,1,2,2,8,256]{9,8,7,6,4,3,2,1,0,5:T(8,128)(2,1)S(1)}, bf16[1,1,2,2,2,1,2,2,8,256]{9,8,7,6,4,3,2,1,0,5:T(8,128)(2,1)S(1)}, u32[]{:S(2)}, u32[]{:S(2)}) %collective-permute-start.8) | collective-permute-done | bytes 131104 | tf_op jit(solution)/shard_map/ppermute | solution.py:329
  101.7 4.9 %collective-permute-done.10 = bf16[1,1,2,2,2,1,2,2,8,256]{9,8,7,6,4,3,2,1,0,5:T(8,128)(2,1)S(1)} collective-permute-done((bf16[1,1,2,2,2,1,2,2,8,256]{9,8,7,6,4,3,2,1,0,5:T(8,128)(2,1)S(1)}, bf16[1,1,2,2,2,1,2,2,8,256]{9,8,7,6,4,3,2,1,0,5:T(8,128)(2,1)S(1)}, u32[]{:S(2)}, u32[]{:S(2)}) %collective-permute-start.10) | collective-permute-done | bytes 131104 | tf_op jit(solution)/shard_map/ppermute | solution.py:329
  106.5 4.6 %collective-permute-done.9 = bf16[1,1,2,2,2,1,2,2,8,256]{9,8,7,6,4,3,2,1,0,5:T(8,128)(2,1)S(1)} collective-permute-done((bf16[1,1,2,2,2,1,2,2,8,256]{9,8,7,6,4,3,2,1,0,5:T(8,128)(2,1)S(1)}, bf16[1,1,2,2,2,1,2,2,8,256]{9,8,7,6,4,3,2,1,0,5:T(8,128)(2,1)S(1)}, u32[]{:S(2)}, u32[]{:S(2)}) %collective-permute-start.9) | collective-permute-done | bytes 131104 | tf_op jit(solution)/shard_map/ppermute | solution.py:329
  111.3 0.1 collective-permute-start.11
  111.3 1.5 %collective-permute-done.11 = bf16[2,2,2,1,2,1,2,2,8,256]{9,8,7,6,4,3,2,1,0,5:T(8,128)(2,1)S(1)} collective-permute-done((bf16[2,2,2,1,2,1,2,2,8,256]{9,8,7,6,4,3,2,1,0,5:T(8,128)(2,1)S(1)}, bf16[2,2,2,1,2,1,2,2,8,256]{9,8,7,6,4,3,2,1,0,5:T(8,128)(2,1)S(1)}, u32[]{:S(2)}, u32[]{:S(2)}) %collective-permute-start.11) | collective-permute-done | bytes 262176 | tf_op jit(solution)/shard_map/ppermute | solution.py:329
  112.9 0.3 collective-permute-start.12
  113.2 0.0 copy-done.2
  113.3 0.1 slice.66.g_ref
  113.4 8.0 %collective-permute-done.12 = bf16[2,2,2,2,1,1,2,2,8,256]{9,8,7,6,4,3,2,1,0,5:T(8,128)(2,1)S(1)} collective-permute-done((bf16[2,2,2,2,1,1,2,2,8,256]{9,8,7,6,4,3,2,1,0,5:T(8,128)(2,1)S(1)}, bf16[2,2,2,2,1,1,2,2,8,256]{9,8,7,6,4,3,2,1,0,5:T(8,128)(2,1)S(1)}, u32[]{:S(2)}, u32[]{:S(2)}) %collective-permute-start.12) | collective-permute-done | bytes 262176 | tf_op jit(solution)/shard_map/ppermute | solution.py:329
  121.3 0.1 pad_maximum_fusion
  121.4 1.6 %shard_map.115 = (bf16[4,2,2,32,8,256]{5,4,3,2,1,0:T(8,128)(2,1)}, bf16[4,2,1,2,256,256]{5,4,3,2,1,0:T(8,128)(2,1)}) custom-call(bf16[32,1,2,2,8,256]{5,4,3,2,1,0:T(8,128)(2,1)S(1)} %bitcast.21, bf16[1,2,1,2,256,256]{5,4,3,2,1,0:T(8,128)(2,1)S(1)} %slice.83.g_ref), custom_call_target="tpu_custom_call" | custom-call | flops 536870912 | bytes 4194304 | tf_op jit(solution)/shard_map/pallas_call | solution.py:292
  123.0 0.0 all-to-all-done.1.s_ref
  123.0 3.1 %shard_map.116 = (bf16[4,2,2,32,8,256]{5,4,3,2,1,0:T(8,128)(2,1)}, bf16[4,2,1,2,256,256]{5,4,3,2,1,0:T(8,128)(2,1)}) custom-call(bf16[32,3,2,2,8,256]{5,4,3,2,1,0:T(8,128)(2,1)S(1)} %all-to-all-done.1.s_ref, bf16[3,2,1,2,256,256]{5,4,3,2,1,0:T(8,128)(2,1)S(1)} %slice.66.g_ref, ...), custom_call_target="tpu_custom_call", output_to_operand_aliasing={{0}: (2, {}), {1}: (3, {})} | custom-call | flops 1610612736 | bytes 12582912 | tf_op jit(solution)/shard_map/pallas_call | solution.py:292
  (8 shorter events, 0.3 us)
Async XLA Ops:
  3.0 51.0 %all-to-all-start = ((bf16[32,3,2,2,8,256]{5,4,3,2,1,0:T(8,128)(2,1)}), bf16[32,3,2,2,8,256]{5,4,3,2,1,0:T(8,128)(2,1)S(1)}, u32[]{:S(2)}, u32[]{:S(2)}) async-start(bf16[32,3,2,2,8,256]{5,4,3,2,1,0:T(8,128)(2,1)} %by_device.1), calls=%async_computation | async-start | bytes 3145728 | tf_op jit(solution)/shard_map/all_to_all | solution.py:317
  10.4 43.6 %copy-start = (bf16[256,768]{1,0:T(8,128)(2,1)S(1)}, bf16[256,768]{1,0:T(8,128)(2,1)}, u32[]{:S(2)}) copy-start(bf16[256,768]{1,0:T(8,128)(2,1)} %constant.16.inv_ref) | copy-start | bytes 1179652
  10.4 43.6 %copy-start.1 = (bf16[256,512]{1,0:T(8,128)(2,1)S(1)}, bf16[256,512]{1,0:T(8,128)(2,1)}, u32[]{:S(2)}) copy-start(bf16[256,512]{1,0:T(8,128)(2,1)} %constant.11.fwd_ref) | copy-start | bytes 786436
  11.6 49.5 %collective-permute-start = (bf16[1,1,2,2,2,1,2,2,8,256]{9,8,7,6,4,3,2,1,0,5:T(8,128)(2,1)S(1)}, bf16[1,1,2,2,2,1,2,2,8,256]{9,8,7,6,4,3,2,1,0,5:T(8,128)(2,1)S(1)}, u32[]{:S(2)}, u32[]{:S(2)}) collective-permute-start(bf16[1,1,2,2,2,1,2,2,8,256]{9,8,7,6,4,3,2,1,0,5:T(8,128)(2,1)S(1)} %bitcast.25), channel_id=1, source_target_pairs={{0,8},{1,9},{2,10},{3,11},{4,12},{5,13},{6,14},{7,15},{8,0},{9,1},... | collective-permute-start | bytes 393224 | tf_op jit(solution)/shard_map/ppermute | solution.py:329
  13.4 47.7 %collective-permute-start.1 = (bf16[1,1,2,2,2,1,2,2,8,256]{9,8,7,6,4,3,2,1,0,5:T(8,128)(2,1)S(1)}, bf16[1,1,2,2,2,1,2,2,8,256]{9,8,7,6,4,3,2,1,0,5:T(8,128)(2,1)S(1)}, u32[]{:S(2)}, u32[]{:S(2)}) collective-permute-start(bf16[1,1,2,2,2,1,2,2,8,256]{9,8,7,6,4,3,2,1,0,5:T(8,128)(2,1)S(1)} %bitcast.24), channel_id=1, source_target_pairs={{0,16},{1,17},{2,18},{3,19},{4,20},{5,21},{6,22},{7,23},{8,24},{9,... | collective-permute-start | bytes 393224 | tf_op jit(solution)/shard_map/ppermute | solution.py:329
  15.9 45.3 %collective-permute-start.2 = (bf16[1,1,2,2,2,1,2,2,8,256]{9,8,7,6,4,3,2,1,0,5:T(8,128)(2,1)S(1)}, bf16[1,1,2,2,2,1,2,2,8,256]{9,8,7,6,4,3,2,1,0,5:T(8,128)(2,1)}, u32[]{:S(2)}, u32[]{:S(2)}) collective-permute-start(bf16[1,1,2,2,2,1,2,2,8,256]{9,8,7,6,4,3,2,1,0,5:T(8,128)(2,1)S(1)} %bitcast.23), channel_id=1, source_target_pairs={{0,24},{1,25},{2,26},{3,27},{4,28},{5,29},{6,30},{7,31},{8,16},{9,... | collective-permute-start | bytes 393224 | tf_op jit(solution)/shard_map/ppermute | solution.py:329
  57.9 65.0 %all-to-all-start.1 = ((bf16[32,3,2,2,8,256]{5,4,3,2,1,0:T(8,128)(2,1)}), bf16[32,3,2,2,8,256]{5,4,3,2,1,0:T(8,128)(2,1)S(1)}, u32[]{:S(2)}, u32[]{:S(2)}) async-start(bf16[32,3,2,2,8,256]{5,4,3,2,1,0:T(8,128)(2,1)} %shard_map.113), calls=%async_computation.1 | async-start | bytes 3145728 | tf_op jit(solution)/shard_map/all_to_all | solution.py:317
  62.2 1.6 %collective-permute-start.3 = (bf16[2,2,2,1,2,1,2,2,8,256]{9,8,7,6,4,3,2,1,0,5:T(8,128)(2,1)S(1)}, bf16[2,2,2,1,2,1,2,2,8,256]{9,8,7,6,4,3,2,1,0,5:T(8,128)(2,1)S(1)}, u32[]{:S(2)}, u32[]{:S(2)}) collective-permute-start(bf16[2,2,2,1,2,1,2,2,8,256]{9,8,7,6,4,3,2,1,0,5:T(8,128)(2,1)S(1)} %get-tuple-element.35), channel_id=1, source_target_pairs={{0,2},{1,3},{2,0},{3,1},{4,6},{5,7},{6,4},{7,5},{8,10},{9,11},{10,... | collective-permute-start | bytes 786440 | tf_op jit(solution)/shard_map/ppermute | solution.py:329
  63.8 15.5 %collective-permute-start.4 = (bf16[2,2,1,2,1,1,2,2,8,256]{9,8,7,6,4,3,2,1,0,5:T(8,128)(2,1)S(1)}, bf16[2,2,1,2,1,1,2,2,8,256]{9,8,7,6,4,3,2,1,0,5:T(8,128)(2,1)S(1)}, u32[]{:S(2)}, u32[]{:S(2)}) collective-permute-start(bf16[2,2,1,2,1,1,2,2,8,256]{9,8,7,6,4,3,2,1,0,5:T(8,128)(2,1)S(1)} %get-tuple-element.31), channel_id=1, source_target_pairs={{0,1},{1,0},{2,3},{3,2},{4,5},{5,4},{6,7},{7,6},{8,9},{9,8},{10,11... | collective-permute-start | bytes 393224 | tf_op jit(solution)/shard_map/ppermute | solution.py:329
  65.7 15.9 %collective-permute-start.6 = (bf16[2,2,1,2,1,1,2,2,8,256]{9,8,7,6,4,3,2,1,0,5:T(8,128)(2,1)S(1)}, bf16[2,2,1,2,1,1,2,2,8,256]{9,8,7,6,4,3,2,1,0,5:T(8,128)(2,1)S(1)}, u32[]{:S(2)}, u32[]{:S(2)}) collective-permute-start(bf16[2,2,1,2,1,1,2,2,8,256]{9,8,7,6,4,3,2,1,0,5:T(8,128)(2,1)S(1)} %get-tuple-element.32), channel_id=1, source_target_pairs={{0,5},{1,4},{2,7},{3,6},{4,1},{5,0},{6,3},{7,2},{8,13},{9,12},{10,... | collective-permute-start | bytes 393224 | tf_op jit(solution)/shard_map/ppermute | solution.py:329
  67.1 14.8 %collective-permute-start.5 = (bf16[2,2,1,2,1,1,2,2,8,256]{9,8,7,6,4,3,2,1,0,5:T(8,128)(2,1)S(1)}, bf16[2,2,1,2,1,1,2,2,8,256]{9,8,7,6,4,3,2,1,0,5:T(8,128)(2,1)S(1)}, u32[]{:S(2)}, u32[]{:S(2)}) collective-permute-start(bf16[2,2,1,2,1,1,2,2,8,256]{9,8,7,6,4,3,2,1,0,5:T(8,128)(2,1)S(1)} %get-tuple-element.33), channel_id=1, source_target_pairs={{0,4},{1,5},{2,6},{3,7},{4,0},{5,1},{6,2},{7,3},{8,12},{9,13},{10,... | collective-permute-start | bytes 393224 | tf_op jit(solution)/shard_map/ppermute | solution.py:329
  83.2 10.7 %collective-permute-start.7 = (bf16[2,2,1,2,2,1,2,2,8,256]{9,8,7,6,4,3,2,1,0,5:T(8,128)(2,1)S(1)}, bf16[2,2,1,2,2,1,2,2,8,256]{9,8,7,6,4,3,2,1,0,5:T(8,128)(2,1)S(1)}, u32[]{:S(2)}, u32[]{:S(2)}) collective-permute-start(bf16[2,2,1,2,2,1,2,2,8,256]{9,8,7,6,4,3,2,1,0,5:T(8,128)(2,1)S(1)} %get-tuple-element.29), channel_id=1, source_target_pairs={{0,4},{1,5},{2,6},{3,7},{4,0},{5,1},{6,2},{7,3},{8,12},{9,13},{10,... | collective-permute-start | bytes 786440 | tf_op jit(solution)/shard_map/ppermute | solution.py:329
  93.9 19.3 %copy-start.2 = (bf16[4,2,1,2,256,256]{5,4,3,2,1,0:T(8,128)(2,1)S(1)}, bf16[4,2,1,2,256,256]{5,4,3,2,1,0:T(8,128)(2,1)}, u32[]{:S(2)}) copy-start(bf16[4,2,1,2,256,256]{5,4,3,2,1,0:T(8,128)(2,1)} %param.10) | copy-start | bytes 6291460
  94.0 7.7 %collective-permute-start.8 = (bf16[1,1,2,2,2,1,2,2,8,256]{9,8,7,6,4,3,2,1,0,5:T(8,128)(2,1)S(1)}, bf16[1,1,2,2,2,1,2,2,8,256]{9,8,7,6,4,3,2,1,0,5:T(8,128)(2,1)S(1)}, u32[]{:S(2)}, u32[]{:S(2)}) collective-permute-start(bf16[1,1,2,2,2,1,2,2,8,256]{9,8,7,6,4,3,2,1,0,5:T(8,128)(2,1)S(1)} %get-tuple-element.25), channel_id=1, source_target_pairs={{0,8},{1,9},{2,10},{3,11},{4,12},{5,13},{6,14},{7,15},{8,0},{9,1},... | collective-permute-start | bytes 393224 | tf_op jit(solution)/shard_map/ppermute | solution.py:329
  96.8 9.8 %collective-permute-start.10 = (bf16[1,1,2,2,2,1,2,2,8,256]{9,8,7,6,4,3,2,1,0,5:T(8,128)(2,1)S(1)}, bf16[1,1,2,2,2,1,2,2,8,256]{9,8,7,6,4,3,2,1,0,5:T(8,128)(2,1)S(1)}, u32[]{:S(2)}, u32[]{:S(2)}) collective-permute-start(bf16[1,1,2,2,2,1,2,2,8,256]{9,8,7,6,4,3,2,1,0,5:T(8,128)(2,1)S(1)} %get-tuple-element.26), channel_id=1, source_target_pairs={{0,24},{1,25},{2,26},{3,27},{4,28},{5,29},{6,30},{7,31},{8,16},{9,... | collective-permute-start | bytes 393224 | tf_op jit(solution)/shard_map/ppermute | solution.py:329
  99.4 11.8 %collective-permute-start.9 = (bf16[1,1,2,2,2,1,2,2,8,256]{9,8,7,6,4,3,2,1,0,5:T(8,128)(2,1)S(1)}, bf16[1,1,2,2,2,1,2,2,8,256]{9,8,7,6,4,3,2,1,0,5:T(8,128)(2,1)S(1)}, u32[]{:S(2)}, u32[]{:S(2)}) collective-permute-start(bf16[1,1,2,2,2,1,2,2,8,256]{9,8,7,6,4,3,2,1,0,5:T(8,128)(2,1)S(1)} %get-tuple-element.27), channel_id=1, source_target_pairs={{0,16},{1,17},{2,18},{3,19},{4,20},{5,21},{6,22},{7,23},{8,24},{9,... | collective-permute-start | bytes 393224 | tf_op jit(solution)/shard_map/ppermute | solution.py:329
  111.3 1.6 %collective-permute-start.11 = (bf16[2,2,2,1,2,1,2,2,8,256]{9,8,7,6,4,3,2,1,0,5:T(8,128)(2,1)S(1)}, bf16[2,2,2,1,2,1,2,2,8,256]{9,8,7,6,4,3,2,1,0,5:T(8,128)(2,1)S(1)}, u32[]{:S(2)}, u32[]{:S(2)}) collective-permute-start(bf16[2,2,2,1,2,1,2,2,8,256]{9,8,7,6,4,3,2,1,0,5:T(8,128)(2,1)S(1)} %get-tuple-element.23), channel_id=1, source_target_pairs={{0,2},{1,3},{2,0},{3,1},{4,6},{5,7},{6,4},{7,5},{8,10},{9,11},{10,... | collective-permute-start | bytes 786440 | tf_op jit(solution)/shard_map/ppermute | solution.py:329
  112.9 8.4 %collective-permute-start.12 = (bf16[2,2,2,2,1,1,2,2,8,256]{9,8,7,6,4,3,2,1,0,5:T(8,128)(2,1)S(1)}, bf16[2,2,2,2,1,1,2,2,8,256]{9,8,7,6,4,3,2,1,0,5:T(8,128)(2,1)S(1)}, u32[]{:S(2)}, u32[]{:S(2)}) collective-permute-start(bf16[2,2,2,2,1,1,2,2,8,256]{9,8,7,6,4,3,2,1,0,5:T(8,128)(2,1)S(1)} %get-tuple-element.21), channel_id=1, source_target_pairs={{0,1},{1,0},{2,3},{3,2},{4,5},{5,4},{6,7},{7,6},{8,9},{9,8},{10,11... | collective-permute-start | bytes 786440 | tf_op jit(solution)/shard_map/ppermute | solution.py:329

commit v4 on v3

--- a/solution.py
+++ b/solution.py
@@ -95,7 +95,7 @@
         for one in range(k_one):
             held[slot(one, c), e, :, k] = value[one]
 
-    for e in range(energies):
+    def forward(e):
         state = []
         for c, k in spots:
             block = load(c, e, k)
@@ -103,9 +103,15 @@
             out = jnp.dot(fwd_ref[...], block, preferred_element_type=jnp.float32)
             out = out.reshape(k_one, 2, rows, width)
             state.append((out[:, 0], out[:, 1]))
-        state = turns(state, 1)
+        return state
+
+    ahead = [forward(0)]
+    for e in range(energies):
+        state = turns(ahead[e], 1)
         state = [(w_ref[:, r] * re, w_ref[:, r] * im) for r, (re, im) in enumerate(state)]
         state = turns(state, -1)
+        if e + 1 < energies:
+            ahead.append(forward(e + 1))
         for (c, k), (re, im) in zip(spots, state):
             block = jnp.stack((re, im), 1).reshape(size, width)
             high = block.astype(jnp.bfloat16)

time: 126 us -> 126 us (level)
  no operation moved by 1% of the time
where the time goes in v4:
time: 126 us
  waiting for transfers between devices  81.3 us (65%)
  starting transfers between devices  27.7 us (22%)
  Pallas kernels  13 us (10%)
  local copies, waits for them, and re-layouts  1.6 us (1%)
    ppermute x13, waiting for transfers between devices, level(): return lax.ppermute(part, AXES, pairs)  44.7 us
    all_to_all x2, waiting for transfers between devices, exchange(): return lax.all_to_all(blocks, AXES, split_axis=0, concat_axis=0, tiled=True)  36.6 us
    ppermute x13, starting transfers between devices, level(): return lax.ppermute(part, AXES, pairs)  17.2 us
    all_to_all x2, starting transfers between devices, exchange(): return lax.all_to_all(blocks, AXES, split_axis=0, concat_axis=0, tiled=True)  10.5 us
    pallas_call x2, Pallas kernels, dyson(): pl.pallas_call(functools.partial(dyson_kernel, first, kcols, relative), i...  4.71 us
    pallas_call x2, Pallas kernels, fourier(): pl.pallas_call(functools.partial(fourier_kernel, kcols, relative), in_spe...  4.65 us
  transfers between devices with their start and end apart: 15, of which 11 were waited for; matrix products, arithmetic and copies ran while one was open for 2% of the time, Pallas kernels for 6%

profile of v4, /device:TPU:0, one launch (start us, length us, event | category | flops | bytes accessed | tf_op | source)
XLA Modules:
  0.0 125.6 jit_solution(13724590586892738325)
XLA Ops:
  0.6 2.4 %by_device.1 = bf16[32,3,2,2,8,256]{5,4,3,2,1,0:T(8,128)(2,1)} custom-call(bf16[4,2,2,32,8,256]{5,4,3,2,1,0:T(8,128)(2,1)} %bitcast.26), custom_call_target="tpu_custom_call" | custom-call | tf_op jit(solution)/shard_map/by_device/pallas_call | solution.py:197
  3.0 7.3 %all-to-all-start = ((bf16[32,3,2,2,8,256]{5,4,3,2,1,0:T(8,128)(2,1)}), bf16[32,3,2,2,8,256]{5,4,3,2,1,0:T(8,128)(2,1)S(1)}, u32[]{:S(2)}, u32[]{:S(2)}) async-start(bf16[32,3,2,2,8,256]{5,4,3,2,1,0:T(8,128)(2,1)} %by_device.1), calls=%async_computation | async-start | bytes 3145728 | tf_op jit(solution)/shard_map/all_to_all | solution.py:323
  10.4 0.0 copy-start
  10.4 0.0 copy-start.1
  10.4 1.2 by_offset.1
  11.6 1.8 %collective-permute-start = (bf16[1,1,2,2,2,1,2,2,8,256]{9,8,7,6,4,3,2,1,0,5:T(8,128)(2,1)S(1)}, bf16[1,1,2,2,2,1,2,2,8,256]{9,8,7,6,4,3,2,1,0,5:T(8,128)(2,1)S(1)}, u32[]{:S(2)}, u32[]{:S(2)}) collective-permute-start(bf16[1,1,2,2,2,1,2,2,8,256]{9,8,7,6,4,3,2,1,0,5:T(8,128)(2,1)S(1)} %bitcast.25), channel_id=1, source_target_pairs={{0,8},{1,9},{2,10},{3,11},{4,12},{5,13},{6,14},{7,15},{8,0},{9,1},... | collective-permute-start | bytes 393224 | tf_op jit(solution)/shard_map/ppermute | solution.py:335
  13.4 2.4 %collective-permute-start.1 = (bf16[1,1,2,2,2,1,2,2,8,256]{9,8,7,6,4,3,2,1,0,5:T(8,128)(2,1)S(1)}, bf16[1,1,2,2,2,1,2,2,8,256]{9,8,7,6,4,3,2,1,0,5:T(8,128)(2,1)S(1)}, u32[]{:S(2)}, u32[]{:S(2)}) collective-permute-start(bf16[1,1,2,2,2,1,2,2,8,256]{9,8,7,6,4,3,2,1,0,5:T(8,128)(2,1)S(1)} %bitcast.24), channel_id=1, source_target_pairs={{0,16},{1,17},{2,18},{3,19},{4,20},{5,21},{6,22},{7,23},{8,24},{9,... | collective-permute-start | bytes 393224 | tf_op jit(solution)/shard_map/ppermute | solution.py:335
  15.9 0.2 collective-permute-start.2
  16.1 1.3 %reshape.35.w_ref = f32[16,4,8,256]{3,2,1,0:T(8,128)S(1)} reshape(f32[16,4,2048]{2,1,0:T(4,128)} %param.11) | data formatting | bytes 1048576 | tf_op jit(solution)/shard_map/reshape | solution.py:363
  17.4 36.6 %all-to-all-done.x_ref = bf16[32,3,2,2,8,256]{5,4,3,2,1,0:T(8,128)(2,1)S(1)} async-done(((bf16[32,3,2,2,8,256]{5,4,3,2,1,0:T(8,128)(2,1)}), bf16[32,3,2,2,8,256]{5,4,3,2,1,0:T(8,128)(2,1)S(1)}, u32[]{:S(2)}, u32[]{:S(2)}) %all-to-all-start) | async-done | bytes 1572896 | tf_op jit(solution)/shard_map/all_to_all | solution.py:323
  54.0 0.0 copy-done
  54.0 0.0 copy-done.1
  54.0 3.5 %shard_map.113 = bf16[32,3,2,2,8,256]{5,4,3,2,1,0:T(8,128)(2,1)} custom-call(bf16[32,3,2,2,8,256]{5,4,3,2,1,0:T(8,128)(2,1)S(1)} %all-to-all-done.x_ref, f32[16,4,8,256]{3,2,1,0:T(8,128)S(1)} %reshape.35.w_ref, bf16[256,512]{1,0:T(8,128)(2,1)S(1)} %copy-done.1, bf16[256,768]{1,0:T(8,128)(2,1)S(1)} %copy-done), custom_call_target="tpu_custom_call" | custom-call | flops 2013265920 | bytes 3670016 | tf_op jit(solution)/shard_map/pallas_call | solution.py:150
  57.5 3.2 %all-to-all-start.1 = ((bf16[32,3,2,2,8,256]{5,4,3,2,1,0:T(8,128)(2,1)}), bf16[32,3,2,2,8,256]{5,4,3,2,1,0:T(8,128)(2,1)S(1)}, u32[]{:S(2)}, u32[]{:S(2)}) async-start(bf16[32,3,2,2,8,256]{5,4,3,2,1,0:T(8,128)(2,1)} %shard_map.113), calls=%async_computation.1 | async-start | bytes 3145728 | tf_op jit(solution)/shard_map/all_to_all | solution.py:323
  60.7 0.0 collective-permute-done
  60.7 0.0 collective-permute-done.1
  60.7 0.0 collective-permute-done.2
  60.7 1.0 maximum_maximum_fusion
  61.7 0.3 collective-permute-start.3
  62.0 1.3 %collective-permute-done.3 = bf16[2,2,2,1,2,1,2,2,8,256]{9,8,7,6,4,3,2,1,0,5:T(8,128)(2,1)S(1)} collective-permute-done((bf16[2,2,2,1,2,1,2,2,8,256]{9,8,7,6,4,3,2,1,0,5:T(8,128)(2,1)S(1)}, bf16[2,2,2,1,2,1,2,2,8,256]{9,8,7,6,4,3,2,1,0,5:T(8,128)(2,1)S(1)}, u32[]{:S(2)}, u32[]{:S(2)}) %collective-permute-start.3) | collective-permute-done | bytes 262176 | tf_op jit(solution)/shard_map/ppermute | solution.py:335
  63.4 1.8 %collective-permute-start.4 = (bf16[2,2,1,2,1,1,2,2,8,256]{9,8,7,6,4,3,2,1,0,5:T(8,128)(2,1)S(1)}, bf16[2,2,1,2,1,1,2,2,8,256]{9,8,7,6,4,3,2,1,0,5:T(8,128)(2,1)S(1)}, u32[]{:S(2)}, u32[]{:S(2)}) collective-permute-start(bf16[2,2,1,2,1,1,2,2,8,256]{9,8,7,6,4,3,2,1,0,5:T(8,128)(2,1)S(1)} %get-tuple-element.31), channel_id=1, source_target_pairs={{0,1},{1,0},{2,3},{3,2},{4,5},{5,4},{6,7},{7,6},{8,9},{9,8},{10,11... | collective-permute-start | bytes 393224 | tf_op jit(solution)/shard_map/ppermute | solution.py:335
  65.2 1.5 %collective-permute-start.6 = (bf16[2,2,1,2,1,1,2,2,8,256]{9,8,7,6,4,3,2,1,0,5:T(8,128)(2,1)S(1)}, bf16[2,2,1,2,1,1,2,2,8,256]{9,8,7,6,4,3,2,1,0,5:T(8,128)(2,1)S(1)}, u32[]{:S(2)}, u32[]{:S(2)}) collective-permute-start(bf16[2,2,1,2,1,1,2,2,8,256]{9,8,7,6,4,3,2,1,0,5:T(8,128)(2,1)S(1)} %get-tuple-element.32), channel_id=1, source_target_pairs={{0,5},{1,4},{2,7},{3,6},{4,1},{5,0},{6,3},{7,2},{8,13},{9,12},{10,... | collective-permute-start | bytes 393224 | tf_op jit(solution)/shard_map/ppermute | solution.py:335
  66.7 0.3 collective-permute-start.5
  66.9 12.0 %collective-permute-done.4 = bf16[2,2,1,2,1,1,2,2,8,256]{9,8,7,6,4,3,2,1,0,5:T(8,128)(2,1)S(1)} collective-permute-done((bf16[2,2,1,2,1,1,2,2,8,256]{9,8,7,6,4,3,2,1,0,5:T(8,128)(2,1)S(1)}, bf16[2,2,1,2,1,1,2,2,8,256]{9,8,7,6,4,3,2,1,0,5:T(8,128)(2,1)S(1)}, u32[]{:S(2)}, u32[]{:S(2)}) %collective-permute-start.4) | collective-permute-done | bytes 131104 | tf_op jit(solution)/shard_map/ppermute | solution.py:335
  78.9 2.2 %collective-permute-done.6 = bf16[2,2,1,2,1,1,2,2,8,256]{9,8,7,6,4,3,2,1,0,5:T(8,128)(2,1)S(1)} collective-permute-done((bf16[2,2,1,2,1,1,2,2,8,256]{9,8,7,6,4,3,2,1,0,5:T(8,128)(2,1)S(1)}, bf16[2,2,1,2,1,1,2,2,8,256]{9,8,7,6,4,3,2,1,0,5:T(8,128)(2,1)S(1)}, u32[]{:S(2)}, u32[]{:S(2)}) %collective-permute-start.6) | collective-permute-done | bytes 131104 | tf_op jit(solution)/shard_map/ppermute | solution.py:335
  81.1 0.4 collective-permute-done.5
  81.5 0.1 maximum_maximum_fusion.1
  81.5 1.2 shard_map.114
  82.8 2.6 %collective-permute-start.7 = (bf16[2,2,1,2,2,1,2,2,8,256]{9,8,7,6,4,3,2,1,0,5:T(8,128)(2,1)S(1)}, bf16[2,2,1,2,2,1,2,2,8,256]{9,8,7,6,4,3,2,1,0,5:T(8,128)(2,1)S(1)}, u32[]{:S(2)}, u32[]{:S(2)}) collective-permute-start(bf16[2,2,1,2,2,1,2,2,8,256]{9,8,7,6,4,3,2,1,0,5:T(8,128)(2,1)S(1)} %get-tuple-element.29), channel_id=1, source_target_pairs={{0,4},{1,5},{2,6},{3,7},{4,0},{5,1},{6,2},{7,3},{8,12},{9,13},{10,... | collective-permute-start | bytes 786440 | tf_op jit(solution)/shard_map/ppermute | solution.py:335
  85.3 8.1 %collective-permute-done.7 = bf16[2,2,1,2,2,1,2,2,8,256]{9,8,7,6,4,3,2,1,0,5:T(8,128)(2,1)S(1)} collective-permute-done((bf16[2,2,1,2,2,1,2,2,8,256]{9,8,7,6,4,3,2,1,0,5:T(8,128)(2,1)S(1)}, bf16[2,2,1,2,2,1,2,2,8,256]{9,8,7,6,4,3,2,1,0,5:T(8,128)(2,1)S(1)}, u32[]{:S(2)}, u32[]{:S(2)}) %collective-permute-start.7) | collective-permute-done | bytes 262176 | tf_op jit(solution)/shard_map/ppermute | solution.py:335
  93.4 0.0 copy-start.2
  93.5 2.8 %collective-permute-start.8 = (bf16[1,1,2,2,2,1,2,2,8,256]{9,8,7,6,4,3,2,1,0,5:T(8,128)(2,1)S(1)}, bf16[1,1,2,2,2,1,2,2,8,256]{9,8,7,6,4,3,2,1,0,5:T(8,128)(2,1)S(1)}, u32[]{:S(2)}, u32[]{:S(2)}) collective-permute-start(bf16[1,1,2,2,2,1,2,2,8,256]{9,8,7,6,4,3,2,1,0,5:T(8,128)(2,1)S(1)} %get-tuple-element.25), channel_id=1, source_target_pairs={{0,8},{1,9},{2,10},{3,11},{4,12},{5,13},{6,14},{7,15},{8,0},{9,1},... | collective-permute-start | bytes 393224 | tf_op jit(solution)/shard_map/ppermute | solution.py:335
  96.3 2.6 %collective-permute-start.10 = (bf16[1,1,2,2,2,1,2,2,8,256]{9,8,7,6,4,3,2,1,0,5:T(8,128)(2,1)S(1)}, bf16[1,1,2,2,2,1,2,2,8,256]{9,8,7,6,4,3,2,1,0,5:T(8,128)(2,1)S(1)}, u32[]{:S(2)}, u32[]{:S(2)}) collective-permute-start(bf16[1,1,2,2,2,1,2,2,8,256]{9,8,7,6,4,3,2,1,0,5:T(8,128)(2,1)S(1)} %get-tuple-element.26), channel_id=1, source_target_pairs={{0,24},{1,25},{2,26},{3,27},{4,28},{5,29},{6,30},{7,31},{8,16},{9,... | collective-permute-start | bytes 393224 | tf_op jit(solution)/shard_map/ppermute | solution.py:335
  98.9 0.5 collective-permute-start.9
  99.4 1.8 %collective-permute-done.8 = bf16[1,1,2,2,2,1,2,2,8,256]{9,8,7,6,4,3,2,1,0,5:T(8,128)(2,1)S(1)} collective-permute-done((bf16[1,1,2,2,2,1,2,2,8,256]{9,8,7,6,4,3,2,1,0,5:T(8,128)(2,1)S(1)}, bf16[1,1,2,2,2,1,2,2,8,256]{9,8,7,6,4,3,2,1,0,5:T(8,128)(2,1)S(1)}, u32[]{:S(2)}, u32[]{:S(2)}) %collective-permute-start.8) | collective-permute-done | bytes 131104 | tf_op jit(solution)/shard_map/ppermute | solution.py:335
  101.2 4.8 %collective-permute-done.10 = bf16[1,1,2,2,2,1,2,2,8,256]{9,8,7,6,4,3,2,1,0,5:T(8,128)(2,1)S(1)} collective-permute-done((bf16[1,1,2,2,2,1,2,2,8,256]{9,8,7,6,4,3,2,1,0,5:T(8,128)(2,1)S(1)}, bf16[1,1,2,2,2,1,2,2,8,256]{9,8,7,6,4,3,2,1,0,5:T(8,128)(2,1)S(1)}, u32[]{:S(2)}, u32[]{:S(2)}) %collective-permute-start.10) | collective-permute-done | bytes 131104 | tf_op jit(solution)/shard_map/ppermute | solution.py:335
  106.1 4.6 %collective-permute-done.9 = bf16[1,1,2,2,2,1,2,2,8,256]{9,8,7,6,4,3,2,1,0,5:T(8,128)(2,1)S(1)} collective-permute-done((bf16[1,1,2,2,2,1,2,2,8,256]{9,8,7,6,4,3,2,1,0,5:T(8,128)(2,1)S(1)}, bf16[1,1,2,2,2,1,2,2,8,256]{9,8,7,6,4,3,2,1,0,5:T(8,128)(2,1)S(1)}, u32[]{:S(2)}, u32[]{:S(2)}) %collective-permute-start.9) | collective-permute-done | bytes 131104 | tf_op jit(solution)/shard_map/ppermute | solution.py:335
  110.8 0.1 collective-permute-start.11
  110.9 1.5 %collective-permute-done.11 = bf16[2,2,2,1,2,1,2,2,8,256]{9,8,7,6,4,3,2,1,0,5:T(8,128)(2,1)S(1)} collective-permute-done((bf16[2,2,2,1,2,1,2,2,8,256]{9,8,7,6,4,3,2,1,0,5:T(8,128)(2,1)S(1)}, bf16[2,2,2,1,2,1,2,2,8,256]{9,8,7,6,4,3,2,1,0,5:T(8,128)(2,1)S(1)}, u32[]{:S(2)}, u32[]{:S(2)}) %collective-permute-start.11) | collective-permute-done | bytes 262176 | tf_op jit(solution)/shard_map/ppermute | solution.py:335
  112.4 0.3 collective-permute-start.12
  112.7 0.0 copy-done.2
  112.8 0.1 slice.66.g_ref
  112.9 7.9 %collective-permute-done.12 = bf16[2,2,2,2,1,1,2,2,8,256]{9,8,7,6,4,3,2,1,0,5:T(8,128)(2,1)S(1)} collective-permute-done((bf16[2,2,2,2,1,1,2,2,8,256]{9,8,7,6,4,3,2,1,0,5:T(8,128)(2,1)S(1)}, bf16[2,2,2,2,1,1,2,2,8,256]{9,8,7,6,4,3,2,1,0,5:T(8,128)(2,1)S(1)}, u32[]{:S(2)}, u32[]{:S(2)}) %collective-permute-start.12) | collective-permute-done | bytes 262176 | tf_op jit(solution)/shard_map/ppermute | solution.py:335
  120.8 0.1 pad_maximum_fusion
  120.9 1.6 %shard_map.115 = (bf16[4,2,2,32,8,256]{5,4,3,2,1,0:T(8,128)(2,1)}, bf16[4,2,1,2,256,256]{5,4,3,2,1,0:T(8,128)(2,1)}) custom-call(bf16[32,1,2,2,8,256]{5,4,3,2,1,0:T(8,128)(2,1)S(1)} %bitcast.21, bf16[1,2,1,2,256,256]{5,4,3,2,1,0:T(8,128)(2,1)S(1)} %slice.83.g_ref), custom_call_target="tpu_custom_call" | custom-call | flops 536870912 | bytes 4194304 | tf_op jit(solution)/shard_map/pallas_call | solution.py:298
  122.5 0.0 all-to-all-done.1.s_ref
  122.5 3.1 %shard_map.116 = (bf16[4,2,2,32,8,256]{5,4,3,2,1,0:T(8,128)(2,1)}, bf16[4,2,1,2,256,256]{5,4,3,2,1,0:T(8,128)(2,1)}) custom-call(bf16[32,3,2,2,8,256]{5,4,3,2,1,0:T(8,128)(2,1)S(1)} %all-to-all-done.1.s_ref, bf16[3,2,1,2,256,256]{5,4,3,2,1,0:T(8,128)(2,1)S(1)} %slice.66.g_ref, ...), custom_call_target="tpu_custom_call", output_to_operand_aliasing={{0}: (2, {}), {1}: (3, {})} | custom-call | flops 1610612736 | bytes 12582912 | tf_op jit(solution)/shard_map/pallas_call | solution.py:298
  (8 shorter events, 0.3 us)
Async XLA Ops:
  3.0 51.0 %all-to-all-start = ((bf16[32,3,2,2,8,256]{5,4,3,2,1,0:T(8,128)(2,1)}), bf16[32,3,2,2,8,256]{5,4,3,2,1,0:T(8,128)(2,1)S(1)}, u32[]{:S(2)}, u32[]{:S(2)}) async-start(bf16[32,3,2,2,8,256]{5,4,3,2,1,0:T(8,128)(2,1)} %by_device.1), calls=%async_computation | async-start | bytes 3145728 | tf_op jit(solution)/shard_map/all_to_all | solution.py:323
  10.4 43.6 %copy-start = (bf16[256,768]{1,0:T(8,128)(2,1)S(1)}, bf16[256,768]{1,0:T(8,128)(2,1)}, u32[]{:S(2)}) copy-start(bf16[256,768]{1,0:T(8,128)(2,1)} %constant.16.inv_ref) | copy-start | bytes 1179652
  10.4 43.6 %copy-start.1 = (bf16[256,512]{1,0:T(8,128)(2,1)S(1)}, bf16[256,512]{1,0:T(8,128)(2,1)}, u32[]{:S(2)}) copy-start(bf16[256,512]{1,0:T(8,128)(2,1)} %constant.11.fwd_ref) | copy-start | bytes 786436
  11.6 49.1 %collective-permute-start = (bf16[1,1,2,2,2,1,2,2,8,256]{9,8,7,6,4,3,2,1,0,5:T(8,128)(2,1)S(1)}, bf16[1,1,2,2,2,1,2,2,8,256]{9,8,7,6,4,3,2,1,0,5:T(8,128)(2,1)S(1)}, u32[]{:S(2)}, u32[]{:S(2)}) collective-permute-start(bf16[1,1,2,2,2,1,2,2,8,256]{9,8,7,6,4,3,2,1,0,5:T(8,128)(2,1)S(1)} %bitcast.25), channel_id=1, source_target_pairs={{0,8},{1,9},{2,10},{3,11},{4,12},{5,13},{6,14},{7,15},{8,0},{9,1},... | collective-permute-start | bytes 393224 | tf_op jit(solution)/shard_map/ppermute | solution.py:335
  13.4 47.2 %collective-permute-start.1 = (bf16[1,1,2,2,2,1,2,2,8,256]{9,8,7,6,4,3,2,1,0,5:T(8,128)(2,1)S(1)}, bf16[1,1,2,2,2,1,2,2,8,256]{9,8,7,6,4,3,2,1,0,5:T(8,128)(2,1)S(1)}, u32[]{:S(2)}, u32[]{:S(2)}) collective-permute-start(bf16[1,1,2,2,2,1,2,2,8,256]{9,8,7,6,4,3,2,1,0,5:T(8,128)(2,1)S(1)} %bitcast.24), channel_id=1, source_target_pairs={{0,16},{1,17},{2,18},{3,19},{4,20},{5,21},{6,22},{7,23},{8,24},{9,... | collective-permute-start | bytes 393224 | tf_op jit(solution)/shard_map/ppermute | solution.py:335
  15.9 44.8 %collective-permute-start.2 = (bf16[1,1,2,2,2,1,2,2,8,256]{9,8,7,6,4,3,2,1,0,5:T(8,128)(2,1)S(1)}, bf16[1,1,2,2,2,1,2,2,8,256]{9,8,7,6,4,3,2,1,0,5:T(8,128)(2,1)}, u32[]{:S(2)}, u32[]{:S(2)}) collective-permute-start(bf16[1,1,2,2,2,1,2,2,8,256]{9,8,7,6,4,3,2,1,0,5:T(8,128)(2,1)S(1)} %bitcast.23), channel_id=1, source_target_pairs={{0,24},{1,25},{2,26},{3,27},{4,28},{5,29},{6,30},{7,31},{8,16},{9,... | collective-permute-start | bytes 393224 | tf_op jit(solution)/shard_map/ppermute | solution.py:335
  57.5 65.0 %all-to-all-start.1 = ((bf16[32,3,2,2,8,256]{5,4,3,2,1,0:T(8,128)(2,1)}), bf16[32,3,2,2,8,256]{5,4,3,2,1,0:T(8,128)(2,1)S(1)}, u32[]{:S(2)}, u32[]{:S(2)}) async-start(bf16[32,3,2,2,8,256]{5,4,3,2,1,0:T(8,128)(2,1)} %shard_map.113), calls=%async_computation.1 | async-start | bytes 3145728 | tf_op jit(solution)/shard_map/all_to_all | solution.py:323
  61.7 1.6 %collective-permute-start.3 = (bf16[2,2,2,1,2,1,2,2,8,256]{9,8,7,6,4,3,2,1,0,5:T(8,128)(2,1)S(1)}, bf16[2,2,2,1,2,1,2,2,8,256]{9,8,7,6,4,3,2,1,0,5:T(8,128)(2,1)S(1)}, u32[]{:S(2)}, u32[]{:S(2)}) collective-permute-start(bf16[2,2,2,1,2,1,2,2,8,256]{9,8,7,6,4,3,2,1,0,5:T(8,128)(2,1)S(1)} %get-tuple-element.35), channel_id=1, source_target_pairs={{0,2},{1,3},{2,0},{3,1},{4,6},{5,7},{6,4},{7,5},{8,10},{9,11},{10,... | collective-permute-start | bytes 786440 | tf_op jit(solution)/shard_map/ppermute | solution.py:335
  63.4 15.5 %collective-permute-start.4 = (bf16[2,2,1,2,1,1,2,2,8,256]{9,8,7,6,4,3,2,1,0,5:T(8,128)(2,1)S(1)}, bf16[2,2,1,2,1,1,2,2,8,256]{9,8,7,6,4,3,2,1,0,5:T(8,128)(2,1)S(1)}, u32[]{:S(2)}, u32[]{:S(2)}) collective-permute-start(bf16[2,2,1,2,1,1,2,2,8,256]{9,8,7,6,4,3,2,1,0,5:T(8,128)(2,1)S(1)} %get-tuple-element.31), channel_id=1, source_target_pairs={{0,1},{1,0},{2,3},{3,2},{4,5},{5,4},{6,7},{7,6},{8,9},{9,8},{10,11... | collective-permute-start | bytes 393224 | tf_op jit(solution)/shard_map/ppermute | solution.py:335
  65.2 15.9 %collective-permute-start.6 = (bf16[2,2,1,2,1,1,2,2,8,256]{9,8,7,6,4,3,2,1,0,5:T(8,128)(2,1)S(1)}, bf16[2,2,1,2,1,1,2,2,8,256]{9,8,7,6,4,3,2,1,0,5:T(8,128)(2,1)S(1)}, u32[]{:S(2)}, u32[]{:S(2)}) collective-permute-start(bf16[2,2,1,2,1,1,2,2,8,256]{9,8,7,6,4,3,2,1,0,5:T(8,128)(2,1)S(1)} %get-tuple-element.32), channel_id=1, source_target_pairs={{0,5},{1,4},{2,7},{3,6},{4,1},{5,0},{6,3},{7,2},{8,13},{9,12},{10,... | collective-permute-start | bytes 393224 | tf_op jit(solution)/shard_map/ppermute | solution.py:335
  66.7 14.8 %collective-permute-start.5 = (bf16[2,2,1,2,1,1,2,2,8,256]{9,8,7,6,4,3,2,1,0,5:T(8,128)(2,1)S(1)}, bf16[2,2,1,2,1,1,2,2,8,256]{9,8,7,6,4,3,2,1,0,5:T(8,128)(2,1)S(1)}, u32[]{:S(2)}, u32[]{:S(2)}) collective-permute-start(bf16[2,2,1,2,1,1,2,2,8,256]{9,8,7,6,4,3,2,1,0,5:T(8,128)(2,1)S(1)} %get-tuple-element.33), channel_id=1, source_target_pairs={{0,4},{1,5},{2,6},{3,7},{4,0},{5,1},{6,2},{7,3},{8,12},{9,13},{10,... | collective-permute-start | bytes 393224 | tf_op jit(solution)/shard_map/ppermute | solution.py:335
  82.8 10.7 %collective-permute-start.7 = (bf16[2,2,1,2,2,1,2,2,8,256]{9,8,7,6,4,3,2,1,0,5:T(8,128)(2,1)S(1)}, bf16[2,2,1,2,2,1,2,2,8,256]{9,8,7,6,4,3,2,1,0,5:T(8,128)(2,1)S(1)}, u32[]{:S(2)}, u32[]{:S(2)}) collective-permute-start(bf16[2,2,1,2,2,1,2,2,8,256]{9,8,7,6,4,3,2,1,0,5:T(8,128)(2,1)S(1)} %get-tuple-element.29), channel_id=1, source_target_pairs={{0,4},{1,5},{2,6},{3,7},{4,0},{5,1},{6,2},{7,3},{8,12},{9,13},{10,... | collective-permute-start | bytes 786440 | tf_op jit(solution)/shard_map/ppermute | solution.py:335
  93.4 19.3 %copy-start.2 = (bf16[4,2,1,2,256,256]{5,4,3,2,1,0:T(8,128)(2,1)S(1)}, bf16[4,2,1,2,256,256]{5,4,3,2,1,0:T(8,128)(2,1)}, u32[]{:S(2)}) copy-start(bf16[4,2,1,2,256,256]{5,4,3,2,1,0:T(8,128)(2,1)} %param.10) | copy-start | bytes 6291460
  93.5 7.7 %collective-permute-start.8 = (bf16[1,1,2,2,2,1,2,2,8,256]{9,8,7,6,4,3,2,1,0,5:T(8,128)(2,1)S(1)}, bf16[1,1,2,2,2,1,2,2,8,256]{9,8,7,6,4,3,2,1,0,5:T(8,128)(2,1)S(1)}, u32[]{:S(2)}, u32[]{:S(2)}) collective-permute-start(bf16[1,1,2,2,2,1,2,2,8,256]{9,8,7,6,4,3,2,1,0,5:T(8,128)(2,1)S(1)} %get-tuple-element.25), channel_id=1, source_target_pairs={{0,8},{1,9},{2,10},{3,11},{4,12},{5,13},{6,14},{7,15},{8,0},{9,1},... | collective-permute-start | bytes 393224 | tf_op jit(solution)/shard_map/ppermute | solution.py:335
  96.3 9.8 %collective-permute-start.10 = (bf16[1,1,2,2,2,1,2,2,8,256]{9,8,7,6,4,3,2,1,0,5:T(8,128)(2,1)S(1)}, bf16[1,1,2,2,2,1,2,2,8,256]{9,8,7,6,4,3,2,1,0,5:T(8,128)(2,1)S(1)}, u32[]{:S(2)}, u32[]{:S(2)}) collective-permute-start(bf16[1,1,2,2,2,1,2,2,8,256]{9,8,7,6,4,3,2,1,0,5:T(8,128)(2,1)S(1)} %get-tuple-element.26), channel_id=1, source_target_pairs={{0,24},{1,25},{2,26},{3,27},{4,28},{5,29},{6,30},{7,31},{8,16},{9,... | collective-permute-start | bytes 393224 | tf_op jit(solution)/shard_map/ppermute | solution.py:335
  98.9 11.8 %collective-permute-start.9 = (bf16[1,1,2,2,2,1,2,2,8,256]{9,8,7,6,4,3,2,1,0,5:T(8,128)(2,1)S(1)}, bf16[1,1,2,2,2,1,2,2,8,256]{9,8,7,6,4,3,2,1,0,5:T(8,128)(2,1)S(1)}, u32[]{:S(2)}, u32[]{:S(2)}) collective-permute-start(bf16[1,1,2,2,2,1,2,2,8,256]{9,8,7,6,4,3,2,1,0,5:T(8,128)(2,1)S(1)} %get-tuple-element.27), channel_id=1, source_target_pairs={{0,16},{1,17},{2,18},{3,19},{4,20},{5,21},{6,22},{7,23},{8,24},{9,... | collective-permute-start | bytes 393224 | tf_op jit(solution)/shard_map/ppermute | solution.py:335
  110.8 1.6 %collective-permute-start.11 = (bf16[2,2,2,1,2,1,2,2,8,256]{9,8,7,6,4,3,2,1,0,5:T(8,128)(2,1)S(1)}, bf16[2,2,2,1,2,1,2,2,8,256]{9,8,7,6,4,3,2,1,0,5:T(8,128)(2,1)S(1)}, u32[]{:S(2)}, u32[]{:S(2)}) collective-permute-start(bf16[2,2,2,1,2,1,2,2,8,256]{9,8,7,6,4,3,2,1,0,5:T(8,128)(2,1)S(1)} %get-tuple-element.23), channel_id=1, source_target_pairs={{0,2},{1,3},{2,0},{3,1},{4,6},{5,7},{6,4},{7,5},{8,10},{9,11},{10,... | collective-permute-start | bytes 786440 | tf_op jit(solution)/shard_map/ppermute | solution.py:335
  112.4 8.4 %collective-permute-start.12 = (bf16[2,2,2,2,1,1,2,2,8,256]{9,8,7,6,4,3,2,1,0,5:T(8,128)(2,1)S(1)}, bf16[2,2,2,2,1,1,2,2,8,256]{9,8,7,6,4,3,2,1,0,5:T(8,128)(2,1)S(1)}, u32[]{:S(2)}, u32[]{:S(2)}) collective-permute-start(bf16[2,2,2,2,1,1,2,2,8,256]{9,8,7,6,4,3,2,1,0,5:T(8,128)(2,1)S(1)} %get-tuple-element.21), channel_id=1, source_target_pairs={{0,1},{1,0},{2,3},{3,2},{4,5},{5,4},{6,7},{7,6},{8,9},{9,8},{10,11... | collective-permute-start | bytes 786440 | tf_op jit(solution)/shard_map/ppermute | solution.py:335

commit v5 on v4

--- a/solution.py
+++ b/solution.py
@@ -74,7 +74,17 @@
     return lax.axis_index("krow") * kcols + lax.axis_index("kcol")
 
 
-def fourier_kernel(kcols, relative, x_ref, w_ref, fwd_ref, inv_ref, o_ref, *scratch):
+def fourier_kernel(kcols, counts, w_ref, fwd_ref, inv_ref, *refs):
+    relative = bool(counts)
+    if relative:
+        o_ref, x_ref = refs[-2:]
+        scratch = ()
+        for j, digits in enumerate(np.ndindex(*counts)):
+            high, low, x, core, y = digits
+            piece = refs[x * counts[4] + y]
+            x_ref[j] = piece[(high * counts[1] + low) * counts[3] + core]
+    else:
+        x_ref, o_ref, *scratch = refs
     devices, energies, _, kcol_each, rows, width = x_ref.shape
     k_one = devices // kcols
     size = k_one * 2 * rows
@@ -142,26 +152,32 @@
     return pltpu.with_memory_space_constraint(value, pltpu.HBM)
 
 
-def fourier(pieces, weights, kcols, relative):
-    _, energies, parts, _, rows, width = pieces.shape
+def fourier(pieces, weights, kcols, counts):
+    if counts:
+        skip = len(counts)
+        pieces = [p.reshape((-1,) + p.shape[skip:]) for row in pieces for p in row]
+        shape = (math.prod(counts),) + pieces[0].shape[1:]
+        scratch = [pltpu.VMEM(shape, jnp.bfloat16)]
+    else:
+        pieces, shape = [pieces], pieces.shape
+        scratch = [pltpu.VMEM(shape, jnp.bfloat16), pltpu.SemaphoreType.DMA(shape[1:2])]
+    _, energies, parts, _, rows, width = shape
     k_one, k_two = weights.shape[:2]
     forward, inverse = row_tables(k_one, k_two, rows)
     size = k_one * parts * rows
     return pl.pallas_call(
-        functools.partial(fourier_kernel, kcols, relative),
-        in_specs=[LOCAL] * 4,
-        out_specs=pl.BlockSpec(memory_space=pltpu.VMEM if relative else pltpu.HBM),
-        out_shape=(pltpu.VMEM if relative else pltpu.HBM)(pieces.shape, jnp.bfloat16),
+        functools.partial(fourier_kernel, kcols, counts),
+        in_specs=[LOCAL] * (3 + len(pieces)),
+        out_specs=pl.BlockSpec(memory_space=pltpu.VMEM if counts else pltpu.HBM),
+        out_shape=(pltpu.VMEM if counts else pltpu.HBM)(shape, jnp.bfloat16),
         cost_estimate=pl.CostEstimate(
             flops=2 * 5 * size * size * width * k_two * energies,
-            bytes_accessed=4 * pieces.size + 4 * weights.size,
+            bytes_accessed=4 * math.prod(shape) + 4 * weights.size,
             transcendentals=0,
         ),
-        scratch_shapes=()
-        if relative
-        else [pltpu.VMEM(pieces.shape, jnp.bfloat16), pltpu.SemaphoreType.DMA((energies,))],
+        scratch_shapes=scratch,
         compiler_params=PARAMS,
-    )(near(pieces), near(weights), near(forward), near(inverse))
+    )(near(weights), near(forward), near(inverse), *map(near, pieces))
 
 
 def gather_kernel(g_ref, o_ref, held, sems, out_sems):
@@ -323,7 +339,7 @@
     return lax.all_to_all(blocks, AXES, split_axis=0, concat_axis=0, tiled=True)
 
 
-def swap(pieces, dims):
+def swap(pieces, dims, join=True):
     counts, devices = pieces.counts, math.prod(pieces.counts)
     strides = [math.prod(counts[d + 1 :]) for d in range(len(counts))]
 
@@ -338,6 +354,8 @@
         if not isinstance(part, (list, tuple)):
             cut = [lax.slice_in_dim(part, q, q + 1, axis=dim) for q in range(counts[dim])]
         back = [level(c, rest, offset + q * strides[dim]) for q, c in enumerate(cut)]
+        if not join:
+            return back
         return lax.concatenate(back, dim)
 
     return Side(counts, level(pieces.blocks, dims, 0))
@@ -372,15 +390,15 @@
         side = Side(counts, [cut[2 * h : 2 * h + 2] for h in range(counts[0])])
         side = swap(side, (0, 1))
         side = swap(side, (3,))
-        side = swap(side, (2, 4))
-        turned = fourier(side.merged(), weights, kcols, True)
-        side = swap(Side.of(counts, turned), (2,))
+        side = swap(side, (2, 4), join=False)
+        turned = fourier(side.blocks, weights, kcols, counts)
+        side = swap(Side.of(counts, turned), (4,))
         side = swap(side, (0, 1))
         side = swap(side, (3,))
-        side = swap(side, (4,))
+        side = swap(side, (2,))
         earlier = dyson(side.merged(), green, main, kcols, True, ())
     middle = exchange(by_device(blocks, main))
-    middle = fourier(middle, weights, kcols, False)
+    middle = fourier(middle, weights, kcols, ())
     middle = exchange(middle)
     sigma, dressed = dyson(middle, green, 0, kcols, False, earlier)
     return sigma.reshape(green.shape), dressed

time: 126 us -> 125 us (level)
  waiting for transfers between devices: 81.3 us -> 79 us
    ppermute x13, waiting for transfers between devices: 44.7 us -> 42.8 us  [level(): return lax.ppermute(part, AXES, pairs)]
    reshape x0 -> x3, local copies, waits for them, and re-layouts: none -> 1.33 us  [per_device(): cut = [c.reshape((1, 1) + counts[2:] + c.shape[1:]) for c in cut]]
  transfers between devices with their start and end apart: 15 -> 15, of which waited for: 11 -> 10; matrix products, arithmetic and copies ran while one was open for 2% -> 3% of each run, Pallas kernels for 6% -> 6%
where the time goes in v5:
time: 125 us
  waiting for transfers between devices  79 us (63%)
  starting transfers between devices  28.8 us (23%)
  Pallas kernels  13.1 us (10%)
  local copies, waits for them, and re-layouts  1.89 us (2%)
  other arithmetic  1.31 us (1%)
    ppermute x13, waiting for transfers between devices, level(): return lax.ppermute(part, AXES, pairs)  42.8 us
    all_to_all x2, waiting for transfers between devices, exchange(): return lax.all_to_all(blocks, AXES, split_axis=0, concat_axis=0, tiled=True)  36.3 us
    ppermute x13, starting transfers between devices, level(): return lax.ppermute(part, AXES, pairs)  18.3 us
    all_to_all x2, starting transfers between devices, exchange(): return lax.all_to_all(blocks, AXES, split_axis=0, concat_axis=0, tiled=True)  10.5 us
    pallas_call x2, Pallas kernels, fourier(): pl.pallas_call(functools.partial(fourier_kernel, kcols, counts), in_specs...  4.73 us
    pallas_call x2, Pallas kernels, dyson(): pl.pallas_call(functools.partial(dyson_kernel, first, kcols, relative), i...  4.7 us
  transfers between devices with their start and end apart: 15, of which 10 were waited for; matrix products, arithmetic and copies ran while one was open for 3% of the time, Pallas kernels for 6%

profile of v5, /device:TPU:0, one launch (start us, length us, event | category | flops | bytes accessed | tf_op | source)
XLA Modules:
  0.0 124.9 jit_solution(84937945128752245)
XLA Ops:
  0.6 2.4 %by_device.1 = bf16[32,3,2,2,8,256]{5,4,3,2,1,0:T(8,128)(2,1)} custom-call(bf16[4,2,2,32,8,256]{5,4,3,2,1,0:T(8,128)(2,1)} %bitcast.24), custom_call_target="tpu_custom_call" | custom-call | tf_op jit(solution)/shard_map/by_device/pallas_call | solution.py:213
  3.0 7.3 %all-to-all-start = ((bf16[32,3,2,2,8,256]{5,4,3,2,1,0:T(8,128)(2,1)}), bf16[32,3,2,2,8,256]{5,4,3,2,1,0:T(8,128)(2,1)S(1)}, u32[]{:S(2)}, u32[]{:S(2)}) async-start(bf16[32,3,2,2,8,256]{5,4,3,2,1,0:T(8,128)(2,1)} %by_device.1), calls=%async_computation | async-start | bytes 3145728 | tf_op jit(solution)/shard_map/all_to_all | solution.py:339
  10.4 0.0 copy-start.3
  10.4 0.0 copy-start
  10.4 0.0 copy-start.1
  10.4 1.2 by_offset.1
  11.7 3.7 %collective-permute-start.2 = (bf16[1,1,2,2,2,1,2,2,8,256]{9,8,7,6,3,1,0,5,4,2:T(8,128)(2,1)S(1)}, bf16[1,1,2,2,2,1,2,2,8,256]{9,8,7,6,3,1,0,5,4,2:T(8,128)(2,1)}, u32[]{:S(2)}, u32[]{:S(2)}) collective-permute-start(bf16[1,1,2,2,2,1,2,2,8,256]{9,8,7,6,3,1,0,5,4,2:T(8,128)(2,1)S(1)} %copy.17), channel_id=1, source_target_pairs={{0,24},{1,25},{2,26},{3,27},{4,28},{5,29},{6,30},{7,31},{8,16},{9,... | collective-permute-start | bytes 393224 | tf_op jit(solution)/shard_map/ppermute | solution.py:351
  15.3 0.7 copy.16
  16.0 0.0 collective-permute-start.1
  16.0 0.7 copy.14
  16.7 0.8 collective-permute-start
  17.4 0.0 copy-done.3
  17.4 0.3 reshape.43.w_ref
  17.7 36.3 %all-to-all-done.refs_0_ = bf16[32,3,2,2,8,256]{5,4,3,2,1,0:T(8,128)(2,1)S(1)} async-done(((bf16[32,3,2,2,8,256]{5,4,3,2,1,0:T(8,128)(2,1)}), bf16[32,3,2,2,8,256]{5,4,3,2,1,0:T(8,128)(2,1)S(1)}, u32[]{:S(2)}, u32[]{:S(2)}) %all-to-all-start) | async-done | bytes 1572896 | tf_op jit(solution)/shard_map/all_to_all | solution.py:339
  54.0 0.0 copy-done
  54.0 0.0 copy-done.1
  54.0 3.5 %shard_map.113 = bf16[32,3,2,2,8,256]{5,4,3,2,1,0:T(8,128)(2,1)} custom-call(f32[16,4,8,256]{3,2,1,0:T(8,128)S(1)} %reshape.43.w_ref, bf16[256,512]{1,0:T(8,128)(2,1)S(1)} %copy-done.1, bf16[256,768]{1,0:T(8,128)(2,1)S(1)} %copy-done, bf16[32,3,2,2,8,256]{5,4,3,2,1,0:T(8,128)(2,1)S(1)} %all-to-all-done.refs_0_), custom_call_target="tpu_custom_call" | custom-call | flops 2013265920 | bytes 3670016 | tf_op jit(solution)/shard_map/pallas_call | solution.py:168
  57.5 3.2 %all-to-all-start.1 = ((bf16[32,3,2,2,8,256]{5,4,3,2,1,0:T(8,128)(2,1)}), bf16[32,3,2,2,8,256]{5,4,3,2,1,0:T(8,128)(2,1)S(1)}, u32[]{:S(2)}, u32[]{:S(2)}) async-start(bf16[32,3,2,2,8,256]{5,4,3,2,1,0:T(8,128)(2,1)} %shard_map.113), calls=%async_computation.1 | async-start | bytes 3145728 | tf_op jit(solution)/shard_map/all_to_all | solution.py:339
  60.7 0.0 collective-permute-done.2
  60.8 0.0 collective-permute-done.1
  60.8 0.0 collective-permute-done
  60.8 1.1 maximum_maximum_fusion
  61.9 0.3 collective-permute-start.3
  62.2 1.3 %collective-permute-done.3 = bf16[2,2,2,1,2,1,2,2,8,256]{9,8,7,6,3,1,0,5,4,2:T(8,128)(2,1)S(1)} collective-permute-done((bf16[2,2,2,1,2,1,2,2,8,256]{9,8,7,6,3,1,0,5,4,2:T(8,128)(2,1)S(1)}, bf16[2,2,2,1,2,1,2,2,8,256]{9,8,7,6,3,1,0,5,4,2:T(8,128)(2,1)S(1)}, u32[]{:S(2)}, u32[]{:S(2)}) %collective-permute-start.3) | collective-permute-done | bytes 262176 | tf_op jit(solution)/shard_map/ppermute | solution.py:351
  63.5 2.7 %collective-permute-start.6 = (bf16[2,2,1,2,1,1,2,2,8,256]{9,8,7,6,3,1,0,5,4,2:T(8,128)(2,1)S(1)}, bf16[2,2,1,2,1,1,2,2,8,256]{9,8,7,6,3,1,0,5,4,2:T(8,128)(2,1)S(1)}, u32[]{:S(2)}, u32[]{:S(2)}) collective-permute-start(bf16[2,2,1,2,1,1,2,2,8,256]{9,8,7,6,3,1,0,5,4,2:T(8,128)(2,1)S(1)} %get-tuple-element.30), channel_id=1, source_target_pairs={{0,5},{1,4},{2,7},{3,6},{4,1},{5,0},{6,3},{7,2},{8,13},{9,12},{10,... | collective-permute-start | bytes 393224 | tf_op jit(solution)/shard_map/ppermute | solution.py:351
  66.3 0.6 collective-permute-start.4
  66.8 0.3 collective-permute-start.5
  67.1 14.1 %collective-permute-done.6 = bf16[2,2,1,2,1,1,2,2,8,256]{9,8,7,6,3,1,0,5,4,2:T(8,128)(2,1)S(1)} collective-permute-done((bf16[2,2,1,2,1,1,2,2,8,256]{9,8,7,6,3,1,0,5,4,2:T(8,128)(2,1)S(1)}, bf16[2,2,1,2,1,1,2,2,8,256]{9,8,7,6,3,1,0,5,4,2:T(8,128)(2,1)S(1)}, u32[]{:S(2)}, u32[]{:S(2)}) %collective-permute-start.6) | collective-permute-done | bytes 131104 | tf_op jit(solution)/shard_map/ppermute | solution.py:351
  81.2 0.0 collective-permute-done.4
  81.2 0.4 collective-permute-done.5
  81.5 1.2 shard_map.114
  82.8 2.4 %collective-permute-start.7 = (bf16[2,2,2,2,1,1,2,2,8,256]{9,8,7,6,4,3,2,1,0,5:T(8,128)(2,1)S(1)}, bf16[2,2,2,2,1,1,2,2,8,256]{9,8,7,6,4,3,2,1,0,5:T(8,128)(2,1)S(1)}, u32[]{:S(2)}, u32[]{:S(2)}) collective-permute-start(bf16[2,2,2,2,1,1,2,2,8,256]{9,8,7,6,4,3,2,1,0,5:T(8,128)(2,1)S(1)} %get-tuple-element.29), channel_id=1, source_target_pairs={{0,1},{1,0},{2,3},{3,2},{4,5},{5,4},{6,7},{7,6},{8,9},{9,8},{10,11... | collective-permute-start | bytes 786440 | tf_op jit(solution)/shard_map/ppermute | solution.py:351
  85.2 8.3 %collective-permute-done.7 = bf16[2,2,2,2,1,1,2,2,8,256]{9,8,7,6,4,3,2,1,0,5:T(8,128)(2,1)S(1)} collective-permute-done((bf16[2,2,2,2,1,1,2,2,8,256]{9,8,7,6,4,3,2,1,0,5:T(8,128)(2,1)S(1)}, bf16[2,2,2,2,1,1,2,2,8,256]{9,8,7,6,4,3,2,1,0,5:T(8,128)(2,1)S(1)}, u32[]{:S(2)}, u32[]{:S(2)}) %collective-permute-start.7) | collective-permute-done | bytes 262176 | tf_op jit(solution)/shard_map/ppermute | solution.py:351
  93.5 2.5 %collective-permute-start.8 = (bf16[1,1,2,2,2,1,2,2,8,256]{9,8,7,6,4,3,2,1,0,5:T(8,128)(2,1)S(1)}, bf16[1,1,2,2,2,1,2,2,8,256]{9,8,7,6,4,3,2,1,0,5:T(8,128)(2,1)S(1)}, u32[]{:S(2)}, u32[]{:S(2)}) collective-permute-start(bf16[1,1,2,2,2,1,2,2,8,256]{9,8,7,6,4,3,2,1,0,5:T(8,128)(2,1)S(1)} %get-tuple-element.25), channel_id=1, source_target_pairs={{0,8},{1,9},{2,10},{3,11},{4,12},{5,13},{6,14},{7,15},{8,0},{9,1},... | collective-permute-start | bytes 393224 | tf_op jit(solution)/shard_map/ppermute | solution.py:351
  96.1 2.8 %collective-permute-start.10 = (bf16[1,1,2,2,2,1,2,2,8,256]{9,8,7,6,4,3,2,1,0,5:T(8,128)(2,1)S(1)}, bf16[1,1,2,2,2,1,2,2,8,256]{9,8,7,6,4,3,2,1,0,5:T(8,128)(2,1)S(1)}, u32[]{:S(2)}, u32[]{:S(2)}) collective-permute-start(bf16[1,1,2,2,2,1,2,2,8,256]{9,8,7,6,4,3,2,1,0,5:T(8,128)(2,1)S(1)} %get-tuple-element.26), channel_id=1, source_target_pairs={{0,24},{1,25},{2,26},{3,27},{4,28},{5,29},{6,30},{7,31},{8,16},{9,... | collective-permute-start | bytes 393224 | tf_op jit(solution)/shard_map/ppermute | solution.py:351
  98.9 0.5 collective-permute-start.9
  99.4 3.1 %collective-permute-done.8 = bf16[1,1,2,2,2,1,2,2,8,256]{9,8,7,6,4,3,2,1,0,5:T(8,128)(2,1)S(1)} collective-permute-done((bf16[1,1,2,2,2,1,2,2,8,256]{9,8,7,6,4,3,2,1,0,5:T(8,128)(2,1)S(1)}, bf16[1,1,2,2,2,1,2,2,8,256]{9,8,7,6,4,3,2,1,0,5:T(8,128)(2,1)S(1)}, u32[]{:S(2)}, u32[]{:S(2)}) %collective-permute-start.8) | collective-permute-done | bytes 131104 | tf_op jit(solution)/shard_map/ppermute | solution.py:351
  102.5 3.0 %collective-permute-done.10 = bf16[1,1,2,2,2,1,2,2,8,256]{9,8,7,6,4,3,2,1,0,5:T(8,128)(2,1)S(1)} collective-permute-done((bf16[1,1,2,2,2,1,2,2,8,256]{9,8,7,6,4,3,2,1,0,5:T(8,128)(2,1)S(1)}, bf16[1,1,2,2,2,1,2,2,8,256]{9,8,7,6,4,3,2,1,0,5:T(8,128)(2,1)S(1)}, u32[]{:S(2)}, u32[]{:S(2)}) %collective-permute-start.10) | collective-permute-done | bytes 131104 | tf_op jit(solution)/shard_map/ppermute | solution.py:351
  105.5 4.5 %collective-permute-done.9 = bf16[1,1,2,2,2,1,2,2,8,256]{9,8,7,6,4,3,2,1,0,5:T(8,128)(2,1)S(1)} collective-permute-done((bf16[1,1,2,2,2,1,2,2,8,256]{9,8,7,6,4,3,2,1,0,5:T(8,128)(2,1)S(1)}, bf16[1,1,2,2,2,1,2,2,8,256]{9,8,7,6,4,3,2,1,0,5:T(8,128)(2,1)S(1)}, u32[]{:S(2)}, u32[]{:S(2)}) %collective-permute-start.9) | collective-permute-done | bytes 131104 | tf_op jit(solution)/shard_map/ppermute | solution.py:351
  110.1 0.1 collective-permute-start.11
  110.2 1.5 %collective-permute-done.11 = bf16[2,2,2,1,2,1,2,2,8,256]{9,8,7,6,4,3,2,1,0,5:T(8,128)(2,1)S(1)} collective-permute-done((bf16[2,2,2,1,2,1,2,2,8,256]{9,8,7,6,4,3,2,1,0,5:T(8,128)(2,1)S(1)}, bf16[2,2,2,1,2,1,2,2,8,256]{9,8,7,6,4,3,2,1,0,5:T(8,128)(2,1)S(1)}, u32[]{:S(2)}, u32[]{:S(2)}) %collective-permute-start.11) | collective-permute-done | bytes 262176 | tf_op jit(solution)/shard_map/ppermute | solution.py:351
  111.7 1.7 %collective-permute-start.12 = (bf16[2,2,1,2,2,1,2,2,8,256]{9,8,7,6,4,3,2,1,0,5:T(8,128)(2,1)S(1)}, bf16[2,2,1,2,2,1,2,2,8,256]{9,8,7,6,4,3,2,1,0,5:T(8,128)(2,1)S(1)}, u32[]{:S(2)}, u32[]{:S(2)}) collective-permute-start(bf16[2,2,1,2,2,1,2,2,8,256]{9,8,7,6,4,3,2,1,0,5:T(8,128)(2,1)S(1)} %get-tuple-element.21), channel_id=1, source_target_pairs={{0,4},{1,5},{2,6},{3,7},{4,0},{5,1},{6,2},{7,3},{8,12},{9,13},{10,... | collective-permute-start | bytes 786440 | tf_op jit(solution)/shard_map/ppermute | solution.py:351
  113.4 0.1 slice.66.g_ref
  113.5 6.6 %collective-permute-done.12 = bf16[2,2,1,2,2,1,2,2,8,256]{9,8,7,6,4,3,2,1,0,5:T(8,128)(2,1)S(1)} collective-permute-done((bf16[2,2,1,2,2,1,2,2,8,256]{9,8,7,6,4,3,2,1,0,5:T(8,128)(2,1)S(1)}, bf16[2,2,1,2,2,1,2,2,8,256]{9,8,7,6,4,3,2,1,0,5:T(8,128)(2,1)S(1)}, u32[]{:S(2)}, u32[]{:S(2)}) %collective-permute-start.12) | collective-permute-done | bytes 262176 | tf_op jit(solution)/shard_map/ppermute | solution.py:351
  120.1 0.1 pad_maximum_fusion
  120.2 1.6 %shard_map.115 = (bf16[4,2,2,32,8,256]{5,4,3,2,1,0:T(8,128)(2,1)}, bf16[4,2,1,2,256,256]{5,4,3,2,1,0:T(8,128)(2,1)}) custom-call(bf16[32,1,2,2,8,256]{5,4,3,2,1,0:T(8,128)(2,1)S(1)} %bitcast.15, bf16[1,2,1,2,256,256]{5,4,3,2,1,0:T(8,128)(2,1)S(1)} %slice.83.g_ref), custom_call_target="tpu_custom_call" | custom-call | flops 536870912 | bytes 4194304 | tf_op jit(solution)/shard_map/pallas_call | solution.py:314
  121.8 0.0 all-to-all-done.1.s_ref
  121.8 3.1 %shard_map.116 = (bf16[4,2,2,32,8,256]{5,4,3,2,1,0:T(8,128)(2,1)}, bf16[4,2,1,2,256,256]{5,4,3,2,1,0:T(8,128)(2,1)}) custom-call(bf16[32,3,2,2,8,256]{5,4,3,2,1,0:T(8,128)(2,1)S(1)} %all-to-all-done.1.s_ref, bf16[3,2,1,2,256,256]{5,4,3,2,1,0:T(8,128)(2,1)S(1)} %slice.66.g_ref, ...), custom_call_target="tpu_custom_call", output_to_operand_aliasing={{0}: (2, {}), {1}: (3, {})} | custom-call | flops 1610612736 | bytes 12582912 | tf_op jit(solution)/shard_map/pallas_call | solution.py:314
  (11 shorter events, 0.4 us)
Async XLA Ops:
  3.0 51.0 %all-to-all-start = ((bf16[32,3,2,2,8,256]{5,4,3,2,1,0:T(8,128)(2,1)}), bf16[32,3,2,2,8,256]{5,4,3,2,1,0:T(8,128)(2,1)S(1)}, u32[]{:S(2)}, u32[]{:S(2)}) async-start(bf16[32,3,2,2,8,256]{5,4,3,2,1,0:T(8,128)(2,1)} %by_device.1), calls=%async_computation | async-start | bytes 3145728 | tf_op jit(solution)/shard_map/all_to_all | solution.py:339
  10.4 7.1 %copy-start.3 = (f32[16,4,2048]{2,1,0:T(4,128)S(1)}, f32[16,4,2048]{2,1,0:T(4,128)}, u32[]{:S(2)}) copy-start(f32[16,4,2048]{2,1,0:T(4,128)} %param.11) | copy-start | bytes 1572868
  10.4 43.6 %copy-start = (bf16[256,768]{1,0:T(8,128)(2,1)S(1)}, bf16[256,768]{1,0:T(8,128)(2,1)}, u32[]{:S(2)}) copy-start(bf16[256,768]{1,0:T(8,128)(2,1)} %constant.16.inv_ref) | copy-start | bytes 1179652
  10.4 43.6 %copy-start.1 = (bf16[256,512]{1,0:T(8,128)(2,1)S(1)}, bf16[256,512]{1,0:T(8,128)(2,1)}, u32[]{:S(2)}) copy-start(bf16[256,512]{1,0:T(8,128)(2,1)} %constant.11.fwd_ref) | copy-start | bytes 786436
  11.7 49.1 %collective-permute-start.2 = (bf16[1,1,2,2,2,1,2,2,8,256]{9,8,7,6,3,1,0,5,4,2:T(8,128)(2,1)S(1)}, bf16[1,1,2,2,2,1,2,2,8,256]{9,8,7,6,3,1,0,5,4,2:T(8,128)(2,1)}, u32[]{:S(2)}, u32[]{:S(2)}) collective-permute-start(bf16[1,1,2,2,2,1,2,2,8,256]{9,8,7,6,3,1,0,5,4,2:T(8,128)(2,1)S(1)} %copy.17), channel_id=1, source_target_pairs={{0,24},{1,25},{2,26},{3,27},{4,28},{5,29},{6,30},{7,31},{8,16},{9,... | collective-permute-start | bytes 393224 | tf_op jit(solution)/shard_map/ppermute | solution.py:351
  16.0 44.7 %collective-permute-start.1 = (bf16[1,1,2,2,2,1,2,2,8,256]{9,8,7,6,3,1,0,5,4,2:T(8,128)(2,1)}, bf16[1,1,2,2,2,1,2,2,8,256]{9,8,7,6,3,1,0,5,4,2:T(8,128)(2,1)}, u32[]{:S(2)}, u32[]{:S(2)}) collective-permute-start(bf16[1,1,2,2,2,1,2,2,8,256]{9,8,7,6,3,1,0,5,4,2:T(8,128)(2,1)} %copy.16), channel_id=1, source_target_pairs={{0,16},{1,17},{2,18},{3,19},{4,20},{5,21},{6,22},{7,23},{8,24},{9,... | collective-permute-start | bytes 393224 | tf_op jit(solution)/shard_map/ppermute | solution.py:351
  16.7 44.1 %collective-permute-start = (bf16[1,1,2,2,2,1,2,2,8,256]{9,8,7,6,3,1,0,5,4,2:T(8,128)(2,1)}, bf16[1,1,2,2,2,1,2,2,8,256]{9,8,7,6,3,1,0,5,4,2:T(8,128)(2,1)}, u32[]{:S(2)}, u32[]{:S(2)}) collective-permute-start(bf16[1,1,2,2,2,1,2,2,8,256]{9,8,7,6,3,1,0,5,4,2:T(8,128)(2,1)} %copy.14), channel_id=1, source_target_pairs={{0,8},{1,9},{2,10},{3,11},{4,12},{5,13},{6,14},{7,15},{8,0},{9,1},... | collective-permute-start | bytes 393224 | tf_op jit(solution)/shard_map/ppermute | solution.py:351
  57.5 64.2 %all-to-all-start.1 = ((bf16[32,3,2,2,8,256]{5,4,3,2,1,0:T(8,128)(2,1)}), bf16[32,3,2,2,8,256]{5,4,3,2,1,0:T(8,128)(2,1)S(1)}, u32[]{:S(2)}, u32[]{:S(2)}) async-start(bf16[32,3,2,2,8,256]{5,4,3,2,1,0:T(8,128)(2,1)} %shard_map.113), calls=%async_computation.1 | async-start | bytes 3145728 | tf_op jit(solution)/shard_map/all_to_all | solution.py:339
  61.9 1.6 %collective-permute-start.3 = (bf16[2,2,2,1,2,1,2,2,8,256]{9,8,7,6,3,1,0,5,4,2:T(8,128)(2,1)S(1)}, bf16[2,2,2,1,2,1,2,2,8,256]{9,8,7,6,3,1,0,5,4,2:T(8,128)(2,1)S(1)}, u32[]{:S(2)}, u32[]{:S(2)}) collective-permute-start(bf16[2,2,2,1,2,1,2,2,8,256]{9,8,7,6,3,1,0,5,4,2:T(8,128)(2,1)S(1)} %get-tuple-element.34), channel_id=1, source_target_pairs={{0,2},{1,3},{2,0},{3,1},{4,6},{5,7},{6,4},{7,5},{8,10},{9,11},{10,... | collective-permute-start | bytes 786440 | tf_op jit(solution)/shard_map/ppermute | solution.py:351
  63.5 17.6 %collective-permute-start.6 = (bf16[2,2,1,2,1,1,2,2,8,256]{9,8,7,6,3,1,0,5,4,2:T(8,128)(2,1)S(1)}, bf16[2,2,1,2,1,1,2,2,8,256]{9,8,7,6,3,1,0,5,4,2:T(8,128)(2,1)S(1)}, u32[]{:S(2)}, u32[]{:S(2)}) collective-permute-start(bf16[2,2,1,2,1,1,2,2,8,256]{9,8,7,6,3,1,0,5,4,2:T(8,128)(2,1)S(1)} %get-tuple-element.30), channel_id=1, source_target_pairs={{0,5},{1,4},{2,7},{3,6},{4,1},{5,0},{6,3},{7,2},{8,13},{9,12},{10,... | collective-permute-start | bytes 393224 | tf_op jit(solution)/shard_map/ppermute | solution.py:351
  66.3 14.9 %collective-permute-start.4 = (bf16[2,2,1,2,1,1,2,2,8,256]{9,8,7,6,3,1,0,5,4,2:T(8,128)(2,1)S(1)}, bf16[2,2,1,2,1,1,2,2,8,256]{9,8,7,6,3,1,0,5,4,2:T(8,128)(2,1)S(1)}, u32[]{:S(2)}, u32[]{:S(2)}) collective-permute-start(bf16[2,2,1,2,1,1,2,2,8,256]{9,8,7,6,3,1,0,5,4,2:T(8,128)(2,1)S(1)} %get-tuple-element.32), channel_id=1, source_target_pairs={{0,1},{1,0},{2,3},{3,2},{4,5},{5,4},{6,7},{7,6},{8,9},{9,8},{10,11... | collective-permute-start | bytes 393224 | tf_op jit(solution)/shard_map/ppermute | solution.py:351
  66.8 14.7 %collective-permute-start.5 = (bf16[2,2,1,2,1,1,2,2,8,256]{9,8,7,6,3,1,0,5,4,2:T(8,128)(2,1)S(1)}, bf16[2,2,1,2,1,1,2,2,8,256]{9,8,7,6,3,1,0,5,4,2:T(8,128)(2,1)S(1)}, u32[]{:S(2)}, u32[]{:S(2)}) collective-permute-start(bf16[2,2,1,2,1,1,2,2,8,256]{9,8,7,6,3,1,0,5,4,2:T(8,128)(2,1)S(1)} %get-tuple-element.33), channel_id=1, source_target_pairs={{0,4},{1,5},{2,6},{3,7},{4,0},{5,1},{6,2},{7,3},{8,12},{9,13},{10,... | collective-permute-start | bytes 393224 | tf_op jit(solution)/shard_map/ppermute | solution.py:351
  82.8 10.7 %collective-permute-start.7 = (bf16[2,2,2,2,1,1,2,2,8,256]{9,8,7,6,4,3,2,1,0,5:T(8,128)(2,1)S(1)}, bf16[2,2,2,2,1,1,2,2,8,256]{9,8,7,6,4,3,2,1,0,5:T(8,128)(2,1)S(1)}, u32[]{:S(2)}, u32[]{:S(2)}) collective-permute-start(bf16[2,2,2,2,1,1,2,2,8,256]{9,8,7,6,4,3,2,1,0,5:T(8,128)(2,1)S(1)} %get-tuple-element.29), channel_id=1, source_target_pairs={{0,1},{1,0},{2,3},{3,2},{4,5},{5,4},{6,7},{7,6},{8,9},{9,8},{10,11... | collective-permute-start | bytes 786440 | tf_op jit(solution)/shard_map/ppermute | solution.py:351
  93.5 19.9 %copy-start.2 = (bf16[4,2,1,2,256,256]{5,4,3,2,1,0:T(8,128)(2,1)S(1)}, bf16[4,2,1,2,256,256]{5,4,3,2,1,0:T(8,128)(2,1)}, u32[]{:S(2)}) copy-start(bf16[4,2,1,2,256,256]{5,4,3,2,1,0:T(8,128)(2,1)} %param.10) | copy-start | bytes 6291460
  93.5 8.9 %collective-permute-start.8 = (bf16[1,1,2,2,2,1,2,2,8,256]{9,8,7,6,4,3,2,1,0,5:T(8,128)(2,1)S(1)}, bf16[1,1,2,2,2,1,2,2,8,256]{9,8,7,6,4,3,2,1,0,5:T(8,128)(2,1)S(1)}, u32[]{:S(2)}, u32[]{:S(2)}) collective-permute-start(bf16[1,1,2,2,2,1,2,2,8,256]{9,8,7,6,4,3,2,1,0,5:T(8,128)(2,1)S(1)} %get-tuple-element.25), channel_id=1, source_target_pairs={{0,8},{1,9},{2,10},{3,11},{4,12},{5,13},{6,14},{7,15},{8,0},{9,1},... | collective-permute-start | bytes 393224 | tf_op jit(solution)/shard_map/ppermute | solution.py:351
  96.1 9.4 %collective-permute-start.10 = (bf16[1,1,2,2,2,1,2,2,8,256]{9,8,7,6,4,3,2,1,0,5:T(8,128)(2,1)S(1)}, bf16[1,1,2,2,2,1,2,2,8,256]{9,8,7,6,4,3,2,1,0,5:T(8,128)(2,1)S(1)}, u32[]{:S(2)}, u32[]{:S(2)}) collective-permute-start(bf16[1,1,2,2,2,1,2,2,8,256]{9,8,7,6,4,3,2,1,0,5:T(8,128)(2,1)S(1)} %get-tuple-element.26), channel_id=1, source_target_pairs={{0,24},{1,25},{2,26},{3,27},{4,28},{5,29},{6,30},{7,31},{8,16},{9,... | collective-permute-start | bytes 393224 | tf_op jit(solution)/shard_map/ppermute | solution.py:351
  98.9 11.1 %collective-permute-start.9 = (bf16[1,1,2,2,2,1,2,2,8,256]{9,8,7,6,4,3,2,1,0,5:T(8,128)(2,1)S(1)}, bf16[1,1,2,2,2,1,2,2,8,256]{9,8,7,6,4,3,2,1,0,5:T(8,128)(2,1)S(1)}, u32[]{:S(2)}, u32[]{:S(2)}) collective-permute-start(bf16[1,1,2,2,2,1,2,2,8,256]{9,8,7,6,4,3,2,1,0,5:T(8,128)(2,1)S(1)} %get-tuple-element.27), channel_id=1, source_target_pairs={{0,16},{1,17},{2,18},{3,19},{4,20},{5,21},{6,22},{7,23},{8,24},{9,... | collective-permute-start | bytes 393224 | tf_op jit(solution)/shard_map/ppermute | solution.py:351
  110.1 1.6 %collective-permute-start.11 = (bf16[2,2,2,1,2,1,2,2,8,256]{9,8,7,6,4,3,2,1,0,5:T(8,128)(2,1)S(1)}, bf16[2,2,2,1,2,1,2,2,8,256]{9,8,7,6,4,3,2,1,0,5:T(8,128)(2,1)S(1)}, u32[]{:S(2)}, u32[]{:S(2)}) collective-permute-start(bf16[2,2,2,1,2,1,2,2,8,256]{9,8,7,6,4,3,2,1,0,5:T(8,128)(2,1)S(1)} %get-tuple-element.23), channel_id=1, source_target_pairs={{0,2},{1,3},{2,0},{3,1},{4,6},{5,7},{6,4},{7,5},{8,10},{9,11},{10,... | collective-permute-start | bytes 786440 | tf_op jit(solution)/shard_map/ppermute | solution.py:351
  111.7 8.4 %collective-permute-start.12 = (bf16[2,2,1,2,2,1,2,2,8,256]{9,8,7,6,4,3,2,1,0,5:T(8,128)(2,1)S(1)}, bf16[2,2,1,2,2,1,2,2,8,256]{9,8,7,6,4,3,2,1,0,5:T(8,128)(2,1)S(1)}, u32[]{:S(2)}, u32[]{:S(2)}) collective-permute-start(bf16[2,2,1,2,2,1,2,2,8,256]{9,8,7,6,4,3,2,1,0,5:T(8,128)(2,1)S(1)} %get-tuple-element.21), channel_id=1, source_target_pairs={{0,4},{1,5},{2,6},{3,7},{4,0},{5,1},{6,2},{7,3},{8,12},{9,13},{10,... | collective-permute-start | bytes 786440 | tf_op jit(solution)/shard_map/ppermute | solution.py:351
